TPU v7x, 32 devices: a whole 2x2x4 slice. The times are simulated.
32 devices in a mesh: gx: 4 (over y, x), gy: 2 (over core), gz: 4 (over z).
Axes of the slice: x: 2, y: 2, z: 4, core: 2. Of those that a mesh axis runs over, the one named last changes fastest.
Arguments:
- pair: bfloat16 [128, 1024, 1024], P('gz', 'gy', 'gx'), may hold values from -6 to 6
- pair_mask: int32 [1024, 1024], P('gy', 'gx'), may hold values 0 or 1
- in_gain: float32 [128], replicated, may hold values from 0.5 to 2
- w_left: bfloat16 [128, 128], P(None, 'gz'), may hold values from -0.5 to 0.5
- w_left_gate: bfloat16 [128, 128], P(None, 'gz'), may hold values from -0.5 to 0.5
- w_right: bfloat16 [128, 128], P(None, 'gz'), may hold values from -0.5 to 0.5
- w_right_gate: bfloat16 [128, 128], P(None, 'gz'), may hold values from -0.5 to 0.5
- w_out_gate: bfloat16 [128, 128], P(None, 'gz'), may hold values from -0.5 to 0.5
- out_gain: float32 [128], P('gz'), may hold values from 0.5 to 2
- w_out: bfloat16 [128, 128], P(None, 'gz'), may hold values from -0.5 to 0.5
Outputs:
- update: bfloat16 [128, 1024, 1024], P('gz', 'gy', 'gx')
All inputs are finite; a program needn't handle non-finite values. No bound on the sum of `pair_mask` on one device may be relied on, other than what follows from the above.
Results may differ from a plain program's by a relative error of at most 0.0078.
Values may be sent and summed in bfloat16 or wider, within the bound.
No kernel may reach another device: no remote copies, remote signals or barrier semaphores. Data moves between devices by JAX's collectives and lax.ppermute only.
A program may use at most 192 MiB of HBM per device.

v0:
```python
import functools

import jax
import jax.numpy as jnp
from jax import lax
from jax.experimental import pallas as pl
from jax.experimental.pallas import tpu as pltpu
from jax.sharding import PartitionSpec as P


epsilon = 1e-05
CHUNKS = 4
ROWS = 16
PITCH = 24
LANES = 128
F32, BF16 = jnp.float32, jnp.bfloat16
ARBITRARY = pltpu.GridDimensionSemantics.ARBITRARY

ROW_ORDER = ((0, 1, 2, 3), (1, 0, 2, 3), (2, 3, 1, 0), (3, 2, 1, 0))
COL_ORDER = ((0, 1, 2, 3), (1, 2, 3, 0), (2, 1, 0, 3), (3, 2, 1, 0))

MESSAGES = {
    "1": ("own", ((3, 2), (2, 1), (1, 0)), ((0, 1), (1, 2), (2, 3))),
    "2": ("1", ((2, 1), (1, 0)), ((1, 2), (2, 3))),
    "3": ("2", ((1, 0),), ((2, 3),)),
    "s": ("side", ((3, 2), (2, 1)), ((0, 1), (1, 2))),
    "r": ("side", ((3, 2),), ((0, 1),)),
    "t": ("side", ((2, 1),), ((1, 2),)),
    "l": ("far", ((2, 1),), ((1, 2),)),
}
EVENTS = (
    (("1", 0),),
    (("s", 0),),
    (("2", 0),),
    (("1", 1),),
    (("l", 0), ("r", 1), ("3", 0)),
    (("2", 1),),
    (("1", 2),),
    (("t", 1), ("r", 2), ("3", 1)),
    (("2", 2),),
    (("1", 3),),
    (("l", 1), ("r", 3), ("3", 2)),
    (("2", 3),),
    (("t", 2),),
    (("l", 2), ("3", 3)),
    (("t", 3),),
    (("l", 3),),
)
TASKS = {
    6: (("right", 0),),
    7: (("left", 0),),
    9: (("right", 1),),
    10: (("pass", 0),),
    12: (("right", 2),),
    13: (("left", 1),),
    14: (("pass", 1),),
    15: (("right", 3), ("left", 2)),
}
TAIL = (
    ("multiply", 0),
    ("multiply", 1),
    ("share", 3),
    ("multiply", 2),
    ("complete", 0),
    ("complete", 1),
    ("multiply", 3),
    ("complete", 2),
    ("complete", 3),
)


def sigmoid(x):
    return 1.0 / (1.0 + jnp.exp(-x))


def norm_channels(x, gain):
    average = jnp.mean(x, axis=0, keepdims=True)
    centered = x - average
    spread = jnp.mean(jnp.square(centered), axis=0, keepdims=True)
    return (centered * lax.rsqrt(spread + epsilon) * gain).astype(BF16)


def dot(a, b, dims=(((1,), (0,)), ((), ()))):
    return lax.dot_general(a, b, dims, preferred_element_type=F32)


def project_kernel(slots, emit, parts, plane_ref, *refs):
    n_in = sum(len(slot) for slot in slots)
    ins = refs[:n_in]
    mask_ref, weight_ref, gain_ref = refs[n_in : n_in + 3]
    outs = refs[n_in + 3 : n_in + 3 + parts + (1 if emit else 0)]
    x_ref, y_ref = refs[-2:]
    plane = plane_ref[0]
    width = ins[0].shape[-1]
    halves = width // LANES
    channels = ins[0].shape[0]
    position = 0
    for slot_index, slot in enumerate(slots):
        base = slot_index * channels
        for planes in slot:
            source = ins[position]
            position += 1
            hit = functools.reduce(jnp.logical_or, [plane == p for p in planes])

            @pl.when(hit)
            def _(source=source, base=base):
                for half in range(halves):
                    block = source[:, 0, :, half * LANES : (half + 1) * LANES].astype(F32)
                    x_ref[half, base : base + channels, 0:ROWS, :] = block

    total = len(slots) * channels
    hidden = weight_ref.shape[0] // 2
    x_flat = x_ref.reshape(halves, total * PITCH, LANES)
    y_flat = y_ref.reshape(halves, hidden * PITCH, LANES)
    gain = gain_ref[...]

    def step(row, carry):
        normed = [
            norm_channels(x_flat[half, pl.ds(row, total, stride=PITCH), :], gain) for half in range(halves)
        ]
        if emit:
            upper = (plane >> 1) == 1
            chosen = jnp.where(upper, normed[1].astype(F32), normed[0].astype(F32))
            outs[parts][0, row] = chosen.astype(BF16)
        both = dot(weight_ref[...], jnp.concatenate(normed, axis=1))
        mask = mask_ref[0, pl.ds(row, 1), :]
        value = mask * sigmoid(both[:hidden]) * both[hidden:]
        for half in range(halves):
            y_flat[half, pl.ds(row, hidden, stride=PITCH), :] = value[:, half * LANES : (half + 1) * LANES]
        return carry

    lax.fori_loop(0, ROWS, step, 0, unroll=8)
    part = hidden // parts
    for m in range(parts):
        for half in range(halves):
            block = y_ref[half, m * part : (m + 1) * part, 0:ROWS, :]
            outs[m][:, 0, :, half * LANES : (half + 1) * LANES] = block.astype(BF16)


def project(plane, slots, arrays, mask, weight, gain, parts, emit):
    channels, blocks, size, width = arrays[0].shape
    hidden = weight.shape[0] // 2
    total = len(slots) * channels
    planes = tuple(tuple(p for _, p in slot) for slot in slots)
    ins = [arrays[index] for slot in slots for index, _ in slot]
    block = pl.BlockSpec((channels, 1, ROWS, width), lambda n, t: (0, n, t, 0))
    whole = lambda n, t: (0, 0)
    out_specs = [pl.BlockSpec((hidden // parts, 1, ROWS, width), lambda n, t: (0, n, t, 0))] * parts
    out_shape = [jax.ShapeDtypeStruct((hidden // parts, blocks, size, width), BF16)] * parts
    if emit:
        out_specs = out_specs + [pl.BlockSpec((1, ROWS, total, LANES), lambda n, t: (n, t, 0, 0))]
        out_shape = out_shape + [jax.ShapeDtypeStruct((blocks, size, total, LANES), BF16)]
    pixels = blocks * size * width
    return pl.pallas_call(
        functools.partial(project_kernel, planes, emit, parts),
        grid=(blocks, size // ROWS),
        in_specs=[pl.BlockSpec(memory_space=pltpu.SMEM)]
        + [block] * len(ins)
        + [
            pl.BlockSpec((1, ROWS, width), lambda n, t: (n, t, 0)),
            pl.BlockSpec(weight.shape, whole),
            pl.BlockSpec(gain.shape, whole),
        ],
        out_specs=out_specs,
        out_shape=out_shape,
        scratch_shapes=[
            pltpu.VMEM((width // LANES, total, PITCH, LANES), F32),
            pltpu.VMEM((width // LANES, hidden, PITCH, LANES), F32),
        ],
        compiler_params=pltpu.CompilerParams(dimension_semantics=(ARBITRARY, ARBITRARY)),
        cost_estimate=pl.CostEstimate(
            flops=16 * pixels * total * hidden, bytes_accessed=2 * pixels * (total * 3 + hidden), transcendentals=0
        ),
        name="project",
    )(plane, *ins, mask, weight, gain)


def product_kernel(parts, chunks, left_chunks, target_ref, *refs):
    lefts = refs[: left_chunks * parts]
    rights = refs[left_chunks * parts : (left_chunks + 2 * chunks) * parts]
    outs = refs[(left_chunks + 2 * chunks) * parts :]
    heads, blocks, size, _ = lefts[0].shape
    cores = 2
    for head in range(heads):
        rows = [
            jnp.concatenate([lefts[c * parts + m][head, n] for m in range(parts)], axis=1)
            for n in range(blocks)
            for c in range(left_chunks)
        ]
        left = jnp.concatenate(rows, axis=0)
        rows = [
            jnp.concatenate([rights[(core * chunks + g) * parts + m][head, n] for m in range(parts)], axis=1)
            for core in range(cores)
            for n in range(blocks)
            for g in range(chunks)
        ]
        right = jnp.concatenate(rows, axis=0)
        mixed = dot(left, right, (((1,), (1,)), ((), ())))
        span = chunks * size
        pieces = [mixed[:, p * span : (p + 1) * span] for p in range(cores * blocks)]
        for m in range(parts):
            pick = target_ref[m]
            value = pieces[0]
            for p in range(1, len(pieces)):
                value = jnp.where(pick == p, pieces[p], value)
            outs[m][head] = value.astype(BF16).reshape(blocks, left_chunks * size, span)


def product(target, lefts, rights, parts, heads):
    hidden, blocks, size, width = lefts[0].shape
    cores = 2
    chunks, left_chunks = len(rights) // (cores * parts), len(lefts) // parts
    span = chunks * size
    left_block = pl.BlockSpec((heads, blocks, size, width), lambda h: (h, 0, 0, 0))
    rows = left_chunks * blocks * size
    return pl.pallas_call(
        functools.partial(product_kernel, parts, chunks, left_chunks),
        grid=(hidden // heads,),
        in_specs=[pl.BlockSpec(memory_space=pltpu.SMEM)] + [left_block] * (len(lefts) + len(rights)),
        out_specs=[pl.BlockSpec((heads, blocks, left_chunks * size, span), lambda h: (h, 0, 0, 0))] * parts,
        out_shape=[jax.ShapeDtypeStruct((hidden, blocks, left_chunks * size, span), BF16)] * parts,
        compiler_params=pltpu.CompilerParams(dimension_semantics=(ARBITRARY,)),
        cost_estimate=pl.CostEstimate(
            flops=2 * hidden * rows * (cores * blocks * span) * width * parts,
            bytes_accessed=2 * hidden * width * parts * (rows + cores * blocks * span),
            transcendentals=0,
        ),
        name="product",
    )(target, *lefts, *rights)


def finish_kernel(parts, *refs):
    mixed = refs[:parts]
    normed_ref, out_ref, gate_ref, gain_ref = refs[parts : parts + 4]
    outs = refs[parts + 4 : -2]
    x_ref, y_ref = refs[-2:]
    part = mixed[0].shape[0]
    for m in range(parts):
        x_ref[m * part : (m + 1) * part, 0:ROWS, :] = mixed[m][:, 0].astype(F32)
    total = parts * part
    x_flat = x_ref.reshape(total * PITCH, LANES)
    y_flat = y_ref.reshape(out_ref.shape[0] * PITCH, LANES)
    gain = gain_ref[...]
    together = 2

    def step(pair, carry):
        base = pair * together
        normed = [
            norm_channels(x_flat[pl.ds(base + r, total, stride=PITCH), :], gain) for r in range(together)
        ]
        gates = dot(gate_ref[...], jnp.concatenate([normed_ref[0, base + r] for r in range(together)], axis=1))
        value = sigmoid(gates) * dot(out_ref[...], jnp.concatenate(normed, axis=1))
        for r in range(together):
            y_flat[pl.ds(base + r, value.shape[0], stride=PITCH), :] = value[:, r * LANES : (r + 1) * LANES]
        return carry

    lax.fori_loop(0, ROWS // together, step, 0, unroll=4)
    part = out_ref.shape[0] // len(outs)
    for q, out in enumerate(outs):
        block = y_ref[q * part : (q + 1) * part, 0:ROWS, :]
        out[:, 0] = block.astype(BF16)


def finish(mixed, normed, offset, w_out, w_gate, gain, planes):
    part, width = mixed[0].shape[0], mixed[0].shape[-1]
    blocks, size = normed.shape[:2]
    first = offset // ROWS
    depth = w_out.shape[0]
    total = part * len(mixed)
    whole = lambda n, t: (0, 0)
    pixels = blocks * size * width
    return pl.pallas_call(
        functools.partial(finish_kernel, len(mixed)),
        grid=(blocks, size // ROWS),
        in_specs=[pl.BlockSpec((part, 1, ROWS, width), lambda n, t: (0, n, t + first, 0))] * len(mixed)
        + [
            pl.BlockSpec((1, ROWS, normed.shape[2], width), lambda n, t: (n, t, 0, 0)),
            pl.BlockSpec(w_out.shape, whole),
            pl.BlockSpec(w_gate.shape, whole),
            pl.BlockSpec(gain.shape, whole),
        ],
        out_specs=[pl.BlockSpec((depth // planes, 1, ROWS, width), lambda n, t: (0, n, t, 0))] * planes,
        out_shape=[jax.ShapeDtypeStruct((depth // planes, blocks, size, width), BF16)] * planes,
        scratch_shapes=[pltpu.VMEM((total, PITCH, width), F32), pltpu.VMEM((depth, PITCH, width), F32)],
        compiler_params=pltpu.CompilerParams(dimension_semantics=(ARBITRARY, ARBITRARY)),
        cost_estimate=pl.CostEstimate(
            flops=16 * pixels * total * depth, bytes_accessed=2 * pixels * total * 3, transcendentals=0
        ),
        name="finish",
    )(*mixed, normed, w_out, w_gate, gain)


def assemble_kernel(planes, chunks, plane_ref, *refs):
    ins, out = refs[:-1], refs[-1]
    plane = plane_ref[0]
    size = ins[0].shape[2]
    for mine in range(planes):

        @pl.when(plane == mine)
        def _(mine=mine):
            for source in range(planes):
                a, b = source & 1, source >> 1
                for g in range(chunks):
                    out[:, 0, a, g * size : (g + 1) * size, b * LANES : (b + 1) * LANES] = ins[
                        (source ^ mine) * chunks + g
                    ][:, 0]


def assemble(plane, pieces, planes):
    chunks = len(pieces) // planes
    depth, blocks, size, width = pieces[0].shape
    step = depth // 4
    return pl.pallas_call(
        functools.partial(assemble_kernel, planes, chunks),
        grid=(4, blocks),
        in_specs=[pl.BlockSpec(memory_space=pltpu.SMEM)]
        + [pl.BlockSpec((step, 1, size, width), lambda d, n: (d, n, 0, 0))] * len(pieces),
        out_specs=pl.BlockSpec((step, 1, 2, chunks * size, 2 * width), lambda d, n: (d, n, 0, 0, 0)),
        out_shape=jax.ShapeDtypeStruct((depth, blocks, 2, chunks * size, 2 * width), BF16),
        compiler_params=pltpu.CompilerParams(dimension_semantics=(ARBITRARY, ARBITRARY)),
        name="assemble",
    )(plane, *pieces)


def block_order(array, order, axis):
    split = array.shape[:axis] + (order.shape[0], array.shape[axis] // order.shape[0]) + array.shape[axis + 1 :]
    return jnp.take(array.reshape(split), order, axis=axis).reshape(array.shape)


def local(
    pair,
    pair_mask,
    in_gain,
    w_left,
    w_left_gate,
    w_right,
    w_right_gate,
    w_out_gate,
    out_gain,
    w_out,
):
    gx, gz = lax.axis_size("gx"), lax.axis_size("gz")
    x, y, z = lax.axis_index("gx"), lax.axis_index("gy"), lax.axis_index("gz")
    plane = z.astype(jnp.int32).reshape(1)
    channels, rows, width = pair.shape
    span = width // 2
    blocks = rows // (2 * span)
    size = span // CHUNKS
    tiles = pair.reshape(channels, blocks, 2, span, width)
    masks = pair_mask.astype(F32).reshape(blocks, 2, span, width)

    shared = [w_left_gate, w_left, w_right_gate, w_right, w_out_gate, w_out, out_gain[None]]
    shared = lax.all_gather(jnp.concatenate([w.astype(F32) for w in shared], axis=0), "gz", axis=1, tiled=True)
    tiles, shared = lax.optimization_barrier((tiles, shared))
    weights = [shared[i * channels * gz : (i + 1) * channels * gz].astype(BF16) for i in range(6)]
    gains = shared[-1]
    row_order, col_order = jnp.asarray(ROW_ORDER)[z], jnp.asarray(COL_ORDER)[z]
    head_order, plane_order = x ^ jnp.arange(gx), z ^ jnp.arange(gz)

    def pair_weight(gate, linear, order):
        halves = [block_order(block_order(w.T, head_order, 0), order, 1) for w in (gate, linear)]
        return jnp.concatenate(halves, axis=0)

    def lanes(vector):
        return jnp.broadcast_to(vector[:, None], (vector.shape[0], LANES))

    left_weight = pair_weight(weights[0], weights[1], row_order)
    right_weight = pair_weight(weights[2], weights[3], col_order)
    gate_weight = block_order(block_order(weights[4].T, plane_order, 0), row_order, 1)
    out_weight = block_order(block_order(weights[5].T, plane_order, 0), head_order, 1)
    left_gain, right_gain = (lanes(block_order(in_gain, order, 0)) for order in (row_order, col_order))
    mix_gain = lanes(block_order(gains, head_order, 0))
    left_mask = lax.dynamic_index_in_dim(masks, z & 1, 1, keepdims=False)
    right_mask = lax.dynamic_index_in_dim(masks, z >> 1, 1, keepdims=False)

    values = {}

    def sync(*keys):
        keys = list(dict.fromkeys(keys))
        values.update(zip(keys, lax.optimization_barrier(tuple(values[key] for key in keys))))

    def start(kind, g):
        operand, down, up = MESSAGES[kind]
        sources = (1, 0) if operand == "side" else (0, 1)
        if operand == "far":
            operand = "s" if ("s", g, 0) in values else "r"
        for way, pairs in enumerate((down, up)):
            source = ("own", g, sources[way]) if operand in ("own", "side") else (operand, g, way)
            values[kind, g, way] = lax.ppermute(values[source], "gz", pairs)

    def operands(kind, g):
        operand = MESSAGES[kind][0]
        if operand == "far":
            operand = "s" if ("s", g, 0) in values else "r"
        return [("own" if operand == "side" else operand, g, way) for way in range(2)]

    def swap(value, axis, bits):
        return lax.ppermute(value, axis, [(i, i ^ bits) for i in range(lax.axis_size(axis))])

    def share(name, g):
        for m in range(1, gx):
            values[name, g, m] = swap(values[name, g, m], "gx", m)

    def pass_on(g):
        for m in range(gx):
            values["other", g, m] = swap(values["right", g, m], "gy", 1)

    def sides(g):
        far, near = ("s", "s") if ("s", g, 0) in values else ("r", "t")
        return [values[far, g, way] for way in range(2)], [values.get((near, g, way)) for way in range(2)]

    def project_right(g):
        (far_down, far_up), _ = sides(g)
        arrays = [values[key, g, way] for key in ("own", "1", "2", "3") for way in range(2)] + [far_down, far_up]
        slots = (
            ((0, (0, 1)), (1, (2, 3))),
            ((2, (0, 1)), (3, (2, 3))),
            ((4, (0, 1)), (5, (2, 3))),
            ((6, (0,)), (9, (1,)), (8, (2,)), (7, (3,))),
        )
        mask = right_mask[:, g * size : (g + 1) * size]
        outs = project(plane, slots, arrays, mask, right_weight, right_gain, gx, False)
        values.update({("right", g, m): outs[m] for m in range(gx)})

    def project_left(g):
        _, (near_down, near_up) = sides(g)
        arrays = [values[key, g, way] for key in ("own", "1", "2", "3", "l") for way in range(2)] + [near_down, near_up]
        slots = (
            ((0, (0, 2)), (1, (1, 3))),
            ((2, (0, 2)), (3, (1, 3))),
            ((4, (0,)), (10, (1,)), (11, (2,)), (5, (3,))),
            ((6, (0,)), (8, (1,)), (9, (2,)), (7, (3,))),
        )
        mask = left_mask[:, g * size : (g + 1) * size]
        outs = project(plane, slots, arrays, mask, left_weight, left_gain, gx, True)
        values.update({("left", g, m): outs[m] for m in range(gx)})
        values["normed", g] = outs[gx]

    target = (((x // blocks) ^ y) * blocks + x % blocks) ^ jnp.arange(gx)
    target = target.astype(jnp.int32)

    def multiply(g):
        rights = [values[key, c, m] for key in ("right", "other") for c in range(CHUNKS) for m in range(gx)]
        outs = product(target, [values["left", g, m] for m in range(gx)], rights, gx, 2)
        values.update({("mixed", g, m): outs[m] for m in range(gx)})

    def complete(g):
        mixed = [values["mixed", g, m] for m in range(gx)]
        outs = finish(mixed, values["normed", g], 0, out_weight, gate_weight, mix_gain, gz)
        values.update({("out", g, q): outs[q] for q in range(gz)})
        for q in range(1, gz):
            values["out", g, q] = swap(outs[q], "gz", q)

    for g in range(CHUNKS):
        for p in range(2):
            values["own", g, p] = tiles[:, :, p, g * size : (g + 1) * size]

    waits = []
    for e, messages in enumerate(EVENTS):
        keys = [(kind, g, way) for kind, g in EVENTS[e - 2] for way in range(2)] if e >= 2 else []
        keys += [key for kind, g in messages for key in operands(kind, g)]
        sync(*keys, *waits)
        waits = []
        for kind, g in messages:
            start(kind, g)
        for name, g in TASKS.get(e, ()):
            if name == "pass":
                pass_on(g)
            else:
                (project_right if name == "right" else project_left)(g)
                share(name, g)
                waits.append((name, g, 0))
        for name, g in TASKS.get(e + 1, ()):
            if name == "pass":
                waits += [("right", g, m) for m in range(gx)]
        for name, g in TASKS.get(e - 1, ()):
            if name == "pass":
                waits += [("other", g, m) for m in range(gx)]

    last = CHUNKS - 1
    sync(*waits, *[(kind, g, way) for event in EVENTS[-2:] for kind, g in event for way in range(2)])
    project_left(last)
    sync(("left", last, 0), *[("right", last - 1, m) for m in range(gx)])
    pass_on(last - 1)
    sync(*[("right", g, m) for g in (last - 1, last) for m in range(gx)])
    pass_on(last)
    previous = None
    for step, g in TAIL:
        needs = {"multiply": ["left"], "complete": ["mixed"], "share": ["left"]}[step]
        keys = [(name, g, m) for name in needs for m in range(gx)]
        sync(*keys, *([previous] if previous else []))
        if step == "multiply":
            multiply(g)
            previous = ("mixed", g, 0)
            share("mixed", g)
        elif step == "share":
            share("left", g)
        else:
            complete(g)
            previous = ("out", g, 0)
    ordered = [values["out", g, q] for q in range(gz) for g in range(CHUNKS)]
    return assemble(plane, ordered, gz).reshape(pair.shape)


def plain_local(
    pair,
    pair_mask,
    in_gain,
    w_left,
    w_left_gate,
    w_right,
    w_right_gate,
    w_out_gate,
    out_gain,
    w_out,
):
    gathered = lax.all_gather(pair, "gz", axis=0, tiled=True).astype(F32)
    average = jnp.mean(gathered, axis=0)
    centered = gathered - average
    spread = jnp.mean(jnp.square(centered), axis=0)
    normed = (centered * lax.rsqrt(spread + epsilon) * in_gain[:, None, None]).astype(BF16)
    mask_float = pair_mask.astype(F32)[None]

    def project_all(weight):
        return jnp.einsum("cik,ch->hik", normed, weight, preferred_element_type=F32)

    left_rows = (mask_float * jax.nn.sigmoid(project_all(w_left_gate)) * project_all(w_left)).astype(BF16)
    right_rows = (mask_float * jax.nn.sigmoid(project_all(w_right_gate)) * project_all(w_right)).astype(BF16)
    out_gate = jax.nn.sigmoid(jnp.einsum("cij,cd->dij", normed, w_out_gate, preferred_element_type=F32))
    left_group, right_group = (
        lax.all_to_all(left_rows, "gx", split_axis=0, concat_axis=2, tiled=True),
        lax.all_to_all(right_rows, "gx", split_axis=0, concat_axis=2, tiled=True),
    )
    full_product = lax.dot_general(
        left_group,
        lax.all_gather(right_group, "gy", axis=1, tiled=True),
        (((2,), (2,)), ((0,), (0,))),
        preferred_element_type=F32,
    )
    mixed_sum = lax.all_to_all(full_product, "gx", split_axis=2, concat_axis=0, tiled=True)
    channel_count = lax.axis_size("gz") * mixed_sum.shape[0]
    mix_average = lax.psum(jnp.sum(mixed_sum, axis=0), "gz") / channel_count
    mix_centered = mixed_sum - mix_average
    mix_spread = lax.psum(jnp.sum(jnp.square(mix_centered), axis=0), "gz") / channel_count
    local_mix = (mix_centered * lax.rsqrt(mix_spread + epsilon) * out_gain[:, None, None]).astype(BF16)
    normed_mix = lax.all_gather(local_mix, "gz", axis=0, tiled=True)
    projected = jnp.einsum("hij,hd->dij", normed_mix, w_out, preferred_element_type=F32)
    return (out_gate * projected).astype(BF16)


def solution(mesh):
    placed = (
        P("gz", "gy", "gx"),
        P("gy", "gx"),
        P(),
        P(None, "gz"),
        P(None, "gz"),
        P(None, "gz"),
        P(None, "gz"),
        P(None, "gz"),
        P("gz"),
        P(None, "gz"),
    )
    fits = mesh.shape["gx"] == 4 and mesh.shape["gy"] == 2 and mesh.shape["gz"] == 4

    def step(*args):
        return local(*args) if fits else plain_local(*args)

    step = jax.shard_map(step, mesh=mesh, in_specs=placed, out_specs=P("gz", "gy", "gx"), check_vma=False)
    return step
```

profile of v0, /device:TPU:0, one launch (start us, length us, event | category | flops | bytes accessed | tf_op | source)
XLA Modules:
  0.0 979.3 jit_solution(13131218265121160633)
XLA Ops:
  4.9 16.8 %all_gather.3 = f32[769,128]{0,1:T(8,128)S(1)} all-gather(f32[769,32]{0,1:T(8,128)S(1)} %constant_dynamic-update-slice_fusion), channel_id=1, replica_groups=mesh['gx'=4,'gy'=2,'gz'=4] {'gz'}, dimensions={1}, use_global_device_ids=true | all-gather | bytes 492160 | tf_op jit(solution)/shard_map/all_gather | solution.py:353
  38.7 13.7 %collective-permute-done.refs_2_ = bf16[32,2,32,256]{3,2,1,0:T(8,128)(2,1)S(1)} collective-permute-done((bf16[32,2,32,256]{3,2,1,0:T(8,128)(2,1)S(1)}, bf16[32,2,32,256]{3,2,1,0:T(8,128)(2,1)S(1)}, u32[]{:S(2)}, u32[]{:S(2)}) %collective-permute-start) | collective-permute-done | bytes 1048608 | tf_op jit(solution)/shard_map/ppermute | solution.py:389
  58.9 17.1 %collective-permute-done.5.refs_6_.refs_7_ = bf16[32,2,32,256]{3,2,1,0:T(8,128)(2,1)S(1)} collective-permute-done((bf16[32,2,32,256]{3,2,1,0:T(8,128)(2,1)S(1)}, bf16[32,2,32,256]{3,2,1,0:T(8,128)(2,1)S(1)}, u32[]{:S(2)}, u32[]{:S(2)}) %collective-permute-start.5) | collective-permute-done | bytes 1048608 | tf_op jit(solution)/shard_map/ppermute | solution.py:389
  100.9 26.9 %collective-permute-start.9 = (bf16[32,2,32,256]{3,2,1,0:T(8,128)(2,1)}, bf16[32,2,32,256]{3,2,1,0:T(8,128)(2,1)}, u32[]{:S(2)}, u32[]{:S(2)}) collective-permute-start(bf16[32,2,32,256]{3,2,1,0:T(8,128)(2,1)} %get-tuple-element.267.refs_0_), channel_id=1, source_target_pairs={{0,1},{4,5},{8,9},{12,13},{16,17},{20,21},{24,25},{28,29}} | collective-permute-start | bytes 3145736 | tf_op jit(solution)/shard_map/ppermute | solution.py:389
  147.1 17.6 %collective-permute-start.13 = (bf16[32,2,32,256]{3,2,1,0:T(8,128)(2,1)S(1)}, bf16[32,2,32,256]{3,2,1,0:T(8,128)(2,1)}, u32[]{:S(2)}, u32[]{:S(2)}) collective-permute-start(bf16[32,2,32,256]{3,2,1,0:T(8,128)(2,1)S(1)} %get-tuple-element.291.refs_1_), channel_id=1, source_target_pairs={{0,1},{1,2},{2,3},{4,5},{5,6},{6,7},{8,9},{9,10},{10,11},{12,13},{... | collective-permute-start | bytes 3145736 | tf_op jit(solution)/shard_map/ppermute | solution.py:389
  182.2 11.8 %collective-permute-done.12.refs_2_ = bf16[32,2,32,256]{3,2,1,0:T(8,128)(2,1)} collective-permute-done((bf16[32,2,32,256]{3,2,1,0:T(8,128)(2,1)S(1)}, bf16[32,2,32,256]{3,2,1,0:T(8,128)(2,1)}, u32[]{:S(2)}, u32[]{:S(2)}) %collective-permute-start.12) | collective-permute-done | bytes 1048608 | tf_op jit(solution)/shard_map/ppermute | solution.py:389
  219.1 11.5 %project.8 = (bf16[32,2,32,256]{3,2,1,0:T(8,128)(2,1)}, bf16[32,2,32,256]{3,2,1,0:T(8,128)(2,1)}, bf16[32,2,32,256]{3,2,1,0:T(8,128)(2,1)}, bf16[32,2,32,256]{3,2,1,0:T(8,128)(2,1)}, bf16[2,32,128,128]{3,2,1,0:T(8,128)(2,1)}) custom-call(s32[1]{0:T(128)} %bitcast.plane_ref, bf16[32,2,32,256]{3,2,1,0:T(8,128)(2,1)} %copy-done.23, ...), custom_call_target="tpu_custom_call" | custom-call | flops 4294967296 | bytes 16777216 | tf_op jit(solution)/shard_map/project/pallas_call | solution.py:154
  239.9 15.8 %collective-permute-done.27.refs_6_ = bf16[32,2,32,256]{3,2,1,0:T(8,128)(2,1)S(1)} collective-permute-done((bf16[32,2,32,256]{3,2,1,0:T(8,128)(2,1)}, bf16[32,2,32,256]{3,2,1,0:T(8,128)(2,1)S(1)}, u32[]{:S(2)}, u32[]{:S(2)}) %collective-permute-start.27) | collective-permute-done | bytes 1048608 | tf_op jit(solution)/shard_map/ppermute | solution.py:398
  261.5 14.3 %collective-permute-start.45 = (bf16[32,2,32,256]{3,2,1,0:T(8,128)(2,1)}, bf16[32,2,32,256]{3,2,1,0:T(8,128)(2,1)}, u32[]{:S(2)}, u32[]{:S(2)}) collective-permute-start(bf16[32,2,32,256]{3,2,1,0:T(8,128)(2,1)} %get-tuple-element.303.refs_1_), channel_id=1, source_target_pairs={{0,1},{1,2},{2,3},{4,5},{5,6},{6,7},{8,9},{9,10},{10,11},{12,13},{... | collective-permute-start | bytes 3145736 | tf_op jit(solution)/shard_map/ppermute | solution.py:389
  289.6 13.6 %collective-permute-start.32 = (bf16[32,2,32,256]{3,2,1,0:T(8,128)(2,1)}, bf16[32,2,32,256]{3,2,1,0:T(8,128)(2,1)}, u32[]{:S(2)}, u32[]{:S(2)}) collective-permute-start(bf16[32,2,32,256]{3,2,1,0:T(8,128)(2,1)} %get-tuple-element.302.refs_0_), channel_id=1, source_target_pairs={{0,1},{4,5},{8,9},{12,13},{16,17},{20,21},{24,25},{28,29}} | collective-permute-start | bytes 3145736 | tf_op jit(solution)/shard_map/ppermute | solution.py:389
  327.1 20.9 %collective-permute-done.46.refs_4_ = bf16[32,2,32,256]{3,2,1,0:T(8,128)(2,1)} collective-permute-done((bf16[32,2,32,256]{3,2,1,0:T(8,128)(2,1)}, bf16[32,2,32,256]{3,2,1,0:T(8,128)(2,1)}, u32[]{:S(2)}, u32[]{:S(2)}) %collective-permute-start.46) | collective-permute-done | bytes 1048608 | tf_op jit(solution)/shard_map/ppermute | solution.py:389
  351.3 10.7 %project.12 = (bf16[32,2,32,256]{3,2,1,0:T(8,128)(2,1)}, bf16[32,2,32,256]{3,2,1,0:T(8,128)(2,1)}, bf16[32,2,32,256]{3,2,1,0:T(8,128)(2,1)}, bf16[32,2,32,256]{3,2,1,0:T(8,128)(2,1)}) custom-call(s32[1]{0:T(128)} %bitcast.plane_ref, bf16[32,2,32,256]{3,2,1,0:T(8,128)(2,1)} %copy-done.21, bf16[32,2,32,256]{3,2,1,0:T(8,128)(2,1)} %copy-done.20, ...), custom_call_target="tpu_custom_call" | custom-call | flops 4294967296 | bytes 16777216 | tf_op jit(solution)/shard_map/project/pallas_call | solution.py:154
  380.9 11.7 %project.11 = (bf16[32,2,32,256]{3,2,1,0:T(8,128)(2,1)}, bf16[32,2,32,256]{3,2,1,0:T(8,128)(2,1)}, bf16[32,2,32,256]{3,2,1,0:T(8,128)(2,1)}, bf16[32,2,32,256]{3,2,1,0:T(8,128)(2,1)}, bf16[2,32,128,128]{3,2,1,0:T(8,128)(2,1)}) custom-call(s32[1]{0:T(128)} %bitcast.plane_ref, bf16[32,2,32,256]{3,2,1,0:T(8,128)(2,1)} %get-tuple-element.267.refs_0_, ...), custom_call_target="tpu_custom_call" | custom-call | flops 4294967296 | bytes 16777216 | tf_op jit(solution)/shard_map/project/pallas_call | solution.py:154
  402.7 22.5 %collective-permute-done.64.refs_14_ = bf16[32,2,32,256]{3,2,1,0:T(8,128)(2,1)S(1)} collective-permute-done((bf16[32,2,32,256]{3,2,1,0:T(8,128)(2,1)}, bf16[32,2,32,256]{3,2,1,0:T(8,128)(2,1)S(1)}, u32[]{:S(2)}, u32[]{:S(2)}) %collective-permute-start.64) | collective-permute-done | bytes 1048608 | tf_op jit(solution)/shard_map/ppermute | solution.py:398
  448.0 11.7 %project.14 = (bf16[32,2,32,256]{3,2,1,0:T(8,128)(2,1)}, bf16[32,2,32,256]{3,2,1,0:T(8,128)(2,1)}, bf16[32,2,32,256]{3,2,1,0:T(8,128)(2,1)}, bf16[32,2,32,256]{3,2,1,0:T(8,128)(2,1)}, bf16[2,32,128,128]{3,2,1,0:T(8,128)(2,1)}) custom-call(s32[1]{0:T(128)} %bitcast.plane_ref, bf16[32,2,32,256]{3,2,1,0:T(8,128)(2,1)} %copy-done.21, ...), custom_call_target="tpu_custom_call" | custom-call | flops 4294967296 | bytes 16777216 | tf_op jit(solution)/shard_map/project/pallas_call | solution.py:154
  459.7 11.7 %project.15 = (bf16[32,2,32,256]{3,2,1,0:T(8,128)(2,1)}, bf16[32,2,32,256]{3,2,1,0:T(8,128)(2,1)}, bf16[32,2,32,256]{3,2,1,0:T(8,128)(2,1)}, bf16[32,2,32,256]{3,2,1,0:T(8,128)(2,1)}, bf16[2,32,128,128]{3,2,1,0:T(8,128)(2,1)}) custom-call(s32[1]{0:T(128)} %bitcast.plane_ref, bf16[32,2,32,256]{3,2,1,0:T(8,128)(2,1)} %get-tuple-element.302.refs_0_, ...), custom_call_target="tpu_custom_call" | custom-call | flops 4294967296 | bytes 16777216 | tf_op jit(solution)/shard_map/project/pallas_call | solution.py:154
  471.6 43.1 %collective-permute-done.73.refs_18_ = bf16[32,2,32,256]{3,2,1,0:T(8,128)(2,1)} collective-permute-done((bf16[32,2,32,256]{3,2,1,0:T(8,128)(2,1)}, bf16[32,2,32,256]{3,2,1,0:T(8,128)(2,1)}, u32[]{:S(2)}, u32[]{:S(2)}) %collective-permute-start.73) | collective-permute-done | bytes 1048608 | tf_op jit(solution)/shard_map/ppermute | solution.py:398
  515.3 20.8 %collective-permute-done.66.refs_1_ = bf16[32,2,32,256]{3,2,1,0:T(8,128)(2,1)} collective-permute-done((bf16[32,2,32,256]{3,2,1,0:T(8,128)(2,1)}, bf16[32,2,32,256]{3,2,1,0:T(8,128)(2,1)}, u32[]{:S(2)}, u32[]{:S(2)}) %collective-permute-start.66) | collective-permute-done | bytes 1048608 | tf_op jit(solution)/shard_map/ppermute | solution.py:398
  546.0 21.4 %product.4 = (bf16[32,2,32,128]{3,2,1,0:T(8,128)(2,1)}, bf16[32,2,32,128]{3,2,1,0:T(8,128)(2,1)}, bf16[32,2,32,128]{3,2,1,0:T(8,128)(2,1)}, bf16[32,2,32,128]{3,2,1,0:T(8,128)(2,1)}) custom-call(s32[4]{0:T(128)} %iota_xor_fusion.target_ref, bf16[32,2,32,256]{3,2,1,0:T(8,128)(2,1)} %get-tuple-element.356.refs_0_, ...), custom_call_target="tpu_custom_call" | custom-call | flops 2147483648 | bytes 37748736 | tf_op jit(solution)/shard_map/product/pallas_call | solution.py:216
  567.4 20.7 %collective-permute-done.67.refs_2_ = bf16[32,2,32,256]{3,2,1,0:T(8,128)(2,1)} collective-permute-done((bf16[32,2,32,256]{3,2,1,0:T(8,128)(2,1)}, bf16[32,2,32,256]{3,2,1,0:T(8,128)(2,1)}, u32[]{:S(2)}, u32[]{:S(2)}) %collective-permute-start.67) | collective-permute-done | bytes 1048608 | tf_op jit(solution)/shard_map/ppermute | solution.py:398
  588.1 21.3 %product.5 = (bf16[32,2,32,128]{3,2,1,0:T(8,128)(2,1)}, bf16[32,2,32,128]{3,2,1,0:T(8,128)(2,1)}, bf16[32,2,32,128]{3,2,1,0:T(8,128)(2,1)}, bf16[32,2,32,128]{3,2,1,0:T(8,128)(2,1)}) custom-call(s32[4]{0:T(128)} %iota_xor_fusion.target_ref, bf16[32,2,32,256]{3,2,1,0:T(8,128)(2,1)} %get-tuple-element.385.refs_0_, ...), custom_call_target="tpu_custom_call" | custom-call | flops 2147483648 | bytes 37748736 | tf_op jit(solution)/shard_map/product/pallas_call | solution.py:216
  611.6 21.2 %collective-permute-done.61.refs_2_ = bf16[32,2,32,256]{3,2,1,0:T(8,128)(2,1)} collective-permute-done((bf16[32,2,32,256]{3,2,1,0:T(8,128)(2,1)}, bf16[32,2,32,256]{3,2,1,0:T(8,128)(2,1)}, u32[]{:S(2)}, u32[]{:S(2)}) %collective-permute-start.61) | collective-permute-done | bytes 1048608 | tf_op jit(solution)/shard_map/ppermute | solution.py:398
  639.8 15.5 %collective-permute-done.87.refs_2_ = bf16[32,2,32,128]{3,2,1,0:T(8,128)(2,1)} collective-permute-done((bf16[32,2,32,128]{3,2,1,0:T(8,128)(2,1)}, bf16[32,2,32,128]{3,2,1,0:T(8,128)(2,1)}, u32[]{:S(2)}, u32[]{:S(2)}) %collective-permute-start.87) | collective-permute-done | bytes 524320 | tf_op jit(solution)/shard_map/ppermute | solution.py:398
  659.9 21.3 %product.6 = (bf16[32,2,32,128]{3,2,1,0:T(8,128)(2,1)}, bf16[32,2,32,128]{3,2,1,0:T(8,128)(2,1)}, bf16[32,2,32,128]{3,2,1,0:T(8,128)(2,1)}, bf16[32,2,32,128]{3,2,1,0:T(8,128)(2,1)}) custom-call(s32[4]{0:T(128)} %iota_xor_fusion.target_ref, bf16[32,2,32,256]{3,2,1,0:T(8,128)(2,1)} %get-tuple-element.399.refs_0_, ...), custom_call_target="tpu_custom_call" | custom-call | flops 2147483648 | bytes 37748736 | tf_op jit(solution)/shard_map/product/pallas_call | solution.py:216
  681.1 41.1 %collective-permute-done.84.refs_2_ = bf16[32,2,32,128]{3,2,1,0:T(8,128)(2,1)} collective-permute-done((bf16[32,2,32,128]{3,2,1,0:T(8,128)(2,1)}, bf16[32,2,32,128]{3,2,1,0:T(8,128)(2,1)}, u32[]{:S(2)}, u32[]{:S(2)}) %collective-permute-start.84) | collective-permute-done | bytes 524320 | tf_op jit(solution)/shard_map/ppermute | solution.py:398
  739.7 27.2 %collective-permute-start.98 = (bf16[32,2,32,128]{3,2,1,0:T(8,128)(2,1)}, bf16[32,2,32,128]{3,2,1,0:T(8,128)(2,1)}, u32[]{:S(2)}, u32[]{:S(2)}) collective-permute-start(bf16[32,2,32,128]{3,2,1,0:T(8,128)(2,1)} %get-tuple-element.448), channel_id=1, source_target_pairs={{0,1},{1,0},{2,3},{3,2},{4,5},{5,4},{6,7},{7,6},{8,9},{9,8},{10,11... | collective-permute-start | bytes 1572872 | tf_op jit(solution)/shard_map/ppermute | solution.py:398
  767.8 21.3 %product.7 = (bf16[32,2,32,128]{3,2,1,0:T(8,128)(2,1)}, bf16[32,2,32,128]{3,2,1,0:T(8,128)(2,1)}, bf16[32,2,32,128]{3,2,1,0:T(8,128)(2,1)}, bf16[32,2,32,128]{3,2,1,0:T(8,128)(2,1)}) custom-call(s32[4]{0:T(128)} %iota_xor_fusion.target_ref, bf16[32,2,32,256]{3,2,1,0:T(8,128)(2,1)} %get-tuple-element.426.refs_0_, bf16[32,2,32,256]{3,2,1,0:T(8,128)(2,1)} %copy-done.24, ...), custom_call_target="tpu_custom_call" | custom-call | flops 2147483648 | bytes 37748736 | tf_op jit(solution)/shard_map/product/pallas_call | solution.py:216
  822.2 35.2 %collective-permute-done.102.refs_8_ = bf16[32,2,32,128]{3,2,1,0:T(8,128)(2,1)S(1)} collective-permute-done((bf16[32,2,32,128]{3,2,1,0:T(8,128)(2,1)}, bf16[32,2,32,128]{3,2,1,0:T(8,128)(2,1)S(1)}, u32[]{:S(2)}, u32[]{:S(2)}) %collective-permute-start.102) | collective-permute-done | bytes 524320 | tf_op jit(solution)/shard_map/ppermute | solution.py:398
  857.4 22.4 %collective-permute-done.103.refs_9_ = bf16[32,2,32,128]{3,2,1,0:T(8,128)(2,1)S(1)} collective-permute-done((bf16[32,2,32,128]{3,2,1,0:T(8,128)(2,1)}, bf16[32,2,32,128]{3,2,1,0:T(8,128)(2,1)S(1)}, u32[]{:S(2)}, u32[]{:S(2)}) %collective-permute-start.103) | collective-permute-done | bytes 524320 | tf_op jit(solution)/shard_map/ppermute | solution.py:398
  880.7 22.1 %collective-permute-start.101 = (bf16[32,2,32,128]{3,2,1,0:T(8,128)(2,1)}, bf16[32,2,32,128]{3,2,1,0:T(8,128)(2,1)}, u32[]{:S(2)}, u32[]{:S(2)}) collective-permute-start(bf16[32,2,32,128]{3,2,1,0:T(8,128)(2,1)} %get-tuple-element.451), channel_id=1, source_target_pairs={{0,1},{1,0},{2,3},{3,2},{4,5},{5,4},{6,7},{7,6},{8,9},{9,8},{10,11... | collective-permute-start | bytes 1572872 | tf_op jit(solution)/shard_map/ppermute | solution.py:398
  916.5 30.8 %collective-permute-done.104.refs_10_ = bf16[32,2,32,128]{3,2,1,0:T(8,128)(2,1)S(1)} collective-permute-done((bf16[32,2,32,128]{3,2,1,0:T(8,128)(2,1)}, bf16[32,2,32,128]{3,2,1,0:T(8,128)(2,1)S(1)}, u32[]{:S(2)}, u32[]{:S(2)}) %collective-permute-start.104) | collective-permute-done | bytes 524320 | tf_op jit(solution)/shard_map/ppermute | solution.py:398
  947.3 22.6 %collective-permute-done.105.refs_11_ = bf16[32,2,32,128]{3,2,1,0:T(8,128)(2,1)} collective-permute-done((bf16[32,2,32,128]{3,2,1,0:T(8,128)(2,1)}, bf16[32,2,32,128]{3,2,1,0:T(8,128)(2,1)}, u32[]{:S(2)}, u32[]{:S(2)}) %collective-permute-start.105) | collective-permute-done | bytes 524320 | tf_op jit(solution)/shard_map/ppermute | solution.py:398
  (379 shorter events, 322.0 us)
Async XLA Ops:
  77.3 50.5 %collective-permute-start.17 = (bf16[32,2,32,256]{3,2,1,0:T(8,128)(2,1)}, bf16[32,2,32,256]{3,2,1,0:T(8,128)(2,1)}, u32[]{:S(2)}, u32[]{:S(2)}) collective-permute-start(bf16[32,2,32,256]{3,2,1,0:T(8,128)(2,1)} %get-tuple-element.266.refs_1_), channel_id=1, source_target_pairs={{0,1},{1,2},{2,3},{4,5},{5,6},{6,7},{8,9},{9,10},{10,11},{12,13},{... | collective-permute-start | bytes 3145736 | tf_op jit(solution)/shard_map/ppermute | solution.py:389
  88.0 49.9 %collective-permute-start.7 = (bf16[32,2,32,256]{3,2,1,0:T(8,128)(2,1)}, bf16[32,2,32,256]{3,2,1,0:T(8,128)(2,1)}, u32[]{:S(2)}, u32[]{:S(2)}) collective-permute-start(bf16[32,2,32,256]{3,2,1,0:T(8,128)(2,1)} %copy-done.36), channel_id=1, source_target_pairs={{1,2},{5,6},{9,10},{13,14},{17,18},{21,22},{25,26},{29,30}} | collective-permute-start | bytes 3145736 | tf_op jit(solution)/shard_map/ppermute | solution.py:389
  89.6 49.6 %collective-permute-start.8 = (bf16[32,2,32,256]{3,2,1,0:T(8,128)(2,1)}, bf16[32,2,32,256]{3,2,1,0:T(8,128)(2,1)}, u32[]{:S(2)}, u32[]{:S(2)}) collective-permute-start(bf16[32,2,32,256]{3,2,1,0:T(8,128)(2,1)} %get-tuple-element.266.refs_1_), channel_id=1, source_target_pairs={{3,2},{7,6},{11,10},{15,14},{19,18},{23,22},{27,26},{31,30}} | collective-permute-start | bytes 3145736 | tf_op jit(solution)/shard_map/ppermute | solution.py:389
  147.1 61.1 %collective-permute-start.13 = (bf16[32,2,32,256]{3,2,1,0:T(8,128)(2,1)S(1)}, bf16[32,2,32,256]{3,2,1,0:T(8,128)(2,1)}, u32[]{:S(2)}, u32[]{:S(2)}) collective-permute-start(bf16[32,2,32,256]{3,2,1,0:T(8,128)(2,1)S(1)} %get-tuple-element.291.refs_1_), channel_id=1, source_target_pairs={{0,1},{1,2},{2,3},{4,5},{5,6},{6,7},{8,9},{9,10},{10,11},{12,13},{... | collective-permute-start | bytes 3145736 | tf_op jit(solution)/shard_map/ppermute | solution.py:389
  232.1 54.4 %collective-permute-start.15 = (bf16[32,2,32,256]{3,2,1,0:T(8,128)(2,1)}, bf16[32,2,32,256]{3,2,1,0:T(8,128)(2,1)}, u32[]{:S(2)}, u32[]{:S(2)}) collective-permute-start(bf16[32,2,32,256]{3,2,1,0:T(8,128)(2,1)} %collective-permute-done.13.refs_3_), channel_id=1, source_target_pairs={{1,2},{2,3},{5,6},{6,7},{9,10},{10,11},{13,14},{14,15},{17,18},{18... | collective-permute-start | bytes 3145736 | tf_op jit(solution)/shard_map/ppermute | solution.py:389
  444.1 70.5 %collective-permute-start.73 = (bf16[32,2,32,256]{3,2,1,0:T(8,128)(2,1)}, bf16[32,2,32,256]{3,2,1,0:T(8,128)(2,1)}, u32[]{:S(2)}, u32[]{:S(2)}) collective-permute-start(bf16[32,2,32,256]{3,2,1,0:T(8,128)(2,1)} %get-tuple-element.366), channel_id=1, source_target_pairs={{0,16},{8,24},{16,0},{24,8},{1,17},{9,25},{17,1},{25,9},{2,18},{10... | collective-permute-start | bytes 3145736 | tf_op jit(solution)/shard_map/ppermute | solution.py:398
  444.4 70.3 %collective-permute-start.74 = (bf16[32,2,32,256]{3,2,1,0:T(8,128)(2,1)}, bf16[32,2,32,256]{3,2,1,0:T(8,128)(2,1)}, u32[]{:S(2)}, u32[]{:S(2)}) collective-permute-start(bf16[32,2,32,256]{3,2,1,0:T(8,128)(2,1)} %get-tuple-element.367), channel_id=1, source_target_pairs={{0,24},{8,16},{16,8},{24,0},{1,25},{9,17},{17,9},{25,1},{2,26},{10... | collective-permute-start | bytes 3145736 | tf_op jit(solution)/shard_map/ppermute | solution.py:398
  446.3 68.9 %collective-permute-start.71 = (bf16[32,2,32,256]{3,2,1,0:T(8,128)(2,1)}, bf16[32,2,32,256]{3,2,1,0:T(8,128)(2,1)}, u32[]{:S(2)}, u32[]{:S(2)}) collective-permute-start(bf16[32,2,32,256]{3,2,1,0:T(8,128)(2,1)} %get-tuple-element.355), channel_id=1, source_target_pairs={{0,24},{8,16},{16,8},{24,0},{1,25},{9,17},{17,9},{25,1},{2,26},{10... | collective-permute-start | bytes 3145736 | tf_op jit(solution)/shard_map/ppermute | solution.py:398
  447.4 88.7 %collective-permute-start.66 = (bf16[32,2,32,256]{3,2,1,0:T(8,128)(2,1)}, bf16[32,2,32,256]{3,2,1,0:T(8,128)(2,1)}, u32[]{:S(2)}, u32[]{:S(2)}) collective-permute-start(bf16[32,2,32,256]{3,2,1,0:T(8,128)(2,1)} %get-tuple-element.349), channel_id=1, source_target_pairs={{0,8},{8,0},{16,24},{24,16},{1,9},{9,1},{17,25},{25,17},{2,10},{10... | collective-permute-start | bytes 3145736 | tf_op jit(solution)/shard_map/ppermute | solution.py:398
  471.5 64.6 %collective-permute-start.75 = (bf16[32,2,32,256]{3,2,1,0:T(8,128)(2,1)S(1)}, bf16[32,2,32,256]{3,2,1,0:T(8,128)(2,1)S(1)}, u32[]{:S(2)}, u32[]{:S(2)}) collective-permute-start(bf16[32,2,32,256]{3,2,1,0:T(8,128)(2,1)S(1)} %copy-done.8), channel_id=1, source_target_pairs={{0,4},{4,0},{1,5},{5,1},{2,6},{6,2},{3,7},{7,3},{8,12},{12,8},{9,1... | collective-permute-start | bytes 3145736 | tf_op jit(solution)/shard_map/ppermute | solution.py:398
  541.9 69.6 %collective-permute-start.60 = (bf16[32,2,32,256]{3,2,1,0:T(8,128)(2,1)}, bf16[32,2,32,256]{3,2,1,0:T(8,128)(2,1)}, u32[]{:S(2)}, u32[]{:S(2)}) collective-permute-start(bf16[32,2,32,256]{3,2,1,0:T(8,128)(2,1)} %get-tuple-element.332), channel_id=1, source_target_pairs={{0,8},{8,0},{16,24},{24,16},{1,9},{9,1},{17,25},{25,17},{2,10},{10... | collective-permute-start | bytes 3145736 | tf_op jit(solution)/shard_map/ppermute | solution.py:398
  542.5 90.3 %collective-permute-start.61 = (bf16[32,2,32,256]{3,2,1,0:T(8,128)(2,1)}, bf16[32,2,32,256]{3,2,1,0:T(8,128)(2,1)}, u32[]{:S(2)}, u32[]{:S(2)}) collective-permute-start(bf16[32,2,32,256]{3,2,1,0:T(8,128)(2,1)} %get-tuple-element.333), channel_id=1, source_target_pairs={{0,16},{8,24},{16,0},{24,8},{1,17},{9,25},{17,1},{25,9},{2,18},{10... | collective-permute-start | bytes 3145736 | tf_op jit(solution)/shard_map/ppermute | solution.py:398
  543.4 90.5 %collective-permute-start.62 = (bf16[32,2,32,256]{3,2,1,0:T(8,128)(2,1)}, bf16[32,2,32,256]{3,2,1,0:T(8,128)(2,1)}, u32[]{:S(2)}, u32[]{:S(2)}) collective-permute-start(bf16[32,2,32,256]{3,2,1,0:T(8,128)(2,1)} %get-tuple-element.334), channel_id=1, source_target_pairs={{0,24},{8,16},{16,8},{24,0},{1,25},{9,17},{17,9},{25,1},{2,26},{10... | collective-permute-start | bytes 3145736 | tf_op jit(solution)/shard_map/ppermute | solution.py:398
  633.9 90.0 %collective-permute-start.89 = (bf16[32,2,32,256]{3,2,1,0:T(8,128)(2,1)}, bf16[32,2,32,256]{3,2,1,0:T(8,128)(2,1)S(1)}, u32[]{:S(2)}, u32[]{:S(2)}) collective-permute-start(bf16[32,2,32,256]{3,2,1,0:T(8,128)(2,1)} %get-tuple-element.412), channel_id=1, source_target_pairs={{0,8},{8,0},{16,24},{24,16},{1,9},{9,1},{17,25},{25,17},{2,10},{10... | collective-permute-start | bytes 3145736 | tf_op jit(solution)/shard_map/ppermute | solution.py:398
  635.4 104.3 %collective-permute-start.90 = (bf16[32,2,32,256]{3,2,1,0:T(8,128)(2,1)}, bf16[32,2,32,256]{3,2,1,0:T(8,128)(2,1)S(1)}, u32[]{:S(2)}, u32[]{:S(2)}) collective-permute-start(bf16[32,2,32,256]{3,2,1,0:T(8,128)(2,1)} %get-tuple-element.413), channel_id=1, source_target_pairs={{0,16},{8,24},{16,0},{24,8},{1,17},{9,25},{17,1},{25,9},{2,18},{10... | collective-permute-start | bytes 3145736 | tf_op jit(solution)/shard_map/ppermute | solution.py:398
  637.1 129.7 %collective-permute-start.91 = (bf16[32,2,32,256]{3,2,1,0:T(8,128)(2,1)}, bf16[32,2,32,256]{3,2,1,0:T(8,128)(2,1)S(1)}, u32[]{:S(2)}, u32[]{:S(2)}) collective-permute-start(bf16[32,2,32,256]{3,2,1,0:T(8,128)(2,1)} %get-tuple-element.414), channel_id=1, source_target_pairs={{0,24},{8,16},{16,8},{24,0},{1,25},{9,17},{17,9},{25,1},{2,26},{10... | collective-permute-start | bytes 3145736 | tf_op jit(solution)/shard_map/ppermute | solution.py:398
  655.3 67.0 %collective-permute-start.84 = (bf16[32,2,32,128]{3,2,1,0:T(8,128)(2,1)}, bf16[32,2,32,128]{3,2,1,0:T(8,128)(2,1)}, u32[]{:S(2)}, u32[]{:S(2)}) collective-permute-start(bf16[32,2,32,128]{3,2,1,0:T(8,128)(2,1)} %get-tuple-element.393), channel_id=1, source_target_pairs={{0,16},{8,24},{16,0},{24,8},{1,17},{9,25},{17,1},{25,9},{2,18},{10... | collective-permute-start | bytes 1572872 | tf_op jit(solution)/shard_map/ppermute | solution.py:398
  655.6 68.0 %collective-permute-start.85 = (bf16[32,2,32,128]{3,2,1,0:T(8,128)(2,1)}, bf16[32,2,32,128]{3,2,1,0:T(8,128)(2,1)}, u32[]{:S(2)}, u32[]{:S(2)}) collective-permute-start(bf16[32,2,32,128]{3,2,1,0:T(8,128)(2,1)} %get-tuple-element.394), channel_id=1, source_target_pairs={{0,24},{8,16},{16,8},{24,0},{1,25},{9,17},{17,9},{25,1},{2,26},{10... | collective-permute-start | bytes 1572872 | tf_op jit(solution)/shard_map/ppermute | solution.py:398
  722.2 66.9 %collective-permute-start.92 = (bf16[32,2,32,128]{3,2,1,0:T(8,128)(2,1)}, bf16[32,2,32,128]{3,2,1,0:T(8,128)(2,1)}, u32[]{:S(2)}, u32[]{:S(2)}) collective-permute-start(bf16[32,2,32,128]{3,2,1,0:T(8,128)(2,1)} %get-tuple-element.423), channel_id=1, source_target_pairs={{0,8},{8,0},{16,24},{24,16},{1,9},{9,1},{17,25},{25,17},{2,10},{10... | collective-permute-start | bytes 1572872 | tf_op jit(solution)/shard_map/ppermute | solution.py:398
  723.6 65.9 %collective-permute-start.93 = (bf16[32,2,32,128]{3,2,1,0:T(8,128)(2,1)}, bf16[32,2,32,128]{3,2,1,0:T(8,128)(2,1)}, u32[]{:S(2)}, u32[]{:S(2)}) collective-permute-start(bf16[32,2,32,128]{3,2,1,0:T(8,128)(2,1)} %get-tuple-element.424), channel_id=1, source_target_pairs={{0,16},{8,24},{16,0},{24,8},{1,17},{9,25},{17,1},{25,9},{2,18},{10... | collective-permute-start | bytes 1572872 | tf_op jit(solution)/shard_map/ppermute | solution.py:398
  723.9 66.2 %collective-permute-start.94 = (bf16[32,2,32,128]{3,2,1,0:T(8,128)(2,1)}, bf16[32,2,32,128]{3,2,1,0:T(8,128)(2,1)}, u32[]{:S(2)}, u32[]{:S(2)}) collective-permute-start(bf16[32,2,32,128]{3,2,1,0:T(8,128)(2,1)} %get-tuple-element.425), channel_id=1, source_target_pairs={{0,24},{8,16},{16,8},{24,0},{1,25},{9,17},{17,9},{25,1},{2,26},{10... | collective-permute-start | bytes 1572872 | tf_op jit(solution)/shard_map/ppermute | solution.py:398
  739.7 59.6 %collective-permute-start.98 = (bf16[32,2,32,128]{3,2,1,0:T(8,128)(2,1)}, bf16[32,2,32,128]{3,2,1,0:T(8,128)(2,1)}, u32[]{:S(2)}, u32[]{:S(2)}) collective-permute-start(bf16[32,2,32,128]{3,2,1,0:T(8,128)(2,1)} %get-tuple-element.448), channel_id=1, source_target_pairs={{0,1},{1,0},{2,3},{3,2},{4,5},{5,4},{6,7},{7,6},{8,9},{9,8},{10,11... | collective-permute-start | bytes 1572872 | tf_op jit(solution)/shard_map/ppermute | solution.py:398
  799.3 58.1 %collective-permute-start.102 = (bf16[32,2,32,128]{3,2,1,0:T(8,128)(2,1)}, bf16[32,2,32,128]{3,2,1,0:T(8,128)(2,1)S(1)}, u32[]{:S(2)}, u32[]{:S(2)}) collective-permute-start(bf16[32,2,32,128]{3,2,1,0:T(8,128)(2,1)} %get-tuple-element.452), channel_id=1, source_target_pairs={{0,2},{1,3},{2,0},{3,1},{4,6},{5,7},{6,4},{7,5},{8,10},{9,11},{10,... | collective-permute-start | bytes 1572872 | tf_op jit(solution)/shard_map/ppermute | solution.py:398
  799.4 80.4 %collective-permute-start.103 = (bf16[32,2,32,128]{3,2,1,0:T(8,128)(2,1)}, bf16[32,2,32,128]{3,2,1,0:T(8,128)(2,1)S(1)}, u32[]{:S(2)}, u32[]{:S(2)}) collective-permute-start(bf16[32,2,32,128]{3,2,1,0:T(8,128)(2,1)} %get-tuple-element.453), channel_id=1, source_target_pairs={{0,2},{1,3},{2,0},{3,1},{4,6},{5,7},{6,4},{7,5},{8,10},{9,11},{10,... | collective-permute-start | bytes 1572872 | tf_op jit(solution)/shard_map/ppermute | solution.py:398
  804.2 76.5 %collective-permute-start.106 = (bf16[32,2,32,128]{3,2,1,0:T(8,128)(2,1)}, bf16[32,2,32,128]{3,2,1,0:T(8,128)(2,1)S(1)}, u32[]{:S(2)}, u32[]{:S(2)}) collective-permute-start(bf16[32,2,32,128]{3,2,1,0:T(8,128)(2,1)} %get-tuple-element.456), channel_id=1, source_target_pairs={{0,3},{1,2},{2,1},{3,0},{4,7},{5,6},{6,5},{7,4},{8,11},{9,10},{10,... | collective-permute-start | bytes 1572872 | tf_op jit(solution)/shard_map/ppermute | solution.py:398
  813.9 89.0 %collective-permute-start.107 = (bf16[32,2,32,128]{3,2,1,0:T(8,128)(2,1)}, bf16[32,2,32,128]{3,2,1,0:T(8,128)(2,1)S(1)}, u32[]{:S(2)}, u32[]{:S(2)}) collective-permute-start(bf16[32,2,32,128]{3,2,1,0:T(8,128)(2,1)} %get-tuple-element.457), channel_id=1, source_target_pairs={{0,3},{1,2},{2,1},{3,0},{4,7},{5,6},{6,5},{7,4},{8,11},{9,10},{10,... | collective-permute-start | bytes 1572872 | tf_op jit(solution)/shard_map/ppermute | solution.py:398
  814.7 98.8 %collective-permute-start.100 = (bf16[32,2,32,128]{3,2,1,0:T(8,128)(2,1)}, bf16[32,2,32,128]{3,2,1,0:T(8,128)(2,1)S(1)}, u32[]{:S(2)}, u32[]{:S(2)}) collective-permute-start(bf16[32,2,32,128]{3,2,1,0:T(8,128)(2,1)} %get-tuple-element.450), channel_id=1, source_target_pairs={{0,1},{1,0},{2,3},{3,2},{4,5},{5,4},{6,7},{7,6},{8,9},{9,8},{10,11... | collective-permute-start | bytes 1572872 | tf_op jit(solution)/shard_map/ppermute | solution.py:398
  857.4 89.9 %collective-permute-start.104 = (bf16[32,2,32,128]{3,2,1,0:T(8,128)(2,1)}, bf16[32,2,32,128]{3,2,1,0:T(8,128)(2,1)S(1)}, u32[]{:S(2)}, u32[]{:S(2)}) collective-permute-start(bf16[32,2,32,128]{3,2,1,0:T(8,128)(2,1)} %get-tuple-element.454), channel_id=1, source_target_pairs={{0,2},{1,3},{2,0},{3,1},{4,6},{5,7},{6,4},{7,5},{8,10},{9,11},{10,... | collective-permute-start | bytes 1572872 | tf_op jit(solution)/shard_map/ppermute | solution.py:398
  879.8 67.5 %collective-permute-start.108 = (bf16[32,2,32,128]{3,2,1,0:T(8,128)(2,1)}, bf16[32,2,32,128]{3,2,1,0:T(8,128)(2,1)}, u32[]{:S(2)}, u32[]{:S(2)}) collective-permute-start(bf16[32,2,32,128]{3,2,1,0:T(8,128)(2,1)} %get-tuple-element.458), channel_id=1, source_target_pairs={{0,3},{1,2},{2,1},{3,0},{4,7},{5,6},{6,5},{7,4},{8,11},{9,10},{10,... | collective-permute-start | bytes 1572872 | tf_op jit(solution)/shard_map/ppermute | solution.py:398
  880.7 66.6 %collective-permute-start.101 = (bf16[32,2,32,128]{3,2,1,0:T(8,128)(2,1)}, bf16[32,2,32,128]{3,2,1,0:T(8,128)(2,1)}, u32[]{:S(2)}, u32[]{:S(2)}) collective-permute-start(bf16[32,2,32,128]{3,2,1,0:T(8,128)(2,1)} %get-tuple-element.451), channel_id=1, source_target_pairs={{0,1},{1,0},{2,3},{3,2},{4,5},{5,4},{6,7},{7,6},{8,9},{9,8},{10,11... | collective-permute-start | bytes 1572872 | tf_op jit(solution)/shard_map/ppermute | solution.py:398
  902.9 67.0 %collective-permute-start.105 = (bf16[32,2,32,128]{3,2,1,0:T(8,128)(2,1)}, bf16[32,2,32,128]{3,2,1,0:T(8,128)(2,1)}, u32[]{:S(2)}, u32[]{:S(2)}) collective-permute-start(bf16[32,2,32,128]{3,2,1,0:T(8,128)(2,1)} %get-tuple-element.455), channel_id=1, source_target_pairs={{0,2},{1,3},{2,0},{3,1},{4,6},{5,7},{6,4},{7,5},{8,10},{9,11},{10,... | collective-permute-start | bytes 1572872 | tf_op jit(solution)/shard_map/ppermute | solution.py:398
  913.5 56.3 %collective-permute-start.109 = (bf16[32,2,32,128]{3,2,1,0:T(8,128)(2,1)}, bf16[32,2,32,128]{3,2,1,0:T(8,128)(2,1)}, u32[]{:S(2)}, u32[]{:S(2)}) collective-permute-start(bf16[32,2,32,128]{3,2,1,0:T(8,128)(2,1)} %get-tuple-element.459), channel_id=1, source_target_pairs={{0,3},{1,2},{2,1},{3,0},{4,7},{5,6},{6,5},{7,4},{8,11},{9,10},{10,... | collective-permute-start | bytes 1572872 | tf_op jit(solution)/shard_map/ppermute | solution.py:398
  (127 other events, 3836.1 us)
where the time goes:
time: 995 us; the launch traced here: 979 us
  waiting for transfers between devices  443 us (45%)
  starting transfers between devices  266 us (27%)
  Pallas kernels  210 us (21%)
  local copies, waits for them, and re-layouts  32.1 us (3%)
  blocking collectives  16.8 us (2%)
    ppermute x64, waiting for transfers between devices, swap(): lax.ppermute(value, axis, [(i, i ^ bits) for i in range(lax.axis_size(axi...  340 us
    ppermute x46, starting transfers between devices, start(): values[kind, g, way] = lax.ppermute(values[source], 'gz', pairs)  153 us
    ppermute x64, starting transfers between devices, swap(): lax.ppermute(value, axis, [(i, i ^ bits) for i in range(lax.axis_size(axi...  114 us
    ppermute x46, waiting for transfers between devices, start(): values[kind, g, way] = lax.ppermute(values[source], 'gz', pairs)  104 us
    pallas_call x8, Pallas kernels, project(): pl.pallas_call(functools.partial(project_kernel, planes, emit, parts), gr...  89.4 us
    pallas_call x4, Pallas kernels, product(): pl.pallas_call(functools.partial(product_kernel, parts, chunks, left_chun...  85.3 us
    pallas_call x4, Pallas kernels, finish(): pl.pallas_call(functools.partial(finish_kernel, len(mixed)), grid=(blocks...  26.5 us
  transfers between devices with their start and end apart: 110, of which 30 were waited for; matrix products, arithmetic and copies ran while one was open for 2% of the time, Pallas kernels for 21%

commit v1 on v0

--- a/solution.py
+++ b/solution.py
@@ -19,30 +19,30 @@
 ROW_ORDER = ((0, 1, 2, 3), (1, 0, 2, 3), (2, 3, 1, 0), (3, 2, 1, 0))
 COL_ORDER = ((0, 1, 2, 3), (1, 2, 3, 0), (2, 1, 0, 3), (3, 2, 1, 0))
 
-MESSAGES = {
-    "1": ("own", ((3, 2), (2, 1), (1, 0)), ((0, 1), (1, 2), (2, 3))),
-    "2": ("1", ((2, 1), (1, 0)), ((1, 2), (2, 3))),
-    "3": ("2", ((1, 0),), ((2, 3),)),
-    "s": ("side", ((3, 2), (2, 1)), ((0, 1), (1, 2))),
-    "r": ("side", ((3, 2),), ((0, 1),)),
-    "t": ("side", ((2, 1),), ((1, 2),)),
-    "l": ("far", ((2, 1),), ((1, 2),)),
+HOPS = {
+    "1d": ((3, 2), (2, 1), (1, 0)),
+    "1u": ((0, 1), (1, 2), (2, 3)),
+    "2d": ((2, 1), (1, 0)),
+    "2u": ((1, 2), (2, 3)),
+    "x": ((0, 1), (1, 0), (2, 3), (3, 2)),
+    "t": ((0, 0), (1, 2), (2, 1), (3, 3)),
+    "l": ((0, 0), (1, 2), (2, 1), (3, 3)),
 }
 EVENTS = (
     (("1", 0),),
-    (("s", 0),),
+    (("x", None, 0), ("t", 0)),
     (("2", 0),),
     (("1", 1),),
-    (("l", 0), ("r", 1), ("3", 0)),
+    (("l", 0), ("x", 0, 1)),
     (("2", 1),),
     (("1", 2),),
-    (("t", 1), ("r", 2), ("3", 1)),
+    (("t", 1), ("x", 1, 2)),
     (("2", 2),),
     (("1", 3),),
-    (("l", 1), ("r", 3), ("3", 2)),
+    (("l", 1), ("x", 2, 3)),
     (("2", 3),),
     (("t", 2),),
-    (("l", 2), ("3", 3)),
+    (("l", 2), ("x", 3, None)),
     (("t", 3),),
     (("l", 3),),
 )
@@ -57,14 +57,13 @@
     15: (("right", 3), ("left", 2)),
 }
 TAIL = (
-    ("multiply", 0),
-    ("multiply", 1),
+    ("multiply", (0, 1)),
+    ("multiply", (2,)),
+    ("complete", 0),
     ("share", 3),
-    ("multiply", 2),
-    ("complete", 0),
     ("complete", 1),
-    ("multiply", 3),
     ("complete", 2),
+    ("multiply", (3,)),
     ("complete", 3),
 )
 
@@ -184,8 +183,8 @@
     for head in range(heads):
         rows = [
             jnp.concatenate([lefts[c * parts + m][head, n] for m in range(parts)], axis=1)
+            for c in range(left_chunks)
             for n in range(blocks)
-            for c in range(left_chunks)
         ]
         left = jnp.concatenate(rows, axis=0)
         rows = [
@@ -203,7 +202,10 @@
             value = pieces[0]
             for p in range(1, len(pieces)):
                 value = jnp.where(pick == p, pieces[p], value)
-            outs[m][head] = value.astype(BF16).reshape(blocks, left_chunks * size, span)
+            value = value.astype(BF16)
+            for c in range(left_chunks):
+                rows = blocks * size
+                outs[c * parts + m][head] = value[c * rows : (c + 1) * rows].reshape(blocks, size, span)
 
 
 def product(target, lefts, rights, parts, heads):
@@ -217,8 +219,8 @@
         functools.partial(product_kernel, parts, chunks, left_chunks),
         grid=(hidden // heads,),
         in_specs=[pl.BlockSpec(memory_space=pltpu.SMEM)] + [left_block] * (len(lefts) + len(rights)),
-        out_specs=[pl.BlockSpec((heads, blocks, left_chunks * size, span), lambda h: (h, 0, 0, 0))] * parts,
-        out_shape=[jax.ShapeDtypeStruct((hidden, blocks, left_chunks * size, span), BF16)] * parts,
+        out_specs=[pl.BlockSpec((heads, blocks, size, span), lambda h: (h, 0, 0, 0))] * len(lefts),
+        out_shape=[jax.ShapeDtypeStruct((hidden, blocks, size, span), BF16)] * len(lefts),
         compiler_params=pltpu.CompilerParams(dimension_semantics=(ARBITRARY,)),
         cost_estimate=pl.CostEstimate(
             flops=2 * hidden * rows * (cores * blocks * span) * width * parts,
@@ -291,7 +293,7 @@
 
 
 def assemble_kernel(planes, chunks, plane_ref, *refs):
-    ins, out = refs[:-1], refs[-1]
+    ins, out = refs[: planes * chunks], refs[-1]
     plane = plane_ref[0]
     size = ins[0].shape[2]
     for mine in range(planes):
@@ -306,20 +308,28 @@
                     ][:, 0]
 
 
-def assemble(plane, pieces, planes):
+def assemble(plane, pieces, planes, position, count, base=None):
     chunks = len(pieces) // planes
     depth, blocks, size, width = pieces[0].shape
     step = depth // 4
+    out_block = (step, 1, 2, chunks * size, 2 * width)
     return pl.pallas_call(
         functools.partial(assemble_kernel, planes, chunks),
         grid=(4, blocks),
         in_specs=[pl.BlockSpec(memory_space=pltpu.SMEM)]
-        + [pl.BlockSpec((step, 1, size, width), lambda d, n: (d, n, 0, 0))] * len(pieces),
-        out_specs=pl.BlockSpec((step, 1, 2, chunks * size, 2 * width), lambda d, n: (d, n, 0, 0, 0)),
-        out_shape=jax.ShapeDtypeStruct((depth, blocks, 2, chunks * size, 2 * width), BF16),
+        + [pl.BlockSpec((step, 1, size, width), lambda d, n: (d, n, 0, 0))] * len(pieces)
+        + ([] if base is None else [pl.BlockSpec(memory_space=pl.ANY)]),
+        out_specs=pl.BlockSpec(out_block, lambda d, n: (d, n, 0, position // chunks, 0)),
+        out_shape=jax.ShapeDtypeStruct((depth, blocks, 2, count * size, 2 * width), BF16),
+        input_output_aliases={} if base is None else {1 + len(pieces): 0},
         compiler_params=pltpu.CompilerParams(dimension_semantics=(ARBITRARY, ARBITRARY)),
+        cost_estimate=pl.CostEstimate(
+            flops=4 * depth * blocks * size * width * len(pieces),
+            bytes_accessed=4 * depth * blocks * size * width * len(pieces),
+            transcendentals=0,
+        ),
         name="assemble",
-    )(plane, *pieces)
+    )(plane, *pieces, *(() if base is None else (base,)))
 
 
 def block_order(array, order, axis):
@@ -348,30 +358,9 @@
     size = span // CHUNKS
     tiles = pair.reshape(channels, blocks, 2, span, width)
     masks = pair_mask.astype(F32).reshape(blocks, 2, span, width)
-
-    shared = [w_left_gate, w_left, w_right_gate, w_right, w_out_gate, w_out, out_gain[None]]
-    shared = lax.all_gather(jnp.concatenate([w.astype(F32) for w in shared], axis=0), "gz", axis=1, tiled=True)
-    tiles, shared = lax.optimization_barrier((tiles, shared))
-    weights = [shared[i * channels * gz : (i + 1) * channels * gz].astype(BF16) for i in range(6)]
-    gains = shared[-1]
-    row_order, col_order = jnp.asarray(ROW_ORDER)[z], jnp.asarray(COL_ORDER)[z]
-    head_order, plane_order = x ^ jnp.arange(gx), z ^ jnp.arange(gz)
-
-    def pair_weight(gate, linear, order):
-        halves = [block_order(block_order(w.T, head_order, 0), order, 1) for w in (gate, linear)]
-        return jnp.concatenate(halves, axis=0)
-
-    def lanes(vector):
-        return jnp.broadcast_to(vector[:, None], (vector.shape[0], LANES))
-
-    left_weight = pair_weight(weights[0], weights[1], row_order)
-    right_weight = pair_weight(weights[2], weights[3], col_order)
-    gate_weight = block_order(block_order(weights[4].T, plane_order, 0), row_order, 1)
-    out_weight = block_order(block_order(weights[5].T, plane_order, 0), head_order, 1)
-    left_gain, right_gain = (lanes(block_order(in_gain, order, 0)) for order in (row_order, col_order))
-    mix_gain = lanes(block_order(gains, head_order, 0))
     left_mask = lax.dynamic_index_in_dim(masks, z & 1, 1, keepdims=False)
     right_mask = lax.dynamic_index_in_dim(masks, z >> 1, 1, keepdims=False)
+    held = (w_left_gate, w_left, w_right_gate, w_right, w_out_gate, w_out, out_gain)
 
     values = {}
 
@@ -379,20 +368,53 @@
         keys = list(dict.fromkeys(keys))
         values.update(zip(keys, lax.optimization_barrier(tuple(values[key] for key in keys))))
 
-    def start(kind, g):
-        operand, down, up = MESSAGES[kind]
-        sources = (1, 0) if operand == "side" else (0, 1)
-        if operand == "far":
-            operand = "s" if ("s", g, 0) in values else "r"
-        for way, pairs in enumerate((down, up)):
-            source = ("own", g, sources[way]) if operand in ("own", "side") else (operand, g, way)
-            values[kind, g, way] = lax.ppermute(values[source], "gz", pairs)
-
-    def operands(kind, g):
-        operand = MESSAGES[kind][0]
-        if operand == "far":
-            operand = "s" if ("s", g, 0) in values else "r"
-        return [("own" if operand == "side" else operand, g, way) for way in range(2)]
+    def by_plane(*choices):
+        value = choices[-1]
+        for p, choice in list(enumerate(choices))[-2::-1]:
+            value = jnp.where(z == p, choice, value)
+        return value
+
+    def sources(message):
+        kind, *chunk = message
+        if kind == "1":
+            return [("own", chunk[0], p) for p in range(2)]
+        if kind == "2":
+            return [("1d", chunk[0]), ("1u", chunk[0])]
+        if kind == "t":
+            return [("side", chunk[0])]
+        if kind == "l":
+            return [("r", chunk[0])]
+        third, side = chunk
+        keys = [] if third is None else [("2d", third), ("2u", third)]
+        return keys + ([] if side is None else [("own", side, p) for p in range(2)])
+
+    def results(message):
+        kind, *chunk = message
+        if kind in ("1", "2"):
+            return [(kind + "d", chunk[0]), (kind + "u", chunk[0])]
+        if kind in ("t", "l"):
+            return [(kind, chunk[0])]
+        third, side = chunk
+        return [("3", third)] if third is not None else [("r", side)]
+
+    def start(message):
+        kind, *chunk = message
+        inputs = [values[key] for key in sources(message)]
+        if kind == "x":
+            third, side = chunk
+            if third is None:
+                inputs = [by_plane(inputs[0], inputs[0], inputs[1], inputs[1])]
+            elif side is None:
+                inputs = [by_plane(inputs[0], inputs[0], inputs[1], inputs[1])]
+            else:
+                inputs = [by_plane(inputs[2], inputs[0], inputs[1], inputs[3])]
+            kinds = ["x"]
+        else:
+            kinds = [key[0] for key in results(message)]
+        outs = [lax.ppermute(v, "gz", HOPS[k]) for v, k in zip(inputs, kinds)]
+        values.update(zip(results(message), outs))
+        if kind == "x" and third is not None and side is not None:
+            values["r", side] = outs[0]
 
     def swap(value, axis, bits):
         return lax.ppermute(value, axis, [(i, i ^ bits) for i in range(lax.axis_size(axis))])
@@ -405,31 +427,27 @@
         for m in range(gx):
             values["other", g, m] = swap(values["right", g, m], "gy", 1)
 
-    def sides(g):
-        far, near = ("s", "s") if ("s", g, 0) in values else ("r", "t")
-        return [values[far, g, way] for way in range(2)], [values.get((near, g, way)) for way in range(2)]
-
     def project_right(g):
-        (far_down, far_up), _ = sides(g)
-        arrays = [values[key, g, way] for key in ("own", "1", "2", "3") for way in range(2)] + [far_down, far_up]
+        names = ("1d", "1u", "2d", "2u", "3", "r")
+        arrays = [values["own", g, p] for p in range(2)] + [values[name, g] for name in names]
         slots = (
             ((0, (0, 1)), (1, (2, 3))),
             ((2, (0, 1)), (3, (2, 3))),
             ((4, (0, 1)), (5, (2, 3))),
-            ((6, (0,)), (9, (1,)), (8, (2,)), (7, (3,))),
+            ((6, (0, 3)), (7, (1, 2))),
         )
         mask = right_mask[:, g * size : (g + 1) * size]
         outs = project(plane, slots, arrays, mask, right_weight, right_gain, gx, False)
         values.update({("right", g, m): outs[m] for m in range(gx)})
 
     def project_left(g):
-        _, (near_down, near_up) = sides(g)
-        arrays = [values[key, g, way] for key in ("own", "1", "2", "3", "l") for way in range(2)] + [near_down, near_up]
+        names = ("1d", "1u", "2d", "2u", "3", "l", "t")
+        arrays = [values["own", g, p] for p in range(2)] + [values[name, g] for name in names]
         slots = (
             ((0, (0, 2)), (1, (1, 3))),
             ((2, (0, 2)), (3, (1, 3))),
-            ((4, (0,)), (10, (1,)), (11, (2,)), (5, (3,))),
-            ((6, (0,)), (8, (1,)), (9, (2,)), (7, (3,))),
+            ((4, (0,)), (8, (1, 2)), (5, (3,))),
+            ((6, (0, 3)), (7, (1, 2))),
         )
         mask = left_mask[:, g * size : (g + 1) * size]
         outs = project(plane, slots, arrays, mask, left_weight, left_gain, gx, True)
@@ -439,10 +457,12 @@
     target = (((x // blocks) ^ y) * blocks + x % blocks) ^ jnp.arange(gx)
     target = target.astype(jnp.int32)
 
-    def multiply(g):
+    def multiply(group):
         rights = [values[key, c, m] for key in ("right", "other") for c in range(CHUNKS) for m in range(gx)]
-        outs = product(target, [values["left", g, m] for m in range(gx)], rights, gx, 2)
-        values.update({("mixed", g, m): outs[m] for m in range(gx)})
+        lefts = [values["left", g, m] for g in group for m in range(gx)]
+        outs = product(target, lefts, rights, gx, 2)
+        for i, g in enumerate(group):
+            values.update({("mixed", g, m): outs[i * gx + m] for m in range(gx)})
 
     def complete(g):
         mixed = [values["mixed", g, m] for m in range(gx)]
@@ -451,18 +471,50 @@
         for q in range(1, gz):
             values["out", g, q] = swap(outs[q], "gz", q)
 
-    for g in range(CHUNKS):
+    def cut(g):
         for p in range(2):
-            values["own", g, p] = tiles[:, :, p, g * size : (g + 1) * size]
-
-    waits = []
+            values["own", g, p] = values["tiles"][:, :, p, g * size : (g + 1) * size]
+        values["side", g] = jnp.where(z < 2, values["own", g, 0], values["own", g, 1])
+
+    values["tiles"] = tiles
+    values.update({("held", i): array for i, array in enumerate(held)})
+    cut(0)
+    waits = ["tiles"]
     for e, messages in enumerate(EVENTS):
-        keys = [(kind, g, way) for kind, g in EVENTS[e - 2] for way in range(2)] if e >= 2 else []
-        keys += [key for kind, g in messages for key in operands(kind, g)]
+        keys = [key for message in EVENTS[e - 2] for key in results(message)] if e >= 2 else []
+        keys += [key for message in messages for key in sources(message)]
         sync(*keys, *waits)
         waits = []
-        for kind, g in messages:
-            start(kind, g)
+        for message in messages:
+            start(message)
+        if e == 0:
+            for g in range(1, CHUNKS):
+                cut(g)
+            waits = [("held", i) for i in range(len(held))]
+        if e == 1:
+            rows_held = [values["held", i] for i in range(len(held) - 1)] + [values["held", len(held) - 1][None]]
+            mine = jnp.concatenate([w.astype(F32) for w in rows_held], axis=0)
+            every = jnp.stack([mine] + [swap(mine, "gz", q) for q in range(1, gz)])
+            depth = channels * gz
+            row_order, col_order = jnp.asarray(ROW_ORDER)[z], jnp.asarray(COL_ORDER)[z]
+            head_order = x ^ jnp.arange(gx)
+            by_head = jnp.take(every, head_order ^ z, axis=0)
+
+            def columns(blocks_of, i):
+                part = blocks_of[:, i * depth : (i + 1) * depth]
+                return jnp.swapaxes(part, 1, 2).reshape(-1, depth).astype(BF16)
+
+            def lanes(vector):
+                return jnp.broadcast_to(vector[:, None], (vector.shape[0], LANES))
+
+            def pair_weight(gate, linear, order):
+                return block_order(jnp.concatenate([columns(by_head, gate), columns(by_head, linear)]), order, 1)
+
+            left_weight, right_weight = pair_weight(0, 1, row_order), pair_weight(2, 3, col_order)
+            gate_weight = block_order(columns(every, 4), row_order, 1)
+            out_weight = block_order(columns(every, 5), head_order, 1)
+            left_gain, right_gain = (lanes(block_order(in_gain, order, 0)) for order in (row_order, col_order))
+            mix_gain = lanes(by_head[:, -1].reshape(-1))
         for name, g in TASKS.get(e, ()):
             if name == "pass":
                 pass_on(g)
@@ -478,28 +530,34 @@
                 waits += [("other", g, m) for m in range(gx)]
 
     last = CHUNKS - 1
-    sync(*waits, *[(kind, g, way) for event in EVENTS[-2:] for kind, g in event for way in range(2)])
+    sync(*waits, *[key for event in EVENTS[-2:] for message in event for key in results(message)])
     project_left(last)
     sync(("left", last, 0), *[("right", last - 1, m) for m in range(gx)])
     pass_on(last - 1)
-    sync(*[("right", g, m) for g in (last - 1, last) for m in range(gx)])
+    sync(*[(name, g, m) for name, g in (("other", last - 1), ("right", last)) for m in range(gx)])
     pass_on(last)
     previous = None
     for step, g in TAIL:
         needs = {"multiply": ["left"], "complete": ["mixed"], "share": ["left"]}[step]
-        keys = [(name, g, m) for name in needs for m in range(gx)]
+        group = g if step == "multiply" else (g,)
+        keys = [(name, c, m) for name in needs for c in group for m in range(gx)]
+        if step == "complete" and g >= 2:
+            keys += [("out", g - 2, q) for q in range(gz)]
         sync(*keys, *([previous] if previous else []))
         if step == "multiply":
-            multiply(g)
-            previous = ("mixed", g, 0)
-            share("mixed", g)
+            multiply(group)
+            previous = ("mixed", group[0], 0)
+            for c in group:
+                share("mixed", c)
         elif step == "share":
             share("left", g)
         else:
             complete(g)
             previous = ("out", g, 0)
-    ordered = [values["out", g, q] for q in range(gz) for g in range(CHUNKS)]
-    return assemble(plane, ordered, gz).reshape(pair.shape)
+    update = None
+    for g in range(0, CHUNKS):
+        update = assemble(plane, [values["out", g, q] for q in range(gz)], gz, g, CHUNKS, update)
+    return update.reshape(pair.shape)
 
 
 def plain_local(

time: 995 us -> 875 us (0.88)
  waiting for transfers between devices: 443 us -> 374 us
  starting transfers between devices: 266 us -> 225 us
  other arithmetic: 9.16 us -> 26.8 us
  blocking collectives: 16.8 us -> 0 us
    ppermute x64 -> x67, waiting for transfers between devices: 340 us -> 287 us  [swap(): lax.ppermute(value, axis, [(i, i ^ bits) for i in range(lax.axis_size(axi...]
    ppermute x46 -> x29, starting transfers between devices: 153 us -> 117 us  [start(): outs = [lax.ppermute(v, 'gz', HOPS[k]) for v, k in zip(inputs, kinds)]]
    pallas_call x4 -> x3, Pallas kernels: 85.3 us -> 65.3 us  [product(): pl.pallas_call(functools.partial(product_kernel, parts, chunks, left_chun...]
    all_gather x1 -> x0, blocking collectives: 16.8 us -> none  [local(): lax.all_gather(jnp.concatenate([w.astype(F32) for w in shared], axis=0),...]
    select_n x0 -> x8, other arithmetic: none -> 16.6 us  [the longest x5 9.54 us: by_plane(): value = jnp.where(z == p, choice, value)]
    ppermute x46 -> x29, waiting for transfers between devices: 104 us -> 87.3 us  [start(): outs = [lax.ppermute(v, 'gz', HOPS[k]) for v, k in zip(inputs, kinds)]]
    pallas_call x1 -> x4, Pallas kernels: 9.25 us -> 23.2 us  [assemble(): pl.pallas_call(functools.partial(assemble_kernel, planes, chunks), grid=(...]
    ppermute x64 -> x67, starting transfers between devices: 114 us -> 108 us  [swap(): lax.ppermute(value, axis, [(i, i ^ bits) for i in range(lax.axis_size(axi...]
  transfers between devices with their start and end apart: 110 -> 96, of which waited for: 30 -> 27; matrix products, arithmetic and copies ran while one was open for 2% -> 5% of each run, Pallas kernels for 21% -> 23%
where the time goes in v1:
time: 875 us; the launch traced here: 858 us
  waiting for transfers between devices  374 us (43%)
  starting transfers between devices  225 us (26%)
  Pallas kernels  201 us (23%)
  local copies, waits for them, and re-layouts  30.4 us (3%)
  other arithmetic  26.8 us (3%)
    ppermute x67, waiting for transfers between devices, swap(): lax.ppermute(value, axis, [(i, i ^ bits) for i in range(lax.axis_size(axi...  287 us
    ppermute x29, starting transfers between devices, start(): outs = [lax.ppermute(v, 'gz', HOPS[k]) for v, k in zip(inputs, kinds)]  117 us
    ppermute x67, starting transfers between devices, swap(): lax.ppermute(value, axis, [(i, i ^ bits) for i in range(lax.axis_size(axi...  108 us
    ppermute x29, waiting for transfers between devices, start(): outs = [lax.ppermute(v, 'gz', HOPS[k]) for v, k in zip(inputs, kinds)]  87.3 us
    pallas_call x8, Pallas kernels, project(): pl.pallas_call(functools.partial(project_kernel, planes, emit, parts), gr...  85.9 us
    pallas_call x3, Pallas kernels, product(): pl.pallas_call(functools.partial(product_kernel, parts, chunks, left_chun...  65.3 us
    pallas_call x4, Pallas kernels, finish(): pl.pallas_call(functools.partial(finish_kernel, len(mixed)), grid=(blocks...  26.4 us
    pallas_call x4, Pallas kernels, assemble(): pl.pallas_call(functools.partial(assemble_kernel, planes, chunks), grid=(...  23.2 us
  transfers between devices with their start and end apart: 96, of which 27 were waited for; matrix products, arithmetic and copies ran while one was open for 5% of the time, Pallas kernels for 23%

profile of v1, /device:TPU:0, one launch (start us, length us, event | category | flops | bytes accessed | tf_op | source)
XLA Modules:
  0.0 857.9 jit_solution(3716999695922535009)
XLA Ops:
  41.5 14.7 %collective-permute-done.4.refs_7_ = bf16[32,2,32,256]{3,2,1,0:T(8,128)(2,1)} collective-permute-done((bf16[32,2,32,256]{3,2,1,0:T(8,128)(2,1)}, bf16[32,2,32,256]{3,2,1,0:T(8,128)(2,1)}, u32[]{:S(2)}, u32[]{:S(2)}) %collective-permute-start.4) | collective-permute-done | bytes 1048608 | tf_op jit(solution)/shard_map/ppermute | solution.py:414
  87.3 21.2 %collective-permute-done.11 = f32[769,32]{0,1:T(8,128)S(1)} collective-permute-done((f32[769,32]{0,1:T(8,128)S(1)}, f32[769,32]{0,1:T(8,128)S(1)}, u32[]{:S(2)}, u32[]{:S(2)}) %collective-permute-start.11) | collective-permute-done | bytes 98464 | tf_op jit(solution)/shard_map/ppermute | solution.py:420
  129.4 13.8 %collective-permute-start.9 = (bf16[32,2,32,256]{3,2,1,0:T(8,128)(2,1)S(1)}, bf16[32,2,32,256]{3,2,1,0:T(8,128)(2,1)}, u32[]{:S(2)}, u32[]{:S(2)}) collective-permute-start(bf16[32,2,32,256]{3,2,1,0:T(8,128)(2,1)S(1)} %get-tuple-element.261.refs_1_), channel_id=1, source_target_pairs={{0,1},{1,2},{2,3},{4,5},{5,6},{6,7},{8,9},{9,10},{10,11},{12,13},{... | collective-permute-start | bytes 3145736 | tf_op jit(solution)/shard_map/ppermute | solution.py:414
  143.9 10.4 %project.9 = (bf16[32,2,32,256]{3,2,1,0:T(8,128)(2,1)}, bf16[32,2,32,256]{3,2,1,0:T(8,128)(2,1)}, bf16[32,2,32,256]{3,2,1,0:T(8,128)(2,1)}, bf16[32,2,32,256]{3,2,1,0:T(8,128)(2,1)}) custom-call(s32[1]{0:T(128)} %bitcast.plane_ref, bf16[32,2,32,256]{3,2,1,0:T(8,128)(2,1)} %copy-done.21, bf16[32,2,32,256]{3,2,1,0:T(8,128)(2,1)} %copy-done.20, ...), custom_call_target="tpu_custom_call" | custom-call | flops 4294967296 | bytes 16777216 | tf_op jit(solution)/shard_map/project/pallas_call | solution.py:153
  163.3 9.5 %collective-permute-start.19 = (bf16[32,2,32,256]{3,2,1,0:T(8,128)(2,1)}, bf16[32,2,32,256]{3,2,1,0:T(8,128)(2,1)}, u32[]{:S(2)}, u32[]{:S(2)}) collective-permute-start(bf16[32,2,32,256]{3,2,1,0:T(8,128)(2,1)} %get-tuple-element.257), channel_id=1, source_target_pairs={{0,0},{1,2},{2,1},{3,3},{4,4},{5,6},{6,5},{7,7},{8,8},{9,10},{10,9... | collective-permute-start | bytes 3145736 | tf_op jit(solution)/shard_map/ppermute | solution.py:414
  177.7 11.0 %project.8 = (bf16[32,2,32,256]{3,2,1,0:T(8,128)(2,1)}, bf16[32,2,32,256]{3,2,1,0:T(8,128)(2,1)}, bf16[32,2,32,256]{3,2,1,0:T(8,128)(2,1)}, bf16[32,2,32,256]{3,2,1,0:T(8,128)(2,1)}, bf16[2,32,128,128]{3,2,1,0:T(8,128)(2,1)}) custom-call(s32[1]{0:T(128)} %bitcast.plane_ref, bf16[32,2,32,256]{3,2,1,0:T(8,128)(2,1)} %copy-done.21, ...), custom_call_target="tpu_custom_call" | custom-call | flops 4294967296 | bytes 16777216 | tf_op jit(solution)/shard_map/project/pallas_call | solution.py:153
  197.7 10.5 %project.10 = (bf16[32,2,32,256]{3,2,1,0:T(8,128)(2,1)}, bf16[32,2,32,256]{3,2,1,0:T(8,128)(2,1)}, bf16[32,2,32,256]{3,2,1,0:T(8,128)(2,1)}, bf16[32,2,32,256]{3,2,1,0:T(8,128)(2,1)}) custom-call(s32[1]{0:T(128)} %bitcast.plane_ref, bf16[32,2,32,256]{3,2,1,0:T(8,128)(2,1)} %get-tuple-element.235.refs_0_, ...), custom_call_target="tpu_custom_call" | custom-call | flops 4294967296 | bytes 16777216 | tf_op jit(solution)/shard_map/project/pallas_call | solution.py:153
  209.5 21.9 %collective-permute-done.22.refs_10_.refs_6_ = bf16[32,2,32,256]{3,2,1,0:T(8,128)(2,1)S(1)} collective-permute-done((bf16[32,2,32,256]{3,2,1,0:T(8,128)(2,1)}, bf16[32,2,32,256]{3,2,1,0:T(8,128)(2,1)S(1)}, u32[]{:S(2)}, u32[]{:S(2)}) %collective-permute-start.22) | collective-permute-done | bytes 1048608 | tf_op jit(solution)/shard_map/ppermute | solution.py:420
  245.3 11.2 %collective-permute-done.25.refs_3_ = bf16[32,2,32,256]{3,2,1,0:T(8,128)(2,1)} collective-permute-done((bf16[32,2,32,256]{3,2,1,0:T(8,128)(2,1)}, bf16[32,2,32,256]{3,2,1,0:T(8,128)(2,1)}, u32[]{:S(2)}, u32[]{:S(2)}) %collective-permute-start.25) | collective-permute-done | bytes 1048608 | tf_op jit(solution)/shard_map/ppermute | solution.py:414
  256.6 16.4 %collective-permute-done.29.refs_6_.refs_7_ = bf16[32,2,32,256]{3,2,1,0:T(8,128)(2,1)} collective-permute-done((bf16[32,2,32,256]{3,2,1,0:T(8,128)(2,1)S(1)}, bf16[32,2,32,256]{3,2,1,0:T(8,128)(2,1)}, u32[]{:S(2)}, u32[]{:S(2)}) %collective-permute-start.29) | collective-permute-done | bytes 1048608 | tf_op jit(solution)/shard_map/ppermute | solution.py:414
  280.6 20.8 %collective-permute-done.26.refs_4_ = bf16[32,2,32,256]{3,2,1,0:T(8,128)(2,1)} collective-permute-done((bf16[32,2,32,256]{3,2,1,0:T(8,128)(2,1)S(1)}, bf16[32,2,32,256]{3,2,1,0:T(8,128)(2,1)}, u32[]{:S(2)}, u32[]{:S(2)}) %collective-permute-start.26) | collective-permute-done | bytes 1048608 | tf_op jit(solution)/shard_map/ppermute | solution.py:414
  310.9 10.4 %project.11 = (bf16[32,2,32,256]{3,2,1,0:T(8,128)(2,1)}, bf16[32,2,32,256]{3,2,1,0:T(8,128)(2,1)}, bf16[32,2,32,256]{3,2,1,0:T(8,128)(2,1)}, bf16[32,2,32,256]{3,2,1,0:T(8,128)(2,1)}) custom-call(s32[1]{0:T(128)} %bitcast.plane_ref, bf16[32,2,32,256]{3,2,1,0:T(8,128)(2,1)} %copy-done.19, bf16[32,2,32,256]{3,2,1,0:T(8,128)(2,1)} %copy-done.18, ...), custom_call_target="tpu_custom_call" | custom-call | flops 4294967296 | bytes 16777216 | tf_op jit(solution)/shard_map/project/pallas_call | solution.py:153
  324.0 9.6 %collective-permute-start.34 = (bf16[32,2,32,256]{3,2,1,0:T(8,128)(2,1)}, bf16[32,2,32,256]{3,2,1,0:T(8,128)(2,1)}, u32[]{:S(2)}, u32[]{:S(2)}) collective-permute-start(bf16[32,2,32,256]{3,2,1,0:T(8,128)(2,1)} %collective-permute-done.20.refs_6_.refs_7_), channel_id=1, source_target_pairs={{0,0},{1,2},{2,1},{3,3},{4,4},{5,6},{6,5},{7,7},{8,8},{9,10},{10,9... | collective-permute-start | bytes 3145736 | tf_op jit(solution)/shard_map/ppermute | solution.py:414
  333.7 11.0 %project.13 = (bf16[32,2,32,256]{3,2,1,0:T(8,128)(2,1)}, bf16[32,2,32,256]{3,2,1,0:T(8,128)(2,1)}, bf16[32,2,32,256]{3,2,1,0:T(8,128)(2,1)}, bf16[32,2,32,256]{3,2,1,0:T(8,128)(2,1)}, bf16[2,32,128,128]{3,2,1,0:T(8,128)(2,1)}) custom-call(s32[1]{0:T(128)} %bitcast.plane_ref, bf16[32,2,32,256]{3,2,1,0:T(8,128)(2,1)} %get-tuple-element.235.refs_0_, ...), custom_call_target="tpu_custom_call" | custom-call | flops 4294967296 | bytes 16777216 | tf_op jit(solution)/shard_map/project/pallas_call | solution.py:153
  358.9 9.5 %collective-permute-start.45 = (bf16[32,2,32,256]{3,2,1,0:T(8,128)(2,1)}, bf16[32,2,32,256]{3,2,1,0:T(8,128)(2,1)}, u32[]{:S(2)}, u32[]{:S(2)}) collective-permute-start(bf16[32,2,32,256]{3,2,1,0:T(8,128)(2,1)} %collective-permute-done.29.refs_6_.refs_7_), channel_id=1, source_target_pairs={{0,0},{1,2},{2,1},{3,3},{4,4},{5,6},{6,5},{7,7},{8,8},{9,10},{10,9... | collective-permute-start | bytes 3145736 | tf_op jit(solution)/shard_map/ppermute | solution.py:414
  370.4 10.4 %project.12 = (bf16[32,2,32,256]{3,2,1,0:T(8,128)(2,1)}, bf16[32,2,32,256]{3,2,1,0:T(8,128)(2,1)}, bf16[32,2,32,256]{3,2,1,0:T(8,128)(2,1)}, bf16[32,2,32,256]{3,2,1,0:T(8,128)(2,1)}) custom-call(s32[1]{0:T(128)} %bitcast.plane_ref, bf16[32,2,32,256]{3,2,1,0:T(8,128)(2,1)} %get-tuple-element.270.refs_0_, ...), custom_call_target="tpu_custom_call" | custom-call | flops 4294967296 | bytes 16777216 | tf_op jit(solution)/shard_map/project/pallas_call | solution.py:153
  384.7 11.0 %project.14 = (bf16[32,2,32,256]{3,2,1,0:T(8,128)(2,1)}, bf16[32,2,32,256]{3,2,1,0:T(8,128)(2,1)}, bf16[32,2,32,256]{3,2,1,0:T(8,128)(2,1)}, bf16[32,2,32,256]{3,2,1,0:T(8,128)(2,1)}, bf16[2,32,128,128]{3,2,1,0:T(8,128)(2,1)}) custom-call(s32[1]{0:T(128)} %bitcast.plane_ref, bf16[32,2,32,256]{3,2,1,0:T(8,128)(2,1)} %copy-done.19, ...), custom_call_target="tpu_custom_call" | custom-call | flops 4294967296 | bytes 16777216 | tf_op jit(solution)/shard_map/project/pallas_call | solution.py:153
  395.8 11.1 %project.15 = (bf16[32,2,32,256]{3,2,1,0:T(8,128)(2,1)}, bf16[32,2,32,256]{3,2,1,0:T(8,128)(2,1)}, bf16[32,2,32,256]{3,2,1,0:T(8,128)(2,1)}, bf16[32,2,32,256]{3,2,1,0:T(8,128)(2,1)}, bf16[2,32,128,128]{3,2,1,0:T(8,128)(2,1)}) custom-call(s32[1]{0:T(128)} %bitcast.plane_ref, bf16[32,2,32,256]{3,2,1,0:T(8,128)(2,1)} %get-tuple-element.270.refs_0_, ...), custom_call_target="tpu_custom_call" | custom-call | flops 4294967296 | bytes 16777216 | tf_op jit(solution)/shard_map/project/pallas_call | solution.py:153
  406.9 10.3 %collective-permute-done.47.refs_18_.refs_14_ = bf16[32,2,32,256]{3,2,1,0:T(8,128)(2,1)} collective-permute-done((bf16[32,2,32,256]{3,2,1,0:T(8,128)(2,1)}, bf16[32,2,32,256]{3,2,1,0:T(8,128)(2,1)}, u32[]{:S(2)}, u32[]{:S(2)}) %collective-permute-start.47) | collective-permute-done | bytes 1048608 | tf_op jit(solution)/shard_map/ppermute | solution.py:420
  419.5 21.8 %collective-permute-done.62.refs_21_.refs_17_ = bf16[32,2,32,256]{3,2,1,0:T(8,128)(2,1)} collective-permute-done((bf16[32,2,32,256]{3,2,1,0:T(8,128)(2,1)}, bf16[32,2,32,256]{3,2,1,0:T(8,128)(2,1)}, u32[]{:S(2)}, u32[]{:S(2)}) %collective-permute-start.62) | collective-permute-done | bytes 1048608 | tf_op jit(solution)/shard_map/ppermute | solution.py:420
  441.8 22.5 %collective-permute-done.64.refs_23_.refs_19_ = bf16[32,2,32,256]{3,2,1,0:T(8,128)(2,1)} collective-permute-done((bf16[32,2,32,256]{3,2,1,0:T(8,128)(2,1)}, bf16[32,2,32,256]{3,2,1,0:T(8,128)(2,1)}, u32[]{:S(2)}, u32[]{:S(2)}) %collective-permute-start.64) | collective-permute-done | bytes 1048608 | tf_op jit(solution)/shard_map/ppermute | solution.py:420
  469.6 44.8 %collective-permute-done.53.refs_2_ = bf16[32,2,32,256]{3,2,1,0:T(8,128)(2,1)S(1)} collective-permute-done((bf16[32,2,32,256]{3,2,1,0:T(8,128)(2,1)}, bf16[32,2,32,256]{3,2,1,0:T(8,128)(2,1)S(1)}, u32[]{:S(2)}, u32[]{:S(2)}) %collective-permute-start.53) | collective-permute-done | bytes 1048608 | tf_op jit(solution)/shard_map/ppermute | solution.py:420
  515.4 40.9 %collective-permute-done.56.refs_6_ = bf16[32,2,32,256]{3,2,1,0:T(8,128)(2,1)S(1)} collective-permute-done((bf16[32,2,32,256]{3,2,1,0:T(8,128)(2,1)}, bf16[32,2,32,256]{3,2,1,0:T(8,128)(2,1)S(1)}, u32[]{:S(2)}, u32[]{:S(2)}) %collective-permute-start.56) | collective-permute-done | bytes 1048608 | tf_op jit(solution)/shard_map/ppermute | solution.py:420
  564.2 22.7 %product.3 = (bf16[32,2,32,128]{3,2,1,0:T(8,128)(2,1)}, bf16[32,2,32,128]{3,2,1,0:T(8,128)(2,1)}, bf16[32,2,32,128]{3,2,1,0:T(8,128)(2,1)}, bf16[32,2,32,128]{3,...) custom-call(s32[4]{0:T(128)} %iota_xor_fusion.1.target_ref, ...), custom_call_target="tpu_custom_call" | custom-call | flops 4294967296 | bytes 41943040 | tf_op jit(solution)/shard_map/product/pallas_call | solution.py:218
  592.9 14.3 %collective-permute-done.51.refs_3_ = bf16[32,2,32,256]{3,2,1,0:T(8,128)(2,1)} collective-permute-done((bf16[32,2,32,256]{3,2,1,0:T(8,128)(2,1)}, bf16[32,2,32,256]{3,2,1,0:T(8,128)(2,1)}, u32[]{:S(2)}, u32[]{:S(2)}) %collective-permute-start.51) | collective-permute-done | bytes 1048608 | tf_op jit(solution)/shard_map/ppermute | solution.py:420
  608.9 21.3 %product.4 = (bf16[32,2,32,128]{3,2,1,0:T(8,128)(2,1)}, bf16[32,2,32,128]{3,2,1,0:T(8,128)(2,1)}, bf16[32,2,32,128]{3,2,1,0:T(8,128)(2,1)}, bf16[32,2,32,128]{3,2,1,0:T(8,128)(2,1)}) custom-call(s32[4]{0:T(128)} %iota_xor_fusion.1.target_ref, bf16[32,2,32,256]{3,2,1,0:T(8,128)(2,1)} %get-tuple-element.365.refs_0_, ...), custom_call_target="tpu_custom_call" | custom-call | flops 2147483648 | bytes 37748736 | tf_op jit(solution)/shard_map/product/pallas_call | solution.py:218
  664.1 11.4 %collective-permute-start.74 = (bf16[32,2,32,256]{3,2,1,0:T(8,128)(2,1)}, bf16[32,2,32,256]{3,2,1,0:T(8,128)(2,1)S(1)}, u32[]{:S(2)}, u32[]{:S(2)}) collective-permute-start(bf16[32,2,32,256]{3,2,1,0:T(8,128)(2,1)} %get-tuple-element.379), channel_id=1, source_target_pairs={{0,24},{8,16},{16,8},{24,0},{1,25},{9,17},{17,9},{25,1},{2,26},{10... | collective-permute-start | bytes 3145736 | tf_op jit(solution)/shard_map/ppermute | solution.py:420
  690.6 24.4 %collective-permute-done.82.refs_2_ = bf16[32,2,32,128]{3,2,1,0:T(8,128)(2,1)} collective-permute-done((bf16[32,2,32,128]{3,2,1,0:T(8,128)(2,1)}, bf16[32,2,32,128]{3,2,1,0:T(8,128)(2,1)}, u32[]{:S(2)}, u32[]{:S(2)}) %collective-permute-start.82) | collective-permute-done | bytes 524320 | tf_op jit(solution)/shard_map/ppermute | solution.py:420
  715.0 10.5 %collective-permute-start.88 = (bf16[32,2,32,128]{3,2,1,0:T(8,128)(2,1)}, bf16[32,2,32,128]{3,2,1,0:T(8,128)(2,1)}, u32[]{:S(2)}, u32[]{:S(2)}) collective-permute-start(bf16[32,2,32,128]{3,2,1,0:T(8,128)(2,1)} %get-tuple-element.415), channel_id=1, source_target_pairs={{0,2},{1,3},{2,0},{3,1},{4,6},{5,7},{6,4},{7,5},{8,10},{9,11},{10,... | collective-permute-start | bytes 1572872 | tf_op jit(solution)/shard_map/ppermute | solution.py:420
  735.6 21.3 %product.5 = (bf16[32,2,32,128]{3,2,1,0:T(8,128)(2,1)}, bf16[32,2,32,128]{3,2,1,0:T(8,128)(2,1)}, bf16[32,2,32,128]{3,2,1,0:T(8,128)(2,1)}, bf16[32,2,32,128]{3,2,1,0:T(8,128)(2,1)}) custom-call(s32[4]{0:T(128)} %iota_xor_fusion.1.target_ref, bf16[32,2,32,256]{3,2,1,0:T(8,128)(2,1)} %get-tuple-element.405.refs_0_, bf16[32,2,32,256]{3,2,1,0:T(8,128)(2,1)} %copy-done.27, ...), custom_call_target="tpu_custom_call" | custom-call | flops 2147483648 | bytes 37748736 | tf_op jit(solution)/shard_map/product/pallas_call | solution.py:218
  760.8 10.9 %collective-permute-start.94 = (bf16[32,2,32,128]{3,2,1,0:T(8,128)(2,1)}, bf16[32,2,32,128]{3,2,1,0:T(8,128)(2,1)S(1)}, u32[]{:S(2)}, u32[]{:S(2)}) collective-permute-start(bf16[32,2,32,128]{3,2,1,0:T(8,128)(2,1)} %get-tuple-element.428), channel_id=1, source_target_pairs={{0,2},{1,3},{2,0},{3,1},{4,6},{5,7},{6,4},{7,5},{8,10},{9,11},{10,... | collective-permute-start | bytes 1572872 | tf_op jit(solution)/shard_map/ppermute | solution.py:420
  817.5 33.6 %collective-permute-done.91.refs_2_ = bf16[32,2,32,128]{3,2,1,0:T(8,128)(2,1)S(1)} collective-permute-done((bf16[32,2,32,128]{3,2,1,0:T(8,128)(2,1)}, bf16[32,2,32,128]{3,2,1,0:T(8,128)(2,1)S(1)}, u32[]{:S(2)}, u32[]{:S(2)}) %collective-permute-start.91) | collective-permute-done | bytes 524320 | tf_op jit(solution)/shard_map/ppermute | solution.py:420
  (368 shorter events, 311.6 us)
Async XLA Ops:
  17.3 70.0 %collective-permute-start.12 = (f32[769,32]{0,1:T(8,128)S(1)}, f32[769,32]{0,1:T(8,128)}, u32[]{:S(2)}, u32[]{:S(2)}) collective-permute-start(f32[769,32]{0,1:T(8,128)S(1)} %constant_dynamic-update-slice_fusion), channel_id=1, source_target_pairs={{0,3},{1,2},{2,1},{3,0},{4,7},{5,6},{6,5},{7,4},{8,11},{9,10},{10,... | collective-permute-start | bytes 295304 | tf_op jit(solution)/shard_map/ppermute | solution.py:420
  36.3 45.5 %collective-permute-start.3 = (bf16[32,2,32,256]{3,2,1,0:T(8,128)(2,1)}, bf16[32,2,32,256]{3,2,1,0:T(8,128)(2,1)S(1)}, u32[]{:S(2)}, u32[]{:S(2)}) collective-permute-start(bf16[32,2,32,256]{3,2,1,0:T(8,128)(2,1)} %collective-permute-done.1.refs_3_), channel_id=1, source_target_pairs={{1,2},{2,3},{5,6},{6,7},{9,10},{10,11},{13,14},{14,15},{17,18},{18... | collective-permute-start | bytes 3145736 | tf_op jit(solution)/shard_map/ppermute | solution.py:414
  56.2 63.9 %collective-permute-start.15 = (bf16[32,2,32,256]{3,2,1,0:T(8,128)(2,1)}, bf16[32,2,32,256]{3,2,1,0:T(8,128)(2,1)}, u32[]{:S(2)}, u32[]{:S(2)}) collective-permute-start(bf16[32,2,32,256]{3,2,1,0:T(8,128)(2,1)} %get-tuple-element.235.refs_0_), channel_id=1, source_target_pairs={{3,2},{2,1},{1,0},{7,6},{6,5},{5,4},{11,10},{10,9},{9,8},{15,14},{... | collective-permute-start | bytes 3145736 | tf_op jit(solution)/shard_map/ppermute | solution.py:414
  57.4 62.6 %collective-permute-start.16 = (bf16[32,2,32,256]{3,2,1,0:T(8,128)(2,1)}, bf16[32,2,32,256]{3,2,1,0:T(8,128)(2,1)}, u32[]{:S(2)}, u32[]{:S(2)}) collective-permute-start(bf16[32,2,32,256]{3,2,1,0:T(8,128)(2,1)} %get-tuple-element.238.refs_1_), channel_id=1, source_target_pairs={{0,1},{1,2},{2,3},{4,5},{5,6},{6,7},{8,9},{9,10},{10,11},{12,13},{... | collective-permute-start | bytes 3145736 | tf_op jit(solution)/shard_map/ppermute | solution.py:414
  128.2 60.5 %collective-permute-start.8 = (bf16[32,2,32,256]{3,2,1,0:T(8,128)(2,1)S(1)}, bf16[32,2,32,256]{3,2,1,0:T(8,128)(2,1)}, u32[]{:S(2)}, u32[]{:S(2)}) collective-permute-start(bf16[32,2,32,256]{3,2,1,0:T(8,128)(2,1)S(1)} %get-tuple-element.258.refs_0_), channel_id=1, source_target_pairs={{3,2},{2,1},{1,0},{7,6},{6,5},{5,4},{11,10},{10,9},{9,8},{15,14},{... | collective-permute-start | bytes 3145736 | tf_op jit(solution)/shard_map/ppermute | solution.py:414
  129.4 60.8 %collective-permute-start.9 = (bf16[32,2,32,256]{3,2,1,0:T(8,128)(2,1)S(1)}, bf16[32,2,32,256]{3,2,1,0:T(8,128)(2,1)}, u32[]{:S(2)}, u32[]{:S(2)}) collective-permute-start(bf16[32,2,32,256]{3,2,1,0:T(8,128)(2,1)S(1)} %get-tuple-element.261.refs_1_), channel_id=1, source_target_pairs={{0,1},{1,2},{2,3},{4,5},{5,6},{6,7},{8,9},{9,10},{10,11},{12,13},{... | collective-permute-start | bytes 3145736 | tf_op jit(solution)/shard_map/ppermute | solution.py:414
  274.3 47.0 %collective-permute-start.27 = (bf16[32,2,32,256]{3,2,1,0:T(8,128)(2,1)}, bf16[32,2,32,256]{3,2,1,0:T(8,128)(2,1)S(1)}, u32[]{:S(2)}, u32[]{:S(2)}) collective-permute-start(bf16[32,2,32,256]{3,2,1,0:T(8,128)(2,1)} %collective-permute-done.25.refs_3_), channel_id=1, source_target_pairs={{1,2},{2,3},{5,6},{6,7},{9,10},{10,11},{13,14},{14,15},{17,18},{18... | collective-permute-start | bytes 3145736 | tf_op jit(solution)/shard_map/ppermute | solution.py:414
  275.1 49.0 %collective-permute-start.37 = (bf16[32,2,32,256]{3,2,1,0:T(8,128)(2,1)}, bf16[32,2,32,256]{3,2,1,0:T(8,128)(2,1)}, u32[]{:S(2)}, u32[]{:S(2)}) collective-permute-start(bf16[32,2,32,256]{3,2,1,0:T(8,128)(2,1)} %get-tuple-element.294), channel_id=1, source_target_pairs={{0,8},{8,0},{16,24},{24,16},{1,9},{9,1},{17,25},{25,17},{2,10},{10... | collective-permute-start | bytes 3145736 | tf_op jit(solution)/shard_map/ppermute | solution.py:420
  276.1 57.6 %collective-permute-start.38 = (bf16[32,2,32,256]{3,2,1,0:T(8,128)(2,1)}, bf16[32,2,32,256]{3,2,1,0:T(8,128)(2,1)}, u32[]{:S(2)}, u32[]{:S(2)}) collective-permute-start(bf16[32,2,32,256]{3,2,1,0:T(8,128)(2,1)} %get-tuple-element.295), channel_id=1, source_target_pairs={{0,16},{8,24},{16,0},{24,8},{1,17},{9,25},{17,1},{25,9},{2,18},{10... | collective-permute-start | bytes 3145736 | tf_op jit(solution)/shard_map/ppermute | solution.py:420
  279.1 65.7 %collective-permute-start.39 = (bf16[32,2,32,256]{3,2,1,0:T(8,128)(2,1)}, bf16[32,2,32,256]{3,2,1,0:T(8,128)(2,1)}, u32[]{:S(2)}, u32[]{:S(2)}) collective-permute-start(bf16[32,2,32,256]{3,2,1,0:T(8,128)(2,1)} %get-tuple-element.296), channel_id=1, source_target_pairs={{0,24},{8,16},{16,8},{24,0},{1,25},{9,17},{17,9},{25,1},{2,26},{10... | collective-permute-start | bytes 3145736 | tf_op jit(solution)/shard_map/ppermute | solution.py:420
  368.3 48.9 %collective-permute-start.47 = (bf16[32,2,32,256]{3,2,1,0:T(8,128)(2,1)}, bf16[32,2,32,256]{3,2,1,0:T(8,128)(2,1)}, u32[]{:S(2)}, u32[]{:S(2)}) collective-permute-start(bf16[32,2,32,256]{3,2,1,0:T(8,128)(2,1)} %get-tuple-element.310), channel_id=1, source_target_pairs={{0,16},{8,24},{16,0},{24,8},{1,17},{9,25},{17,1},{25,9},{2,18},{10... | collective-permute-start | bytes 3145736 | tf_op jit(solution)/shard_map/ppermute | solution.py:420
  370.4 48.5 %collective-permute-start.48 = (bf16[32,2,32,256]{3,2,1,0:T(8,128)(2,1)}, bf16[32,2,32,256]{3,2,1,0:T(8,128)(2,1)}, u32[]{:S(2)}, u32[]{:S(2)}) collective-permute-start(bf16[32,2,32,256]{3,2,1,0:T(8,128)(2,1)} %get-tuple-element.311), channel_id=1, source_target_pairs={{0,24},{8,16},{16,8},{24,0},{1,25},{9,17},{17,9},{25,1},{2,26},{10... | collective-permute-start | bytes 3145736 | tf_op jit(solution)/shard_map/ppermute | solution.py:420
  382.4 58.8 %collective-permute-start.62 = (bf16[32,2,32,256]{3,2,1,0:T(8,128)(2,1)}, bf16[32,2,32,256]{3,2,1,0:T(8,128)(2,1)}, u32[]{:S(2)}, u32[]{:S(2)}) collective-permute-start(bf16[32,2,32,256]{3,2,1,0:T(8,128)(2,1)} %get-tuple-element.341), channel_id=1, source_target_pairs={{0,8},{8,0},{16,24},{24,16},{1,9},{9,1},{17,25},{25,17},{2,10},{10... | collective-permute-start | bytes 3145736 | tf_op jit(solution)/shard_map/ppermute | solution.py:420
  382.9 58.3 %collective-permute-start.63 = (bf16[32,2,32,256]{3,2,1,0:T(8,128)(2,1)}, bf16[32,2,32,256]{3,2,1,0:T(8,128)(2,1)}, u32[]{:S(2)}, u32[]{:S(2)}) collective-permute-start(bf16[32,2,32,256]{3,2,1,0:T(8,128)(2,1)} %get-tuple-element.342), channel_id=1, source_target_pairs={{0,16},{8,24},{16,0},{24,8},{1,17},{9,25},{17,1},{25,9},{2,18},{10... | collective-permute-start | bytes 3145736 | tf_op jit(solution)/shard_map/ppermute | solution.py:420
  417.2 47.1 %collective-permute-start.64 = (bf16[32,2,32,256]{3,2,1,0:T(8,128)(2,1)}, bf16[32,2,32,256]{3,2,1,0:T(8,128)(2,1)}, u32[]{:S(2)}, u32[]{:S(2)}) collective-permute-start(bf16[32,2,32,256]{3,2,1,0:T(8,128)(2,1)} %get-tuple-element.343), channel_id=1, source_target_pairs={{0,24},{8,16},{16,8},{24,0},{1,25},{9,17},{17,9},{25,1},{2,26},{10... | collective-permute-start | bytes 3145736 | tf_op jit(solution)/shard_map/ppermute | solution.py:420
  419.0 45.7 %collective-permute-start.58 = (bf16[32,2,32,256]{3,2,1,0:T(8,128)(2,1)S(1)}, bf16[32,2,32,256]{3,2,1,0:T(8,128)(2,1)S(1)}, u32[]{:S(2)}, u32[]{:S(2)}) collective-permute-start(bf16[32,2,32,256]{3,2,1,0:T(8,128)(2,1)S(1)} %copy-done.8), channel_id=1, source_target_pairs={{0,4},{4,0},{1,5},{5,1},{2,6},{6,2},{3,7},{7,3},{8,12},{12,8},{9,1... | collective-permute-start | bytes 3145736 | tf_op jit(solution)/shard_map/ppermute | solution.py:420
  419.0 47.1 %collective-permute-start.59 = (bf16[32,2,32,256]{3,2,1,0:T(8,128)(2,1)S(1)}, bf16[32,2,32,256]{3,2,1,0:T(8,128)(2,1)S(1)}, u32[]{:S(2)}, u32[]{:S(2)}) collective-permute-start(bf16[32,2,32,256]{3,2,1,0:T(8,128)(2,1)S(1)} %collective-permute-done.46.refs_17_.refs_13_), channel_id=1, source_target_pairs={{0,4},{4,0},{1,5},{5,1},{2,6},{6,2},{3,7},{7,3},{8,12},{12,8},{9,1... | collective-permute-start | bytes 3145736 | tf_op jit(solution)/shard_map/ppermute | solution.py:420
  464.3 50.0 %collective-permute-start.53 = (bf16[32,2,32,256]{3,2,1,0:T(8,128)(2,1)}, bf16[32,2,32,256]{3,2,1,0:T(8,128)(2,1)S(1)}, u32[]{:S(2)}, u32[]{:S(2)}) collective-permute-start(bf16[32,2,32,256]{3,2,1,0:T(8,128)(2,1)} %get-tuple-element.322), channel_id=1, source_target_pairs={{0,16},{8,24},{16,0},{24,8},{1,17},{9,25},{17,1},{25,9},{2,18},{10... | collective-permute-start | bytes 3145736 | tf_op jit(solution)/shard_map/ppermute | solution.py:420
  464.7 49.7 %collective-permute-start.54 = (bf16[32,2,32,256]{3,2,1,0:T(8,128)(2,1)}, bf16[32,2,32,256]{3,2,1,0:T(8,128)(2,1)S(1)}, u32[]{:S(2)}, u32[]{:S(2)}) collective-permute-start(bf16[32,2,32,256]{3,2,1,0:T(8,128)(2,1)} %get-tuple-element.323), channel_id=1, source_target_pairs={{0,24},{8,16},{16,8},{24,0},{1,25},{9,17},{17,9},{25,1},{2,26},{10... | collective-permute-start | bytes 3145736 | tf_op jit(solution)/shard_map/ppermute | solution.py:420
  466.1 48.9 %collective-permute-start.55 = (bf16[32,2,32,256]{3,2,1,0:T(8,128)(2,1)}, bf16[32,2,32,256]{3,2,1,0:T(8,128)(2,1)S(1)}, u32[]{:S(2)}, u32[]{:S(2)}) collective-permute-start(bf16[32,2,32,256]{3,2,1,0:T(8,128)(2,1)} %get-tuple-element.325), channel_id=1, source_target_pairs={{0,8},{8,0},{16,24},{24,16},{1,9},{9,1},{17,25},{25,17},{2,10},{10... | collective-permute-start | bytes 3145736 | tf_op jit(solution)/shard_map/ppermute | solution.py:420
  467.8 88.5 %collective-permute-start.56 = (bf16[32,2,32,256]{3,2,1,0:T(8,128)(2,1)}, bf16[32,2,32,256]{3,2,1,0:T(8,128)(2,1)S(1)}, u32[]{:S(2)}, u32[]{:S(2)}) collective-permute-start(bf16[32,2,32,256]{3,2,1,0:T(8,128)(2,1)} %get-tuple-element.326), channel_id=1, source_target_pairs={{0,16},{8,24},{16,0},{24,8},{1,17},{9,25},{17,1},{25,9},{2,18},{10... | collective-permute-start | bytes 3145736 | tf_op jit(solution)/shard_map/ppermute | solution.py:420
  468.2 88.1 %collective-permute-start.57 = (bf16[32,2,32,256]{3,2,1,0:T(8,128)(2,1)}, bf16[32,2,32,256]{3,2,1,0:T(8,128)(2,1)S(1)}, u32[]{:S(2)}, u32[]{:S(2)}) collective-permute-start(bf16[32,2,32,256]{3,2,1,0:T(8,128)(2,1)} %get-tuple-element.327), channel_id=1, source_target_pairs={{0,24},{8,16},{16,8},{24,0},{1,25},{9,17},{17,9},{25,1},{2,26},{10... | collective-permute-start | bytes 3145736 | tf_op jit(solution)/shard_map/ppermute | solution.py:420
  515.0 49.1 %collective-permute-start.67 = (bf16[32,2,32,256]{3,2,1,0:T(8,128)(2,1)}, bf16[32,2,32,256]{3,2,1,0:T(8,128)(2,1)}, u32[]{:S(2)}, u32[]{:S(2)}) collective-permute-start(bf16[32,2,32,256]{3,2,1,0:T(8,128)(2,1)} %collective-permute-done.63.refs_22_.refs_18_), channel_id=1, source_target_pairs={{0,4},{4,0},{1,5},{5,1},{2,6},{6,2},{3,7},{7,3},{8,12},{12,8},{9,1... | collective-permute-start | bytes 3145736 | tf_op jit(solution)/shard_map/ppermute | solution.py:420
  559.5 47.7 %collective-permute-start.51 = (bf16[32,2,32,256]{3,2,1,0:T(8,128)(2,1)}, bf16[32,2,32,256]{3,2,1,0:T(8,128)(2,1)}, u32[]{:S(2)}, u32[]{:S(2)}) collective-permute-start(bf16[32,2,32,256]{3,2,1,0:T(8,128)(2,1)} %get-tuple-element.319), channel_id=1, source_target_pairs={{0,24},{8,16},{16,8},{24,0},{1,25},{9,17},{17,9},{25,1},{2,26},{10... | collective-permute-start | bytes 3145736 | tf_op jit(solution)/shard_map/ppermute | solution.py:420
  588.1 45.4 %collective-permute-start.71 = (bf16[32,2,32,128]{3,2,1,0:T(8,128)(2,1)}, bf16[32,2,32,128]{3,2,1,0:T(8,128)(2,1)}, u32[]{:S(2)}, u32[]{:S(2)}) collective-permute-start(bf16[32,2,32,128]{3,2,1,0:T(8,128)(2,1)} %get-tuple-element.364), channel_id=1, source_target_pairs={{0,24},{8,16},{16,8},{24,0},{1,25},{9,17},{17,9},{25,1},{2,26},{10... | collective-permute-start | bytes 1572872 | tf_op jit(solution)/shard_map/ppermute | solution.py:420
  654.7 77.4 %collective-permute-start.72 = (bf16[32,2,32,256]{3,2,1,0:T(8,128)(2,1)}, bf16[32,2,32,256]{3,2,1,0:T(8,128)(2,1)S(1)}, u32[]{:S(2)}, u32[]{:S(2)}) collective-permute-start(bf16[32,2,32,256]{3,2,1,0:T(8,128)(2,1)} %get-tuple-element.377), channel_id=1, source_target_pairs={{0,8},{8,0},{16,24},{24,16},{1,9},{9,1},{17,25},{25,17},{2,10},{10... | collective-permute-start | bytes 3145736 | tf_op jit(solution)/shard_map/ppermute | solution.py:420
  663.3 70.9 %collective-permute-start.73 = (bf16[32,2,32,256]{3,2,1,0:T(8,128)(2,1)}, bf16[32,2,32,256]{3,2,1,0:T(8,128)(2,1)S(1)}, u32[]{:S(2)}, u32[]{:S(2)}) collective-permute-start(bf16[32,2,32,256]{3,2,1,0:T(8,128)(2,1)} %get-tuple-element.378), channel_id=1, source_target_pairs={{0,16},{8,24},{16,0},{24,8},{1,17},{9,25},{17,1},{25,9},{2,18},{10... | collective-permute-start | bytes 3145736 | tf_op jit(solution)/shard_map/ppermute | solution.py:420
  664.1 70.1 %collective-permute-start.74 = (bf16[32,2,32,256]{3,2,1,0:T(8,128)(2,1)}, bf16[32,2,32,256]{3,2,1,0:T(8,128)(2,1)S(1)}, u32[]{:S(2)}, u32[]{:S(2)}) collective-permute-start(bf16[32,2,32,256]{3,2,1,0:T(8,128)(2,1)} %get-tuple-element.379), channel_id=1, source_target_pairs={{0,24},{8,16},{16,8},{24,0},{1,25},{9,17},{17,9},{25,1},{2,26},{10... | collective-permute-start | bytes 3145736 | tf_op jit(solution)/shard_map/ppermute | solution.py:420
  715.0 45.8 %collective-permute-start.88 = (bf16[32,2,32,128]{3,2,1,0:T(8,128)(2,1)}, bf16[32,2,32,128]{3,2,1,0:T(8,128)(2,1)}, u32[]{:S(2)}, u32[]{:S(2)}) collective-permute-start(bf16[32,2,32,128]{3,2,1,0:T(8,128)(2,1)} %get-tuple-element.415), channel_id=1, source_target_pairs={{0,2},{1,3},{2,0},{3,1},{4,6},{5,7},{6,4},{7,5},{8,10},{9,11},{10,... | collective-permute-start | bytes 1572872 | tf_op jit(solution)/shard_map/ppermute | solution.py:420
  760.8 47.6 %collective-permute-start.94 = (bf16[32,2,32,128]{3,2,1,0:T(8,128)(2,1)}, bf16[32,2,32,128]{3,2,1,0:T(8,128)(2,1)S(1)}, u32[]{:S(2)}, u32[]{:S(2)}) collective-permute-start(bf16[32,2,32,128]{3,2,1,0:T(8,128)(2,1)} %get-tuple-element.428), channel_id=1, source_target_pairs={{0,2},{1,3},{2,0},{3,1},{4,6},{5,7},{6,4},{7,5},{8,10},{9,11},{10,... | collective-permute-start | bytes 1572872 | tf_op jit(solution)/shard_map/ppermute | solution.py:420
  788.5 62.5 %collective-permute-start.91 = (bf16[32,2,32,128]{3,2,1,0:T(8,128)(2,1)}, bf16[32,2,32,128]{3,2,1,0:T(8,128)(2,1)S(1)}, u32[]{:S(2)}, u32[]{:S(2)}) collective-permute-start(bf16[32,2,32,128]{3,2,1,0:T(8,128)(2,1)} %get-tuple-element.424), channel_id=1, source_target_pairs={{0,2},{1,3},{2,0},{3,1},{4,6},{5,7},{6,4},{7,5},{8,10},{9,11},{10,... | collective-permute-start | bytes 1572872 | tf_op jit(solution)/shard_map/ppermute | solution.py:420
  790.5 60.6 %collective-permute-start.92 = (bf16[32,2,32,128]{3,2,1,0:T(8,128)(2,1)}, bf16[32,2,32,128]{3,2,1,0:T(8,128)(2,1)S(1)}, u32[]{:S(2)}, u32[]{:S(2)}) collective-permute-start(bf16[32,2,32,128]{3,2,1,0:T(8,128)(2,1)} %get-tuple-element.425), channel_id=1, source_target_pairs={{0,3},{1,2},{2,1},{3,0},{4,7},{5,6},{6,5},{7,4},{8,11},{9,10},{10,... | collective-permute-start | bytes 1572872 | tf_op jit(solution)/shard_map/ppermute | solution.py:420
  (121 other events, 3866.7 us)

commit v2 on v1

--- a/solution.py
+++ b/solution.py
@@ -46,8 +46,8 @@
     (("t", 3),),
     (("l", 3),),
 )
+AHEAD = {6: (("right", 0),)}
 TASKS = {
-    6: (("right", 0),),
     7: (("left", 0),),
     9: (("right", 1),),
     10: (("pass", 0),),
@@ -58,8 +58,8 @@
 }
 TAIL = (
     ("multiply", (0, 1)),
+    ("complete", 0),
     ("multiply", (2,)),
-    ("complete", 0),
     ("share", 3),
     ("complete", 1),
     ("complete", 2),
@@ -311,11 +311,11 @@
 def assemble(plane, pieces, planes, position, count, base=None):
     chunks = len(pieces) // planes
     depth, blocks, size, width = pieces[0].shape
-    step = depth // 4
+    step = depth // 2
     out_block = (step, 1, 2, chunks * size, 2 * width)
     return pl.pallas_call(
         functools.partial(assemble_kernel, planes, chunks),
-        grid=(4, blocks),
+        grid=(depth // step, blocks),
         in_specs=[pl.BlockSpec(memory_space=pltpu.SMEM)]
         + [pl.BlockSpec((step, 1, size, width), lambda d, n: (d, n, 0, 0))] * len(pieces)
         + ([] if base is None else [pl.BlockSpec(memory_space=pl.ANY)]),
@@ -460,7 +460,7 @@
     def multiply(group):
         rights = [values[key, c, m] for key in ("right", "other") for c in range(CHUNKS) for m in range(gx)]
         lefts = [values["left", g, m] for g in group for m in range(gx)]
-        outs = product(target, lefts, rights, gx, 2)
+        outs = product(target, lefts, rights, gx, 4)
         for i, g in enumerate(group):
             values.update({("mixed", g, m): outs[i * gx + m] for m in range(gx)})
 
@@ -485,6 +485,11 @@
         keys += [key for message in messages for key in sources(message)]
         sync(*keys, *waits)
         waits = []
+        for name, g in AHEAD.get(e, ()):
+            (project_right if name == "right" else project_left)(g)
+            share(name, g)
+            keys = [(name, g, 0)] + [key for message in messages for key in sources(message)]
+            sync(*keys)
         for message in messages:
             start(message)
         if e == 0:
@@ -541,8 +546,6 @@
         needs = {"multiply": ["left"], "complete": ["mixed"], "share": ["left"]}[step]
         group = g if step == "multiply" else (g,)
         keys = [(name, c, m) for name in needs for c in group for m in range(gx)]
-        if step == "complete" and g >= 2:
-            keys += [("out", g - 2, q) for q in range(gz)]
         sync(*keys, *([previous] if previous else []))
         if step == "multiply":
             multiply(group)

time: 875 us -> 963 us (1.10)
  waiting for transfers between devices: 374 us -> 461 us
  starting transfers between devices: 225 us -> 251 us
  Pallas kernels: 201 us -> 184 us
    ppermute x67, waiting for transfers between devices: 287 us -> 366 us  [swap(): lax.ppermute(value, axis, [(i, i ^ bits) for i in range(lax.axis_size(axi...]
    ppermute x67, starting transfers between devices: 108 us -> 142 us  [swap(): lax.ppermute(value, axis, [(i, i ^ bits) for i in range(lax.axis_size(axi...]
    pallas_call x3, Pallas kernels: 65.3 us -> 55.5 us  [product(): pl.pallas_call(functools.partial(product_kernel, parts, chunks, left_chun...]
  transfers between devices with their start and end apart: 96 -> 96, of which waited for: 27 -> 30; matrix products, arithmetic and copies ran while one was open for 5% -> 5% of each run, Pallas kernels for 23% -> 17%
where the time goes in v2:
time: 963 us; the launch traced here: 952 us
  waiting for transfers between devices  461 us (48%)
  starting transfers between devices  251 us (26%)
  Pallas kernels  184 us (19%)
  local copies, waits for them, and re-layouts  28.9 us (3%)
  other arithmetic  26.2 us (3%)
    ppermute x67, waiting for transfers between devices, swap(): lax.ppermute(value, axis, [(i, i ^ bits) for i in range(lax.axis_size(axi...  366 us
    ppermute x67, starting transfers between devices, swap(): lax.ppermute(value, axis, [(i, i ^ bits) for i in range(lax.axis_size(axi...  142 us
    ppermute x29, starting transfers between devices, start(): outs = [lax.ppermute(v, 'gz', HOPS[k]) for v, k in zip(inputs, kinds)]  109 us
    ppermute x29, waiting for transfers between devices, start(): outs = [lax.ppermute(v, 'gz', HOPS[k]) for v, k in zip(inputs, kinds)]  94.4 us
    pallas_call x8, Pallas kernels, project(): pl.pallas_call(functools.partial(project_kernel, planes, emit, parts), gr...  85.9 us
    pallas_call x3, Pallas kernels, product(): pl.pallas_call(functools.partial(product_kernel, parts, chunks, left_chun...  55.5 us
    pallas_call x4, Pallas kernels, finish(): pl.pallas_call(functools.partial(finish_kernel, len(mixed)), grid=(blocks...  26.5 us
  transfers between devices with their start and end apart: 96, of which 30 were waited for; matrix products, arithmetic and copies ran while one was open for 5% of the time, Pallas kernels for 17%

profile of v2, /device:TPU:0, one launch (start us, length us, event | category | flops | bytes accessed | tf_op | source)
XLA Modules:
  0.0 952.0 jit_solution(13565075870183012319)
XLA Ops:
  41.4 14.7 %collective-permute-done.4.refs_7_ = bf16[32,2,32,256]{3,2,1,0:T(8,128)(2,1)} collective-permute-done((bf16[32,2,32,256]{3,2,1,0:T(8,128)(2,1)}, bf16[32,2,32,256]{3,2,1,0:T(8,128)(2,1)}, u32[]{:S(2)}, u32[]{:S(2)}) %collective-permute-start.4) | collective-permute-done | bytes 1048608 | tf_op jit(solution)/shard_map/ppermute | solution.py:414
  87.3 21.2 %collective-permute-done.9 = f32[769,32]{0,1:T(8,128)S(1)} collective-permute-done((f32[769,32]{0,1:T(8,128)S(1)}, f32[769,32]{0,1:T(8,128)S(1)}, u32[]{:S(2)}, u32[]{:S(2)}) %collective-permute-start.9) | collective-permute-done | bytes 98464 | tf_op jit(solution)/shard_map/ppermute | solution.py:420
  128.9 10.4 %project.8 = (bf16[32,2,32,256]{3,2,1,0:T(8,128)(2,1)}, bf16[32,2,32,256]{3,2,1,0:T(8,128)(2,1)}, bf16[32,2,32,256]{3,2,1,0:T(8,128)(2,1)}, bf16[32,2,32,256]{3,2,1,0:T(8,128)(2,1)}) custom-call(s32[1]{0:T(128)} %bitcast.plane_ref, bf16[32,2,32,256]{3,2,1,0:T(8,128)(2,1)} %copy-done.21, bf16[32,2,32,256]{3,2,1,0:T(8,128)(2,1)} %copy-done.20, ...), custom_call_target="tpu_custom_call" | custom-call | flops 4294967296 | bytes 16777216 | tf_op jit(solution)/shard_map/project/pallas_call | solution.py:153
  140.5 13.8 %collective-permute-start.12 = (bf16[32,2,32,256]{3,2,1,0:T(8,128)(2,1)S(1)}, bf16[32,2,32,256]{3,2,1,0:T(8,128)(2,1)}, u32[]{:S(2)}, u32[]{:S(2)}) collective-permute-start(bf16[32,2,32,256]{3,2,1,0:T(8,128)(2,1)S(1)} %get-tuple-element.256.refs_1_), channel_id=1, source_target_pairs={{0,1},{1,2},{2,3},{4,5},{5,6},{6,7},{8,9},{9,10},{10,11},{12,13},{... | collective-permute-start | bytes 3145736 | tf_op jit(solution)/shard_map/ppermute | solution.py:414
  177.6 11.0 %project.9 = (bf16[32,2,32,256]{3,2,1,0:T(8,128)(2,1)}, bf16[32,2,32,256]{3,2,1,0:T(8,128)(2,1)}, bf16[32,2,32,256]{3,2,1,0:T(8,128)(2,1)}, bf16[32,2,32,256]{3,2,1,0:T(8,128)(2,1)}, bf16[2,32,128,128]{3,2,1,0:T(8,128)(2,1)}) custom-call(s32[1]{0:T(128)} %bitcast.plane_ref, bf16[32,2,32,256]{3,2,1,0:T(8,128)(2,1)} %copy-done.21, ...), custom_call_target="tpu_custom_call" | custom-call | flops 4294967296 | bytes 16777216 | tf_op jit(solution)/shard_map/project/pallas_call | solution.py:153
  197.7 10.5 %project.10 = (bf16[32,2,32,256]{3,2,1,0:T(8,128)(2,1)}, bf16[32,2,32,256]{3,2,1,0:T(8,128)(2,1)}, bf16[32,2,32,256]{3,2,1,0:T(8,128)(2,1)}, bf16[32,2,32,256]{3,2,1,0:T(8,128)(2,1)}) custom-call(s32[1]{0:T(128)} %bitcast.plane_ref, bf16[32,2,32,256]{3,2,1,0:T(8,128)(2,1)} %get-tuple-element.230.refs_0_, ...), custom_call_target="tpu_custom_call" | custom-call | flops 4294967296 | bytes 16777216 | tf_op jit(solution)/shard_map/project/pallas_call | solution.py:153
  209.5 21.9 %collective-permute-done.22.refs_10_.refs_6_ = bf16[32,2,32,256]{3,2,1,0:T(8,128)(2,1)S(1)} collective-permute-done((bf16[32,2,32,256]{3,2,1,0:T(8,128)(2,1)}, bf16[32,2,32,256]{3,2,1,0:T(8,128)(2,1)S(1)}, u32[]{:S(2)}, u32[]{:S(2)}) %collective-permute-start.22) | collective-permute-done | bytes 1048608 | tf_op jit(solution)/shard_map/ppermute | solution.py:420
  244.9 11.7 %collective-permute-done.25.refs_3_ = bf16[32,2,32,256]{3,2,1,0:T(8,128)(2,1)} collective-permute-done((bf16[32,2,32,256]{3,2,1,0:T(8,128)(2,1)}, bf16[32,2,32,256]{3,2,1,0:T(8,128)(2,1)}, u32[]{:S(2)}, u32[]{:S(2)}) %collective-permute-start.25) | collective-permute-done | bytes 1048608 | tf_op jit(solution)/shard_map/ppermute | solution.py:414
  256.5 16.4 %collective-permute-done.29.refs_6_.refs_7_ = bf16[32,2,32,256]{3,2,1,0:T(8,128)(2,1)} collective-permute-done((bf16[32,2,32,256]{3,2,1,0:T(8,128)(2,1)S(1)}, bf16[32,2,32,256]{3,2,1,0:T(8,128)(2,1)}, u32[]{:S(2)}, u32[]{:S(2)}) %collective-permute-start.29) | collective-permute-done | bytes 1048608 | tf_op jit(solution)/shard_map/ppermute | solution.py:414
  280.5 20.8 %collective-permute-done.26.refs_4_ = bf16[32,2,32,256]{3,2,1,0:T(8,128)(2,1)} collective-permute-done((bf16[32,2,32,256]{3,2,1,0:T(8,128)(2,1)S(1)}, bf16[32,2,32,256]{3,2,1,0:T(8,128)(2,1)}, u32[]{:S(2)}, u32[]{:S(2)}) %collective-permute-start.26) | collective-permute-done | bytes 1048608 | tf_op jit(solution)/shard_map/ppermute | solution.py:414
  310.8 10.4 %project.11 = (bf16[32,2,32,256]{3,2,1,0:T(8,128)(2,1)}, bf16[32,2,32,256]{3,2,1,0:T(8,128)(2,1)}, bf16[32,2,32,256]{3,2,1,0:T(8,128)(2,1)}, bf16[32,2,32,256]{3,2,1,0:T(8,128)(2,1)}) custom-call(s32[1]{0:T(128)} %bitcast.plane_ref, bf16[32,2,32,256]{3,2,1,0:T(8,128)(2,1)} %copy-done.19, bf16[32,2,32,256]{3,2,1,0:T(8,128)(2,1)} %copy-done.18, ...), custom_call_target="tpu_custom_call" | custom-call | flops 4294967296 | bytes 16777216 | tf_op jit(solution)/shard_map/project/pallas_call | solution.py:153
  324.0 11.1 %project.13 = (bf16[32,2,32,256]{3,2,1,0:T(8,128)(2,1)}, bf16[32,2,32,256]{3,2,1,0:T(8,128)(2,1)}, bf16[32,2,32,256]{3,2,1,0:T(8,128)(2,1)}, bf16[32,2,32,256]{3,2,1,0:T(8,128)(2,1)}, bf16[2,32,128,128]{3,2,1,0:T(8,128)(2,1)}) custom-call(s32[1]{0:T(128)} %bitcast.plane_ref, bf16[32,2,32,256]{3,2,1,0:T(8,128)(2,1)} %get-tuple-element.230.refs_0_, ...), custom_call_target="tpu_custom_call" | custom-call | flops 4294967296 | bytes 16777216 | tf_op jit(solution)/shard_map/project/pallas_call | solution.py:153
  362.9 10.4 %project.12 = (bf16[32,2,32,256]{3,2,1,0:T(8,128)(2,1)}, bf16[32,2,32,256]{3,2,1,0:T(8,128)(2,1)}, bf16[32,2,32,256]{3,2,1,0:T(8,128)(2,1)}, bf16[32,2,32,256]{3,2,1,0:T(8,128)(2,1)}) custom-call(s32[1]{0:T(128)} %bitcast.plane_ref, bf16[32,2,32,256]{3,2,1,0:T(8,128)(2,1)} %get-tuple-element.265.refs_0_, ...), custom_call_target="tpu_custom_call" | custom-call | flops 4294967296 | bytes 16777216 | tf_op jit(solution)/shard_map/project/pallas_call | solution.py:153
  375.4 11.0 %project.14 = (bf16[32,2,32,256]{3,2,1,0:T(8,128)(2,1)}, bf16[32,2,32,256]{3,2,1,0:T(8,128)(2,1)}, bf16[32,2,32,256]{3,2,1,0:T(8,128)(2,1)}, bf16[32,2,32,256]{3,2,1,0:T(8,128)(2,1)}, bf16[2,32,128,128]{3,2,1,0:T(8,128)(2,1)}) custom-call(s32[1]{0:T(128)} %bitcast.plane_ref, bf16[32,2,32,256]{3,2,1,0:T(8,128)(2,1)} %copy-done.19, ...), custom_call_target="tpu_custom_call" | custom-call | flops 4294967296 | bytes 16777216 | tf_op jit(solution)/shard_map/project/pallas_call | solution.py:153
  386.5 11.1 %project.15 = (bf16[32,2,32,256]{3,2,1,0:T(8,128)(2,1)}, bf16[32,2,32,256]{3,2,1,0:T(8,128)(2,1)}, bf16[32,2,32,256]{3,2,1,0:T(8,128)(2,1)}, bf16[32,2,32,256]{3,2,1,0:T(8,128)(2,1)}, bf16[2,32,128,128]{3,2,1,0:T(8,128)(2,1)}) custom-call(s32[1]{0:T(128)} %bitcast.plane_ref, bf16[32,2,32,256]{3,2,1,0:T(8,128)(2,1)} %get-tuple-element.265.refs_0_, ...), custom_call_target="tpu_custom_call" | custom-call | flops 4294967296 | bytes 16777216 | tf_op jit(solution)/shard_map/project/pallas_call | solution.py:153
  410.1 20.5 %collective-permute-done.62.refs_21_.refs_17_ = bf16[32,2,32,256]{3,2,1,0:T(8,128)(2,1)} collective-permute-done((bf16[32,2,32,256]{3,2,1,0:T(8,128)(2,1)}, bf16[32,2,32,256]{3,2,1,0:T(8,128)(2,1)}, u32[]{:S(2)}, u32[]{:S(2)}) %collective-permute-start.62) | collective-permute-done | bytes 1048608 | tf_op jit(solution)/shard_map/ppermute | solution.py:420
  430.6 21.2 %collective-permute-done.63.refs_22_.refs_18_ = bf16[32,2,32,256]{3,2,1,0:T(8,128)(2,1)} collective-permute-done((bf16[32,2,32,256]{3,2,1,0:T(8,128)(2,1)}, bf16[32,2,32,256]{3,2,1,0:T(8,128)(2,1)}, u32[]{:S(2)}, u32[]{:S(2)}) %collective-permute-start.63) | collective-permute-done | bytes 1048608 | tf_op jit(solution)/shard_map/ppermute | solution.py:420
  459.6 20.2 %collective-permute-done.52.refs_1_ = bf16[32,2,32,256]{3,2,1,0:T(8,128)(2,1)S(1)} collective-permute-done((bf16[32,2,32,256]{3,2,1,0:T(8,128)(2,1)}, bf16[32,2,32,256]{3,2,1,0:T(8,128)(2,1)S(1)}, u32[]{:S(2)}, u32[]{:S(2)}) %collective-permute-start.52) | collective-permute-done | bytes 1048608 | tf_op jit(solution)/shard_map/ppermute | solution.py:420
  481.7 21.3 %collective-permute-done.53.refs_2_ = bf16[32,2,32,256]{3,2,1,0:T(8,128)(2,1)S(1)} collective-permute-done((bf16[32,2,32,256]{3,2,1,0:T(8,128)(2,1)}, bf16[32,2,32,256]{3,2,1,0:T(8,128)(2,1)S(1)}, u32[]{:S(2)}, u32[]{:S(2)}) %collective-permute-start.53) | collective-permute-done | bytes 1048608 | tf_op jit(solution)/shard_map/ppermute | solution.py:420
  503.6 21.2 %collective-permute-done.55.refs_5_ = bf16[32,2,32,256]{3,2,1,0:T(8,128)(2,1)S(1)} collective-permute-done((bf16[32,2,32,256]{3,2,1,0:T(8,128)(2,1)}, bf16[32,2,32,256]{3,2,1,0:T(8,128)(2,1)S(1)}, u32[]{:S(2)}, u32[]{:S(2)}) %collective-permute-start.55) | collective-permute-done | bytes 1048608 | tf_op jit(solution)/shard_map/ppermute | solution.py:420
  524.8 22.4 %collective-permute-done.56.refs_6_ = bf16[32,2,32,256]{3,2,1,0:T(8,128)(2,1)S(1)} collective-permute-done((bf16[32,2,32,256]{3,2,1,0:T(8,128)(2,1)}, bf16[32,2,32,256]{3,2,1,0:T(8,128)(2,1)S(1)}, u32[]{:S(2)}, u32[]{:S(2)}) %collective-permute-start.56) | collective-permute-done | bytes 1048608 | tf_op jit(solution)/shard_map/ppermute | solution.py:420
  551.0 19.5 %product.3 = (bf16[32,2,32,128]{3,2,1,0:T(8,128)(2,1)}, bf16[32,2,32,128]{3,2,1,0:T(8,128)(2,1)}, bf16[32,2,32,128]{3,2,1,0:T(8,128)(2,1)}, bf16[32,2,32,128]{3,...) custom-call(s32[4]{0:T(128)} %iota_xor_fusion.1.target_ref, ...), custom_call_target="tpu_custom_call" | custom-call | flops 4294967296 | bytes 41943040 | tf_op jit(solution)/shard_map/product/pallas_call | solution.py:218
  590.6 52.0 %collective-permute-done.70.refs_2_ = bf16[32,2,32,128]{3,2,1,0:T(8,128)(2,1)} collective-permute-done((bf16[32,2,32,128]{3,2,1,0:T(8,128)(2,1)}, bf16[32,2,32,128]{3,2,1,0:T(8,128)(2,1)}, u32[]{:S(2)}, u32[]{:S(2)}) %collective-permute-start.70) | collective-permute-done | bytes 524320 | tf_op jit(solution)/shard_map/ppermute | solution.py:420
  654.8 17.9 %product.4 = (bf16[32,2,32,128]{3,2,1,0:T(8,128)(2,1)}, bf16[32,2,32,128]{3,2,1,0:T(8,128)(2,1)}, bf16[32,2,32,128]{3,2,1,0:T(8,128)(2,1)}, bf16[32,2,32,128]{3,2,1,0:T(8,128)(2,1)}) custom-call(s32[4]{0:T(128)} %iota_xor_fusion.1.target_ref, bf16[32,2,32,256]{3,2,1,0:T(8,128)(2,1)} %get-tuple-element.365.refs_0_, bf16[32,2,32,256]{3,2,1,0:T(8,128)(2,1)} %copy-done.29, ...), custom_call_target="tpu_custom_call" | custom-call | flops 2147483648 | bytes 37748736 | tf_op jit(solution)/shard_map/product/pallas_call | solution.py:218
  696.0 46.3 %collective-permute-done.79.refs_2_ = bf16[32,2,32,128]{3,2,1,0:T(8,128)(2,1)} collective-permute-done((bf16[32,2,32,128]{3,2,1,0:T(8,128)(2,1)}, bf16[32,2,32,128]{3,2,1,0:T(8,128)(2,1)}, u32[]{:S(2)}, u32[]{:S(2)}) %collective-permute-start.79) | collective-permute-done | bytes 524320 | tf_op jit(solution)/shard_map/ppermute | solution.py:420
  742.4 28.1 %collective-permute-start.93 = (bf16[32,2,32,128]{3,2,1,0:T(8,128)(2,1)}, bf16[32,2,32,128]{3,2,1,0:T(8,128)(2,1)}, u32[]{:S(2)}, u32[]{:S(2)}) collective-permute-start(bf16[32,2,32,128]{3,2,1,0:T(8,128)(2,1)} %get-tuple-element.421), channel_id=1, source_target_pairs={{0,1},{1,0},{2,3},{3,2},{4,5},{5,4},{6,7},{7,6},{8,9},{9,8},{10,11... | collective-permute-start | bytes 1572872 | tf_op jit(solution)/shard_map/ppermute | solution.py:420
  779.8 18.1 %product.5 = (bf16[32,2,32,128]{3,2,1,0:T(8,128)(2,1)}, bf16[32,2,32,128]{3,2,1,0:T(8,128)(2,1)}, bf16[32,2,32,128]{3,2,1,0:T(8,128)(2,1)}, bf16[32,2,32,128]{3,2,1,0:T(8,128)(2,1)}) custom-call(s32[4]{0:T(128)} %iota_xor_fusion.1.target_ref, bf16[32,2,32,256]{3,2,1,0:T(8,128)(2,1)} %get-tuple-element.395.refs_0_, bf16[32,2,32,256]{3,2,1,0:T(8,128)(2,1)} %copy-done.27, ...), custom_call_target="tpu_custom_call" | custom-call | flops 2147483648 | bytes 37748736 | tf_op jit(solution)/shard_map/product/pallas_call | solution.py:218
  822.0 19.8 %collective-permute-start.88 = (bf16[32,2,32,128]{3,2,1,0:T(8,128)(2,1)}, bf16[32,2,32,128]{3,2,1,0:T(8,128)(2,1)S(1)}, u32[]{:S(2)}, u32[]{:S(2)}) collective-permute-start(bf16[32,2,32,128]{3,2,1,0:T(8,128)(2,1)} %get-tuple-element.414), channel_id=1, source_target_pairs={{0,2},{1,3},{2,0},{3,1},{4,6},{5,7},{6,4},{7,5},{8,10},{9,11},{10,... | collective-permute-start | bytes 1572872 | tf_op jit(solution)/shard_map/ppermute | solution.py:420
  848.6 14.7 %collective-permute-done.91.refs_2_ = bf16[32,2,32,128]{3,2,1,0:T(8,128)(2,1)S(1)} collective-permute-done((bf16[32,2,32,128]{3,2,1,0:T(8,128)(2,1)}, bf16[32,2,32,128]{3,2,1,0:T(8,128)(2,1)S(1)}, u32[]{:S(2)}, u32[]{:S(2)}) %collective-permute-start.91) | collective-permute-done | bytes 524320 | tf_op jit(solution)/shard_map/ppermute | solution.py:420
  863.3 29.8 %collective-permute-start.85 = (bf16[32,2,32,128]{3,2,1,0:T(8,128)(2,1)}, bf16[32,2,32,128]{3,2,1,0:T(8,128)(2,1)}, u32[]{:S(2)}, u32[]{:S(2)}) collective-permute-start(bf16[32,2,32,128]{3,2,1,0:T(8,128)(2,1)} %get-tuple-element.410), channel_id=1, source_target_pairs={{0,2},{1,3},{2,0},{3,1},{4,6},{5,7},{6,4},{7,5},{8,10},{9,11},{10,... | collective-permute-start | bytes 1572872 | tf_op jit(solution)/shard_map/ppermute | solution.py:420
  904.9 20.6 %collective-permute-done.88.refs_2_ = bf16[32,2,32,128]{3,2,1,0:T(8,128)(2,1)S(1)} collective-permute-done((bf16[32,2,32,128]{3,2,1,0:T(8,128)(2,1)}, bf16[32,2,32,128]{3,2,1,0:T(8,128)(2,1)S(1)}, u32[]{:S(2)}, u32[]{:S(2)}) %collective-permute-start.88) | collective-permute-done | bytes 524320 | tf_op jit(solution)/shard_map/ppermute | solution.py:420
  931.0 17.0 %collective-permute-done.85.refs_2_ = bf16[32,2,32,128]{3,2,1,0:T(8,128)(2,1)} collective-permute-done((bf16[32,2,32,128]{3,2,1,0:T(8,128)(2,1)}, bf16[32,2,32,128]{3,2,1,0:T(8,128)(2,1)}, u32[]{:S(2)}, u32[]{:S(2)}) %collective-permute-start.85) | collective-permute-done | bytes 524320 | tf_op jit(solution)/shard_map/ppermute | solution.py:420
  (366 shorter events, 334.3 us)
Async XLA Ops:
  17.3 69.9 %collective-permute-start.10 = (f32[769,32]{0,1:T(8,128)S(1)}, f32[769,32]{0,1:T(8,128)}, u32[]{:S(2)}, u32[]{:S(2)}) collective-permute-start(f32[769,32]{0,1:T(8,128)S(1)} %constant_dynamic-update-slice_fusion), channel_id=1, source_target_pairs={{0,3},{1,2},{2,1},{3,0},{4,7},{5,6},{6,5},{7,4},{8,11},{9,10},{10,... | collective-permute-start | bytes 295304 | tf_op jit(solution)/shard_map/ppermute | solution.py:420
  56.2 63.9 %collective-permute-start.15 = (bf16[32,2,32,256]{3,2,1,0:T(8,128)(2,1)}, bf16[32,2,32,256]{3,2,1,0:T(8,128)(2,1)}, u32[]{:S(2)}, u32[]{:S(2)}) collective-permute-start(bf16[32,2,32,256]{3,2,1,0:T(8,128)(2,1)} %get-tuple-element.230.refs_0_), channel_id=1, source_target_pairs={{3,2},{2,1},{1,0},{7,6},{6,5},{5,4},{11,10},{10,9},{9,8},{15,14},{... | collective-permute-start | bytes 3145736 | tf_op jit(solution)/shard_map/ppermute | solution.py:414
  57.4 62.6 %collective-permute-start.16 = (bf16[32,2,32,256]{3,2,1,0:T(8,128)(2,1)}, bf16[32,2,32,256]{3,2,1,0:T(8,128)(2,1)}, u32[]{:S(2)}, u32[]{:S(2)}) collective-permute-start(bf16[32,2,32,256]{3,2,1,0:T(8,128)(2,1)} %get-tuple-element.231.refs_1_), channel_id=1, source_target_pairs={{0,1},{1,2},{2,3},{4,5},{5,6},{6,7},{8,9},{9,10},{10,11},{12,13},{... | collective-permute-start | bytes 3145736 | tf_op jit(solution)/shard_map/ppermute | solution.py:414
  139.2 49.4 %collective-permute-start.11 = (bf16[32,2,32,256]{3,2,1,0:T(8,128)(2,1)S(1)}, bf16[32,2,32,256]{3,2,1,0:T(8,128)(2,1)}, u32[]{:S(2)}, u32[]{:S(2)}) collective-permute-start(bf16[32,2,32,256]{3,2,1,0:T(8,128)(2,1)S(1)} %get-tuple-element.253.refs_0_), channel_id=1, source_target_pairs={{3,2},{2,1},{1,0},{7,6},{6,5},{5,4},{11,10},{10,9},{9,8},{15,14},{... | collective-permute-start | bytes 3145736 | tf_op jit(solution)/shard_map/ppermute | solution.py:414
  140.5 49.7 %collective-permute-start.12 = (bf16[32,2,32,256]{3,2,1,0:T(8,128)(2,1)S(1)}, bf16[32,2,32,256]{3,2,1,0:T(8,128)(2,1)}, u32[]{:S(2)}, u32[]{:S(2)}) collective-permute-start(bf16[32,2,32,256]{3,2,1,0:T(8,128)(2,1)S(1)} %get-tuple-element.256.refs_1_), channel_id=1, source_target_pairs={{0,1},{1,2},{2,3},{4,5},{5,6},{6,7},{8,9},{9,10},{10,11},{12,13},{... | collective-permute-start | bytes 3145736 | tf_op jit(solution)/shard_map/ppermute | solution.py:414
  275.0 60.1 %collective-permute-start.37 = (bf16[32,2,32,256]{3,2,1,0:T(8,128)(2,1)}, bf16[32,2,32,256]{3,2,1,0:T(8,128)(2,1)}, u32[]{:S(2)}, u32[]{:S(2)}) collective-permute-start(bf16[32,2,32,256]{3,2,1,0:T(8,128)(2,1)} %get-tuple-element.289), channel_id=1, source_target_pairs={{0,8},{8,0},{16,24},{24,16},{1,9},{9,1},{17,25},{25,17},{2,10},{10... | collective-permute-start | bytes 3145736 | tf_op jit(solution)/shard_map/ppermute | solution.py:420
  276.1 61.0 %collective-permute-start.38 = (bf16[32,2,32,256]{3,2,1,0:T(8,128)(2,1)}, bf16[32,2,32,256]{3,2,1,0:T(8,128)(2,1)}, u32[]{:S(2)}, u32[]{:S(2)}) collective-permute-start(bf16[32,2,32,256]{3,2,1,0:T(8,128)(2,1)} %get-tuple-element.290), channel_id=1, source_target_pairs={{0,16},{8,24},{16,0},{24,8},{1,17},{9,25},{17,1},{25,9},{2,18},{10... | collective-permute-start | bytes 3145736 | tf_op jit(solution)/shard_map/ppermute | solution.py:420
  279.1 58.0 %collective-permute-start.39 = (bf16[32,2,32,256]{3,2,1,0:T(8,128)(2,1)}, bf16[32,2,32,256]{3,2,1,0:T(8,128)(2,1)}, u32[]{:S(2)}, u32[]{:S(2)}) collective-permute-start(bf16[32,2,32,256]{3,2,1,0:T(8,128)(2,1)} %get-tuple-element.291), channel_id=1, source_target_pairs={{0,24},{8,16},{16,8},{24,0},{1,25},{9,17},{17,9},{25,1},{2,26},{10... | collective-permute-start | bytes 3145736 | tf_op jit(solution)/shard_map/ppermute | solution.py:420
  373.3 57.3 %collective-permute-start.62 = (bf16[32,2,32,256]{3,2,1,0:T(8,128)(2,1)}, bf16[32,2,32,256]{3,2,1,0:T(8,128)(2,1)}, u32[]{:S(2)}, u32[]{:S(2)}) collective-permute-start(bf16[32,2,32,256]{3,2,1,0:T(8,128)(2,1)} %get-tuple-element.336), channel_id=1, source_target_pairs={{0,8},{8,0},{16,24},{24,16},{1,9},{9,1},{17,25},{25,17},{2,10},{10... | collective-permute-start | bytes 3145736 | tf_op jit(solution)/shard_map/ppermute | solution.py:420
  373.9 77.9 %collective-permute-start.63 = (bf16[32,2,32,256]{3,2,1,0:T(8,128)(2,1)}, bf16[32,2,32,256]{3,2,1,0:T(8,128)(2,1)}, u32[]{:S(2)}, u32[]{:S(2)}) collective-permute-start(bf16[32,2,32,256]{3,2,1,0:T(8,128)(2,1)} %get-tuple-element.337), channel_id=1, source_target_pairs={{0,16},{8,24},{16,0},{24,8},{1,17},{9,25},{17,1},{25,9},{2,18},{10... | collective-permute-start | bytes 3145736 | tf_op jit(solution)/shard_map/ppermute | solution.py:420
  397.6 55.9 %collective-permute-start.64 = (bf16[32,2,32,256]{3,2,1,0:T(8,128)(2,1)}, bf16[32,2,32,256]{3,2,1,0:T(8,128)(2,1)S(1)}, u32[]{:S(2)}, u32[]{:S(2)}) collective-permute-start(bf16[32,2,32,256]{3,2,1,0:T(8,128)(2,1)} %get-tuple-element.338), channel_id=1, source_target_pairs={{0,24},{8,16},{16,8},{24,0},{1,25},{9,17},{17,9},{25,1},{2,26},{10... | collective-permute-start | bytes 3145736 | tf_op jit(solution)/shard_map/ppermute | solution.py:420
  457.0 67.7 %collective-permute-start.55 = (bf16[32,2,32,256]{3,2,1,0:T(8,128)(2,1)}, bf16[32,2,32,256]{3,2,1,0:T(8,128)(2,1)S(1)}, u32[]{:S(2)}, u32[]{:S(2)}) collective-permute-start(bf16[32,2,32,256]{3,2,1,0:T(8,128)(2,1)} %get-tuple-element.320), channel_id=1, source_target_pairs={{0,8},{8,0},{16,24},{24,16},{1,9},{9,1},{17,25},{25,17},{2,10},{10... | collective-permute-start | bytes 3145736 | tf_op jit(solution)/shard_map/ppermute | solution.py:420
  457.8 89.3 %collective-permute-start.56 = (bf16[32,2,32,256]{3,2,1,0:T(8,128)(2,1)}, bf16[32,2,32,256]{3,2,1,0:T(8,128)(2,1)S(1)}, u32[]{:S(2)}, u32[]{:S(2)}) collective-permute-start(bf16[32,2,32,256]{3,2,1,0:T(8,128)(2,1)} %get-tuple-element.321), channel_id=1, source_target_pairs={{0,16},{8,24},{16,0},{24,8},{1,17},{9,25},{17,1},{25,9},{2,18},{10... | collective-permute-start | bytes 3145736 | tf_op jit(solution)/shard_map/ppermute | solution.py:420
  479.8 69.1 %collective-permute-start.57 = (bf16[32,2,32,256]{3,2,1,0:T(8,128)(2,1)}, bf16[32,2,32,256]{3,2,1,0:T(8,128)(2,1)}, u32[]{:S(2)}, u32[]{:S(2)}) collective-permute-start(bf16[32,2,32,256]{3,2,1,0:T(8,128)(2,1)} %get-tuple-element.322), channel_id=1, source_target_pairs={{0,24},{8,16},{16,8},{24,0},{1,25},{9,17},{17,9},{25,1},{2,26},{10... | collective-permute-start | bytes 3145736 | tf_op jit(solution)/shard_map/ppermute | solution.py:420
  570.6 81.4 %collective-permute-start.49 = (bf16[32,2,32,256]{3,2,1,0:T(8,128)(2,1)}, bf16[32,2,32,256]{3,2,1,0:T(8,128)(2,1)S(1)}, u32[]{:S(2)}, u32[]{:S(2)}) collective-permute-start(bf16[32,2,32,256]{3,2,1,0:T(8,128)(2,1)} %get-tuple-element.312), channel_id=1, source_target_pairs={{0,8},{8,0},{16,24},{24,16},{1,9},{9,1},{17,25},{25,17},{2,10},{10... | collective-permute-start | bytes 3145736 | tf_op jit(solution)/shard_map/ppermute | solution.py:420
  572.7 80.7 %collective-permute-start.50 = (bf16[32,2,32,256]{3,2,1,0:T(8,128)(2,1)}, bf16[32,2,32,256]{3,2,1,0:T(8,128)(2,1)S(1)}, u32[]{:S(2)}, u32[]{:S(2)}) collective-permute-start(bf16[32,2,32,256]{3,2,1,0:T(8,128)(2,1)} %get-tuple-element.313), channel_id=1, source_target_pairs={{0,16},{8,24},{16,0},{24,8},{1,17},{9,25},{17,1},{25,9},{2,18},{10... | collective-permute-start | bytes 3145736 | tf_op jit(solution)/shard_map/ppermute | solution.py:420
  574.4 79.0 %collective-permute-start.51 = (bf16[32,2,32,256]{3,2,1,0:T(8,128)(2,1)}, bf16[32,2,32,256]{3,2,1,0:T(8,128)(2,1)S(1)}, u32[]{:S(2)}, u32[]{:S(2)}) collective-permute-start(bf16[32,2,32,256]{3,2,1,0:T(8,128)(2,1)} %get-tuple-element.314), channel_id=1, source_target_pairs={{0,24},{8,16},{16,8},{24,0},{1,25},{9,17},{17,9},{25,1},{2,26},{10... | collective-permute-start | bytes 3145736 | tf_op jit(solution)/shard_map/ppermute | solution.py:420
  576.2 66.4 %collective-permute-start.70 = (bf16[32,2,32,128]{3,2,1,0:T(8,128)(2,1)}, bf16[32,2,32,128]{3,2,1,0:T(8,128)(2,1)}, u32[]{:S(2)}, u32[]{:S(2)}) collective-permute-start(bf16[32,2,32,128]{3,2,1,0:T(8,128)(2,1)} %get-tuple-element.357), channel_id=1, source_target_pairs={{0,16},{8,24},{16,0},{24,8},{1,17},{9,25},{17,1},{25,9},{2,18},{10... | collective-permute-start | bytes 1572872 | tf_op jit(solution)/shard_map/ppermute | solution.py:420
  585.7 57.3 %collective-permute-start.71 = (bf16[32,2,32,128]{3,2,1,0:T(8,128)(2,1)}, bf16[32,2,32,128]{3,2,1,0:T(8,128)(2,1)}, u32[]{:S(2)}, u32[]{:S(2)}) collective-permute-start(bf16[32,2,32,128]{3,2,1,0:T(8,128)(2,1)} %get-tuple-element.358), channel_id=1, source_target_pairs={{0,24},{8,16},{16,8},{24,0},{1,25},{9,17},{17,9},{25,1},{2,26},{10... | collective-permute-start | bytes 1572872 | tf_op jit(solution)/shard_map/ppermute | solution.py:420
  673.2 104.8 %collective-permute-start.72 = (bf16[32,2,32,256]{3,2,1,0:T(8,128)(2,1)}, bf16[32,2,32,256]{3,2,1,0:T(8,128)(2,1)S(1)}, u32[]{:S(2)}, u32[]{:S(2)}) collective-permute-start(bf16[32,2,32,256]{3,2,1,0:T(8,128)(2,1)} %get-tuple-element.371), channel_id=1, source_target_pairs={{0,8},{8,0},{16,24},{24,16},{1,9},{9,1},{17,25},{25,17},{2,10},{10... | collective-permute-start | bytes 3145736 | tf_op jit(solution)/shard_map/ppermute | solution.py:420
  674.8 103.3 %collective-permute-start.73 = (bf16[32,2,32,256]{3,2,1,0:T(8,128)(2,1)}, bf16[32,2,32,256]{3,2,1,0:T(8,128)(2,1)S(1)}, u32[]{:S(2)}, u32[]{:S(2)}) collective-permute-start(bf16[32,2,32,256]{3,2,1,0:T(8,128)(2,1)} %get-tuple-element.372), channel_id=1, source_target_pairs={{0,16},{8,24},{16,0},{24,8},{1,17},{9,25},{17,1},{25,9},{2,18},{10... | collective-permute-start | bytes 3145736 | tf_op jit(solution)/shard_map/ppermute | solution.py:420
  676.5 101.6 %collective-permute-start.74 = (bf16[32,2,32,256]{3,2,1,0:T(8,128)(2,1)}, bf16[32,2,32,256]{3,2,1,0:T(8,128)(2,1)S(1)}, u32[]{:S(2)}, u32[]{:S(2)}) collective-permute-start(bf16[32,2,32,256]{3,2,1,0:T(8,128)(2,1)} %get-tuple-element.373), channel_id=1, source_target_pairs={{0,24},{8,16},{16,8},{24,0},{1,25},{9,17},{17,9},{25,1},{2,26},{10... | collective-permute-start | bytes 3145736 | tf_op jit(solution)/shard_map/ppermute | solution.py:420
  676.7 65.6 %collective-permute-start.79 = (bf16[32,2,32,128]{3,2,1,0:T(8,128)(2,1)}, bf16[32,2,32,128]{3,2,1,0:T(8,128)(2,1)}, u32[]{:S(2)}, u32[]{:S(2)}) collective-permute-start(bf16[32,2,32,128]{3,2,1,0:T(8,128)(2,1)} %get-tuple-element.381), channel_id=1, source_target_pairs={{0,16},{8,24},{16,0},{24,8},{1,17},{9,25},{17,1},{25,9},{2,18},{10... | collective-permute-start | bytes 1572872 | tf_op jit(solution)/shard_map/ppermute | solution.py:420
  687.8 82.6 %collective-permute-start.80 = (bf16[32,2,32,128]{3,2,1,0:T(8,128)(2,1)}, bf16[32,2,32,128]{3,2,1,0:T(8,128)(2,1)}, u32[]{:S(2)}, u32[]{:S(2)}) collective-permute-start(bf16[32,2,32,128]{3,2,1,0:T(8,128)(2,1)} %get-tuple-element.382), channel_id=1, source_target_pairs={{0,24},{8,16},{16,8},{24,0},{1,25},{9,17},{17,9},{25,1},{2,26},{10... | collective-permute-start | bytes 1572872 | tf_op jit(solution)/shard_map/ppermute | solution.py:420
  742.4 59.1 %collective-permute-start.93 = (bf16[32,2,32,128]{3,2,1,0:T(8,128)(2,1)}, bf16[32,2,32,128]{3,2,1,0:T(8,128)(2,1)}, u32[]{:S(2)}, u32[]{:S(2)}) collective-permute-start(bf16[32,2,32,128]{3,2,1,0:T(8,128)(2,1)} %get-tuple-element.421), channel_id=1, source_target_pairs={{0,1},{1,0},{2,3},{3,2},{4,5},{5,4},{6,7},{7,6},{8,9},{9,8},{10,11... | collective-permute-start | bytes 1572872 | tf_op jit(solution)/shard_map/ppermute | solution.py:420
  813.0 50.3 %collective-permute-start.91 = (bf16[32,2,32,128]{3,2,1,0:T(8,128)(2,1)}, bf16[32,2,32,128]{3,2,1,0:T(8,128)(2,1)S(1)}, u32[]{:S(2)}, u32[]{:S(2)}) collective-permute-start(bf16[32,2,32,128]{3,2,1,0:T(8,128)(2,1)} %get-tuple-element.418), channel_id=1, source_target_pairs={{0,2},{1,3},{2,0},{3,1},{4,6},{5,7},{6,4},{7,5},{8,10},{9,11},{10,... | collective-permute-start | bytes 1572872 | tf_op jit(solution)/shard_map/ppermute | solution.py:420
  822.0 71.1 %collective-permute-start.87 = (bf16[32,2,32,128]{3,2,1,0:T(8,128)(2,1)}, bf16[32,2,32,128]{3,2,1,0:T(8,128)(2,1)S(1)}, u32[]{:S(2)}, u32[]{:S(2)}) collective-permute-start(bf16[32,2,32,128]{3,2,1,0:T(8,128)(2,1)} %get-tuple-element.413), channel_id=1, source_target_pairs={{0,1},{1,0},{2,3},{3,2},{4,5},{5,4},{6,7},{7,6},{8,9},{9,8},{10,11... | collective-permute-start | bytes 1572872 | tf_op jit(solution)/shard_map/ppermute | solution.py:420
  822.0 103.4 %collective-permute-start.88 = (bf16[32,2,32,128]{3,2,1,0:T(8,128)(2,1)}, bf16[32,2,32,128]{3,2,1,0:T(8,128)(2,1)S(1)}, u32[]{:S(2)}, u32[]{:S(2)}) collective-permute-start(bf16[32,2,32,128]{3,2,1,0:T(8,128)(2,1)} %get-tuple-element.414), channel_id=1, source_target_pairs={{0,2},{1,3},{2,0},{3,1},{4,6},{5,7},{6,4},{7,5},{8,10},{9,11},{10,... | collective-permute-start | bytes 1572872 | tf_op jit(solution)/shard_map/ppermute | solution.py:420
  841.8 83.6 %collective-permute-start.89 = (bf16[32,2,32,128]{3,2,1,0:T(8,128)(2,1)}, bf16[32,2,32,128]{3,2,1,0:T(8,128)(2,1)S(1)}, u32[]{:S(2)}, u32[]{:S(2)}) collective-permute-start(bf16[32,2,32,128]{3,2,1,0:T(8,128)(2,1)} %get-tuple-element.415), channel_id=1, source_target_pairs={{0,3},{1,2},{2,1},{3,0},{4,7},{5,6},{6,5},{7,4},{8,11},{9,10},{10,... | collective-permute-start | bytes 1572872 | tf_op jit(solution)/shard_map/ppermute | solution.py:420
  863.3 67.7 %collective-permute-start.84 = (bf16[32,2,32,128]{3,2,1,0:T(8,128)(2,1)}, bf16[32,2,32,128]{3,2,1,0:T(8,128)(2,1)}, u32[]{:S(2)}, u32[]{:S(2)}) collective-permute-start(bf16[32,2,32,128]{3,2,1,0:T(8,128)(2,1)} %get-tuple-element.409), channel_id=1, source_target_pairs={{0,1},{1,0},{2,3},{3,2},{4,5},{5,4},{6,7},{7,6},{8,9},{9,8},{10,11... | collective-permute-start | bytes 1572872 | tf_op jit(solution)/shard_map/ppermute | solution.py:420
  863.3 84.7 %collective-permute-start.85 = (bf16[32,2,32,128]{3,2,1,0:T(8,128)(2,1)}, bf16[32,2,32,128]{3,2,1,0:T(8,128)(2,1)}, u32[]{:S(2)}, u32[]{:S(2)}) collective-permute-start(bf16[32,2,32,128]{3,2,1,0:T(8,128)(2,1)} %get-tuple-element.410), channel_id=1, source_target_pairs={{0,2},{1,3},{2,0},{3,1},{4,6},{5,7},{6,4},{7,5},{8,10},{9,11},{10,... | collective-permute-start | bytes 1572872 | tf_op jit(solution)/shard_map/ppermute | solution.py:420
  893.1 54.9 %collective-permute-start.86 = (bf16[32,2,32,128]{3,2,1,0:T(8,128)(2,1)}, bf16[32,2,32,128]{3,2,1,0:T(8,128)(2,1)}, u32[]{:S(2)}, u32[]{:S(2)}) collective-permute-start(bf16[32,2,32,128]{3,2,1,0:T(8,128)(2,1)} %get-tuple-element.411), channel_id=1, source_target_pairs={{0,3},{1,2},{2,1},{3,0},{4,7},{5,6},{6,5},{7,4},{8,11},{9,10},{10,... | collective-permute-start | bytes 1572872 | tf_op jit(solution)/shard_map/ppermute | solution.py:420
  (120 other events, 3914.3 us)

commit v3 on v2

--- a/solution.py
+++ b/solution.py
@@ -54,7 +54,7 @@
     12: (("right", 2),),
     13: (("left", 1),),
     14: (("pass", 1),),
-    15: (("right", 3), ("left", 2)),
+    15: (("right", 3), ("early", 3), ("left", 2)),
 }
 TAIL = (
     ("multiply", (0, 1)),
@@ -423,8 +423,8 @@
         for m in range(1, gx):
             values[name, g, m] = swap(values[name, g, m], "gx", m)
 
-    def pass_on(g):
-        for m in range(gx):
+    def pass_on(g, which=None):
+        for m in range(gx) if which is None else which:
             values["other", g, m] = swap(values["right", g, m], "gy", 1)
 
     def project_right(g):
@@ -523,6 +523,8 @@
         for name, g in TASKS.get(e, ()):
             if name == "pass":
                 pass_on(g)
+            elif name == "early":
+                pass_on(g, range(1))
             else:
                 (project_right if name == "right" else project_left)(g)
                 share(name, g)
@@ -533,14 +535,19 @@
         for name, g in TASKS.get(e - 1, ()):
             if name == "pass":
                 waits += [("other", g, m) for m in range(gx)]
+        for name, g in TASKS.get(e - 3, ()):
+            if name == "left":
+                waits += [("left", g, m) for m in range(gx)]
 
     last = CHUNKS - 1
     sync(*waits, *[key for event in EVENTS[-2:] for message in event for key in results(message)])
     project_left(last)
     sync(("left", last, 0), *[("right", last - 1, m) for m in range(gx)])
     pass_on(last - 1)
-    sync(*[(name, g, m) for name, g in (("other", last - 1), ("right", last)) for m in range(gx)])
-    pass_on(last)
+    sync(("right", last, 1), *[("other", last - 1, m) for m in range(gx)])
+    pass_on(last, range(1, 2))
+    sync(("other", last, 1), *[("right", last, m) for m in range(2, gx)])
+    pass_on(last, range(2, gx))
     previous = None
     for step, g in TAIL:
         needs = {"multiply": ["left"], "complete": ["mixed"], "share": ["left"]}[step]

time: 963 us -> 926 us (0.962)
  waiting for transfers between devices: 461 us -> 408 us
  starting transfers between devices: 251 us -> 269 us
    ppermute x29, waiting for transfers between devices: 94.4 us -> 62.2 us  [start(): outs = [lax.ppermute(v, 'gz', HOPS[k]) for v, k in zip(inputs, kinds)]]
    ppermute x67, waiting for transfers between devices: 366 us -> 345 us  [swap(): lax.ppermute(value, axis, [(i, i ^ bits) for i in range(lax.axis_size(axi...]
    ppermute x67, starting transfers between devices: 142 us -> 153 us  [swap(): lax.ppermute(value, axis, [(i, i ^ bits) for i in range(lax.axis_size(axi...]
  transfers between devices with their start and end apart: 96 -> 96, of which waited for: 30 -> 28; matrix products, arithmetic and copies ran while one was open for 5% -> 5% of each run, Pallas kernels for 17% -> 17%
where the time goes in v3:
time: 926 us; the launch traced here: 917 us
  waiting for transfers between devices  408 us (44%)
  starting transfers between devices  269 us (29%)
  Pallas kernels  184 us (20%)
  local copies, waits for them, and re-layouts  29.8 us (3%)
  other arithmetic  25.7 us (3%)
    ppermute x67, waiting for transfers between devices, swap(): lax.ppermute(value, axis, [(i, i ^ bits) for i in range(lax.axis_size(axi...  345 us
    ppermute x67, starting transfers between devices, swap(): lax.ppermute(value, axis, [(i, i ^ bits) for i in range(lax.axis_size(axi...  153 us
    ppermute x29, starting transfers between devices, start(): outs = [lax.ppermute(v, 'gz', HOPS[k]) for v, k in zip(inputs, kinds)]  116 us
    pallas_call x8, Pallas kernels, project(): pl.pallas_call(functools.partial(project_kernel, planes, emit, parts), gr...  85.8 us
    ppermute x29, waiting for transfers between devices, start(): outs = [lax.ppermute(v, 'gz', HOPS[k]) for v, k in zip(inputs, kinds)]  62.2 us
    pallas_call x3, Pallas kernels, product(): pl.pallas_call(functools.partial(product_kernel, parts, chunks, left_chun...  55.6 us
    pallas_call x4, Pallas kernels, finish(): pl.pallas_call(functools.partial(finish_kernel, len(mixed)), grid=(blocks...  26.4 us
  transfers between devices with their start and end apart: 96, of which 28 were waited for; matrix products, arithmetic and copies ran while one was open for 5% of the time, Pallas kernels for 17%

profile of v3, /device:TPU:0, one launch (start us, length us, event | category | flops | bytes accessed | tf_op | source)
XLA Modules:
  0.0 916.6 jit_solution(10715253653831543664)
XLA Ops:
  41.5 14.6 %collective-permute-done.4.refs_7_ = bf16[32,2,32,256]{3,2,1,0:T(8,128)(2,1)} collective-permute-done((bf16[32,2,32,256]{3,2,1,0:T(8,128)(2,1)}, bf16[32,2,32,256]{3,2,1,0:T(8,128)(2,1)}, u32[]{:S(2)}, u32[]{:S(2)}) %collective-permute-start.4) | collective-permute-done | bytes 1048608 | tf_op jit(solution)/shard_map/ppermute | solution.py:414
  87.3 21.2 %collective-permute-done.9 = f32[769,32]{0,1:T(8,128)S(1)} collective-permute-done((f32[769,32]{0,1:T(8,128)S(1)}, f32[769,32]{0,1:T(8,128)S(1)}, u32[]{:S(2)}, u32[]{:S(2)}) %collective-permute-start.9) | collective-permute-done | bytes 98464 | tf_op jit(solution)/shard_map/ppermute | solution.py:420
  128.9 10.4 %project.8 = (bf16[32,2,32,256]{3,2,1,0:T(8,128)(2,1)}, bf16[32,2,32,256]{3,2,1,0:T(8,128)(2,1)}, bf16[32,2,32,256]{3,2,1,0:T(8,128)(2,1)}, bf16[32,2,32,256]{3,2,1,0:T(8,128)(2,1)}) custom-call(s32[1]{0:T(128)} %bitcast.plane_ref, bf16[32,2,32,256]{3,2,1,0:T(8,128)(2,1)} %copy-done.26, bf16[32,2,32,256]{3,2,1,0:T(8,128)(2,1)} %copy-done.25, ...), custom_call_target="tpu_custom_call" | custom-call | flops 4294967296 | bytes 16777216 | tf_op jit(solution)/shard_map/project/pallas_call | solution.py:153
  140.6 13.7 %collective-permute-start.12 = (bf16[32,2,32,256]{3,2,1,0:T(8,128)(2,1)S(1)}, bf16[32,2,32,256]{3,2,1,0:T(8,128)(2,1)}, u32[]{:S(2)}, u32[]{:S(2)}) collective-permute-start(bf16[32,2,32,256]{3,2,1,0:T(8,128)(2,1)S(1)} %get-tuple-element.260.refs_1_), channel_id=1, source_target_pairs={{0,1},{1,2},{2,3},{4,5},{5,6},{6,7},{8,9},{9,10},{10,11},{12,13},{... | collective-permute-start | bytes 3145736 | tf_op jit(solution)/shard_map/ppermute | solution.py:414
  163.3 9.5 %collective-permute-start.19 = (bf16[32,2,32,256]{3,2,1,0:T(8,128)(2,1)}, bf16[32,2,32,256]{3,2,1,0:T(8,128)(2,1)}, u32[]{:S(2)}, u32[]{:S(2)}) collective-permute-start(bf16[32,2,32,256]{3,2,1,0:T(8,128)(2,1)} %get-tuple-element.256), channel_id=1, source_target_pairs={{0,0},{1,2},{2,1},{3,3},{4,4},{5,6},{6,5},{7,7},{8,8},{9,10},{10,9... | collective-permute-start | bytes 3145736 | tf_op jit(solution)/shard_map/ppermute | solution.py:414
  180.0 11.0 %project.9 = (bf16[32,2,32,256]{3,2,1,0:T(8,128)(2,1)}, bf16[32,2,32,256]{3,2,1,0:T(8,128)(2,1)}, bf16[32,2,32,256]{3,2,1,0:T(8,128)(2,1)}, bf16[32,2,32,256]{3,2,1,0:T(8,128)(2,1)}, bf16[2,32,128,128]{3,2,1,0:T(8,128)(2,1)}) custom-call(s32[1]{0:T(128)} %bitcast.plane_ref, bf16[32,2,32,256]{3,2,1,0:T(8,128)(2,1)} %copy-done.26, ...), custom_call_target="tpu_custom_call" | custom-call | flops 4294967296 | bytes 16777216 | tf_op jit(solution)/shard_map/project/pallas_call | solution.py:153
  201.9 20.1 %collective-permute-done.22.refs_10_.refs_6_ = bf16[32,2,32,256]{3,2,1,0:T(8,128)(2,1)S(1)} collective-permute-done((bf16[32,2,32,256]{3,2,1,0:T(8,128)(2,1)}, bf16[32,2,32,256]{3,2,1,0:T(8,128)(2,1)S(1)}, u32[]{:S(2)}, u32[]{:S(2)}) %collective-permute-start.22) | collective-permute-done | bytes 1048608 | tf_op jit(solution)/shard_map/ppermute | solution.py:420
  225.7 10.4 %project.10 = (bf16[32,2,32,256]{3,2,1,0:T(8,128)(2,1)}, bf16[32,2,32,256]{3,2,1,0:T(8,128)(2,1)}, bf16[32,2,32,256]{3,2,1,0:T(8,128)(2,1)}, bf16[32,2,32,256]{3,2,1,0:T(8,128)(2,1)}) custom-call(s32[1]{0:T(128)} %bitcast.plane_ref, bf16[32,2,32,256]{3,2,1,0:T(8,128)(2,1)} %get-tuple-element.234.refs_0_, ...), custom_call_target="tpu_custom_call" | custom-call | flops 4294967296 | bytes 16777216 | tf_op jit(solution)/shard_map/project/pallas_call | solution.py:153
  248.2 16.6 %collective-permute-done.27.refs_2_ = bf16[32,2,32,256]{3,2,1,0:T(8,128)(2,1)} collective-permute-done((bf16[32,2,32,256]{3,2,1,0:T(8,128)(2,1)}, bf16[32,2,32,256]{3,2,1,0:T(8,128)(2,1)}, u32[]{:S(2)}, u32[]{:S(2)}) %collective-permute-start.27) | collective-permute-done | bytes 1048608 | tf_op jit(solution)/shard_map/ppermute | solution.py:420
  268.2 17.1 %collective-permute-done.32.refs_6_.refs_7_ = bf16[32,2,32,256]{3,2,1,0:T(8,128)(2,1)} collective-permute-done((bf16[32,2,32,256]{3,2,1,0:T(8,128)(2,1)S(1)}, bf16[32,2,32,256]{3,2,1,0:T(8,128)(2,1)}, u32[]{:S(2)}, u32[]{:S(2)}) %collective-permute-start.32) | collective-permute-done | bytes 1048608 | tf_op jit(solution)/shard_map/ppermute | solution.py:414
  292.8 10.4 %project.11 = (bf16[32,2,32,256]{3,2,1,0:T(8,128)(2,1)}, bf16[32,2,32,256]{3,2,1,0:T(8,128)(2,1)}, bf16[32,2,32,256]{3,2,1,0:T(8,128)(2,1)}, bf16[32,2,32,256]{3,2,1,0:T(8,128)(2,1)}) custom-call(s32[1]{0:T(128)} %bitcast.plane_ref, bf16[32,2,32,256]{3,2,1,0:T(8,128)(2,1)} %copy-done.24, bf16[32,2,32,256]{3,2,1,0:T(8,128)(2,1)} %copy-done.23, ...), custom_call_target="tpu_custom_call" | custom-call | flops 4294967296 | bytes 16777216 | tf_op jit(solution)/shard_map/project/pallas_call | solution.py:153
  303.2 12.1 %collective-permute-done.29.refs_4_ = bf16[32,2,32,256]{3,2,1,0:T(8,128)(2,1)} collective-permute-done((bf16[32,2,32,256]{3,2,1,0:T(8,128)(2,1)}, bf16[32,2,32,256]{3,2,1,0:T(8,128)(2,1)}, u32[]{:S(2)}, u32[]{:S(2)}) %collective-permute-start.29) | collective-permute-done | bytes 1048608 | tf_op jit(solution)/shard_map/ppermute | solution.py:414
  328.0 11.2 %project.13 = (bf16[32,2,32,256]{3,2,1,0:T(8,128)(2,1)}, bf16[32,2,32,256]{3,2,1,0:T(8,128)(2,1)}, bf16[32,2,32,256]{3,2,1,0:T(8,128)(2,1)}, bf16[32,2,32,256]{3,2,1,0:T(8,128)(2,1)}, bf16[2,32,128,128]{3,2,1,0:T(8,128)(2,1)}) custom-call(s32[1]{0:T(128)} %bitcast.plane_ref, bf16[32,2,32,256]{3,2,1,0:T(8,128)(2,1)} %get-tuple-element.234.refs_0_, ...), custom_call_target="tpu_custom_call" | custom-call | flops 4294967296 | bytes 16777216 | tf_op jit(solution)/shard_map/project/pallas_call | solution.py:153
  348.1 9.5 %collective-permute-start.48 = (bf16[32,2,32,256]{3,2,1,0:T(8,128)(2,1)}, bf16[32,2,32,256]{3,2,1,0:T(8,128)(2,1)}, u32[]{:S(2)}, u32[]{:S(2)}) collective-permute-start(bf16[32,2,32,256]{3,2,1,0:T(8,128)(2,1)} %collective-permute-done.32.refs_6_.refs_7_), channel_id=1, source_target_pairs={{0,0},{1,2},{2,1},{3,3},{4,4},{5,6},{6,5},{7,7},{8,8},{9,10},{10,9... | collective-permute-start | bytes 3145736 | tf_op jit(solution)/shard_map/ppermute | solution.py:414
  363.8 10.4 %project.12 = (bf16[32,2,32,256]{3,2,1,0:T(8,128)(2,1)}, bf16[32,2,32,256]{3,2,1,0:T(8,128)(2,1)}, bf16[32,2,32,256]{3,2,1,0:T(8,128)(2,1)}, bf16[32,2,32,256]{3,2,1,0:T(8,128)(2,1)}) custom-call(s32[1]{0:T(128)} %bitcast.plane_ref, bf16[32,2,32,256]{3,2,1,0:T(8,128)(2,1)} %get-tuple-element.269.refs_0_, ...), custom_call_target="tpu_custom_call" | custom-call | flops 4294967296 | bytes 16777216 | tf_op jit(solution)/shard_map/project/pallas_call | solution.py:153
  374.2 11.0 %project.14 = (bf16[32,2,32,256]{3,2,1,0:T(8,128)(2,1)}, bf16[32,2,32,256]{3,2,1,0:T(8,128)(2,1)}, bf16[32,2,32,256]{3,2,1,0:T(8,128)(2,1)}, bf16[32,2,32,256]{3,2,1,0:T(8,128)(2,1)}, bf16[2,32,128,128]{3,2,1,0:T(8,128)(2,1)}) custom-call(s32[1]{0:T(128)} %bitcast.plane_ref, bf16[32,2,32,256]{3,2,1,0:T(8,128)(2,1)} %copy-done.24, ...), custom_call_target="tpu_custom_call" | custom-call | flops 4294967296 | bytes 16777216 | tf_op jit(solution)/shard_map/project/pallas_call | solution.py:153
  386.8 11.0 %project.15 = (bf16[32,2,32,256]{3,2,1,0:T(8,128)(2,1)}, bf16[32,2,32,256]{3,2,1,0:T(8,128)(2,1)}, bf16[32,2,32,256]{3,2,1,0:T(8,128)(2,1)}, bf16[32,2,32,256]{3,2,1,0:T(8,128)(2,1)}, bf16[2,32,128,128]{3,2,1,0:T(8,128)(2,1)}) custom-call(s32[1]{0:T(128)} %bitcast.plane_ref, bf16[32,2,32,256]{3,2,1,0:T(8,128)(2,1)} %get-tuple-element.269.refs_0_, ...), custom_call_target="tpu_custom_call" | custom-call | flops 4294967296 | bytes 16777216 | tf_op jit(solution)/shard_map/project/pallas_call | solution.py:153
  397.7 10.1 %collective-permute-done.50.refs_18_.refs_14_ = bf16[32,2,32,256]{3,2,1,0:T(8,128)(2,1)} collective-permute-done((bf16[32,2,32,256]{3,2,1,0:T(8,128)(2,1)}, bf16[32,2,32,256]{3,2,1,0:T(8,128)(2,1)}, u32[]{:S(2)}, u32[]{:S(2)}) %collective-permute-start.50) | collective-permute-done | bytes 1048608 | tf_op jit(solution)/shard_map/ppermute | solution.py:420
  410.5 17.4 %collective-permute-done.58.refs_21_.refs_17_ = bf16[32,2,32,256]{3,2,1,0:T(8,128)(2,1)S(1)} collective-permute-done((bf16[32,2,32,256]{3,2,1,0:T(8,128)(2,1)}, bf16[32,2,32,256]{3,2,1,0:T(8,128)(2,1)S(1)}, u32[]{:S(2)}, u32[]{:S(2)}) %collective-permute-start.58) | collective-permute-done | bytes 1048608 | tf_op jit(solution)/shard_map/ppermute | solution.py:420
  435.2 43.1 %collective-permute-done.64.refs_22_.refs_18_ = bf16[32,2,32,256]{3,2,1,0:T(8,128)(2,1)} collective-permute-done((bf16[32,2,32,256]{3,2,1,0:T(8,128)(2,1)}, bf16[32,2,32,256]{3,2,1,0:T(8,128)(2,1)}, u32[]{:S(2)}, u32[]{:S(2)}) %collective-permute-start.64) | collective-permute-done | bytes 1048608 | tf_op jit(solution)/shard_map/ppermute | solution.py:420
  483.7 38.1 %collective-permute-done.56.refs_6_ = bf16[32,2,32,256]{3,2,1,0:T(8,128)(2,1)} collective-permute-done((bf16[32,2,32,256]{3,2,1,0:T(8,128)(2,1)}, bf16[32,2,32,256]{3,2,1,0:T(8,128)(2,1)}, u32[]{:S(2)}, u32[]{:S(2)}) %collective-permute-start.56) | collective-permute-done | bytes 1048608 | tf_op jit(solution)/shard_map/ppermute | solution.py:420
  521.8 19.6 %product.3 = (bf16[32,2,32,128]{3,2,1,0:T(8,128)(2,1)}, bf16[32,2,32,128]{3,2,1,0:T(8,128)(2,1)}, bf16[32,2,32,128]{3,2,1,0:T(8,128)(2,1)}, bf16[32,2,32,128]{3,...) custom-call(s32[4]{0:T(128)} %iota_xor_fusion.1.target_ref, ...), custom_call_target="tpu_custom_call" | custom-call | flops 4294967296 | bytes 41943040 | tf_op jit(solution)/shard_map/product/pallas_call | solution.py:218
  562.6 48.8 %collective-permute-done.70.refs_2_ = bf16[32,2,32,128]{3,2,1,0:T(8,128)(2,1)} collective-permute-done((bf16[32,2,32,128]{3,2,1,0:T(8,128)(2,1)}, bf16[32,2,32,128]{3,2,1,0:T(8,128)(2,1)}, u32[]{:S(2)}, u32[]{:S(2)}) %collective-permute-start.70) | collective-permute-done | bytes 524320 | tf_op jit(solution)/shard_map/ppermute | solution.py:420
  625.5 17.9 %product.4 = (bf16[32,2,32,128]{3,2,1,0:T(8,128)(2,1)}, bf16[32,2,32,128]{3,2,1,0:T(8,128)(2,1)}, bf16[32,2,32,128]{3,2,1,0:T(8,128)(2,1)}, bf16[32,2,32,128]{3,2,1,0:T(8,128)(2,1)}) custom-call(s32[4]{0:T(128)} %iota_xor_fusion.1.target_ref, bf16[32,2,32,256]{3,2,1,0:T(8,128)(2,1)} %get-tuple-element.373.refs_0_, bf16[32,2,32,256]{3,2,1,0:T(8,128)(2,1)} %copy-done.30, ...), custom_call_target="tpu_custom_call" | custom-call | flops 2147483648 | bytes 37748736 | tf_op jit(solution)/shard_map/product/pallas_call | solution.py:218
  667.1 44.0 %collective-permute-done.79.refs_2_ = bf16[32,2,32,128]{3,2,1,0:T(8,128)(2,1)} collective-permute-done((bf16[32,2,32,128]{3,2,1,0:T(8,128)(2,1)}, bf16[32,2,32,128]{3,2,1,0:T(8,128)(2,1)}, u32[]{:S(2)}, u32[]{:S(2)}) %collective-permute-start.79) | collective-permute-done | bytes 524320 | tf_op jit(solution)/shard_map/ppermute | solution.py:420
  711.1 25.8 %collective-permute-start.93 = (bf16[32,2,32,128]{3,2,1,0:T(8,128)(2,1)}, bf16[32,2,32,128]{3,2,1,0:T(8,128)(2,1)}, u32[]{:S(2)}, u32[]{:S(2)}) collective-permute-start(bf16[32,2,32,128]{3,2,1,0:T(8,128)(2,1)} %get-tuple-element.429), channel_id=1, source_target_pairs={{0,1},{1,0},{2,3},{3,2},{4,5},{5,4},{6,7},{7,6},{8,9},{9,8},{10,11... | collective-permute-start | bytes 1572872 | tf_op jit(solution)/shard_map/ppermute | solution.py:420
  745.2 18.2 %product.5 = (bf16[32,2,32,128]{3,2,1,0:T(8,128)(2,1)}, bf16[32,2,32,128]{3,2,1,0:T(8,128)(2,1)}, bf16[32,2,32,128]{3,2,1,0:T(8,128)(2,1)}, bf16[32,2,32,128]{3,2,1,0:T(8,128)(2,1)}) custom-call(s32[4]{0:T(128)} %iota_xor_fusion.1.target_ref, bf16[32,2,32,256]{3,2,1,0:T(8,128)(2,1)} %get-tuple-element.403.refs_0_, bf16[32,2,32,256]{3,2,1,0:T(8,128)(2,1)} %copy-done.28, ...), custom_call_target="tpu_custom_call" | custom-call | flops 2147483648 | bytes 37748736 | tf_op jit(solution)/shard_map/product/pallas_call | solution.py:218
  786.2 20.6 %collective-permute-start.88 = (bf16[32,2,32,128]{3,2,1,0:T(8,128)(2,1)}, bf16[32,2,32,128]{3,2,1,0:T(8,128)(2,1)S(1)}, u32[]{:S(2)}, u32[]{:S(2)}) collective-permute-start(bf16[32,2,32,128]{3,2,1,0:T(8,128)(2,1)} %get-tuple-element.422), channel_id=1, source_target_pairs={{0,2},{1,3},{2,0},{3,1},{4,6},{5,7},{6,4},{7,5},{8,10},{9,11},{10,... | collective-permute-start | bytes 1572872 | tf_op jit(solution)/shard_map/ppermute | solution.py:420
  815.0 24.1 %collective-permute-done.91.refs_2_ = bf16[32,2,32,128]{3,2,1,0:T(8,128)(2,1)S(1)} collective-permute-done((bf16[32,2,32,128]{3,2,1,0:T(8,128)(2,1)}, bf16[32,2,32,128]{3,2,1,0:T(8,128)(2,1)S(1)}, u32[]{:S(2)}, u32[]{:S(2)}) %collective-permute-start.91) | collective-permute-done | bytes 524320 | tf_op jit(solution)/shard_map/ppermute | solution.py:420
  839.1 30.0 %collective-permute-start.85 = (bf16[32,2,32,128]{3,2,1,0:T(8,128)(2,1)}, bf16[32,2,32,128]{3,2,1,0:T(8,128)(2,1)}, u32[]{:S(2)}, u32[]{:S(2)}) collective-permute-start(bf16[32,2,32,128]{3,2,1,0:T(8,128)(2,1)} %get-tuple-element.418), channel_id=1, source_target_pairs={{0,2},{1,3},{2,0},{3,1},{4,6},{5,7},{6,4},{7,5},{8,10},{9,11},{10,... | collective-permute-start | bytes 1572872 | tf_op jit(solution)/shard_map/ppermute | solution.py:420
  878.5 11.5 %collective-permute-done.88.refs_2_ = bf16[32,2,32,128]{3,2,1,0:T(8,128)(2,1)S(1)} collective-permute-done((bf16[32,2,32,128]{3,2,1,0:T(8,128)(2,1)}, bf16[32,2,32,128]{3,2,1,0:T(8,128)(2,1)S(1)}, u32[]{:S(2)}, u32[]{:S(2)}) %collective-permute-start.88) | collective-permute-done | bytes 524320 | tf_op jit(solution)/shard_map/ppermute | solution.py:420
  895.6 17.0 %collective-permute-done.85.refs_2_ = bf16[32,2,32,128]{3,2,1,0:T(8,128)(2,1)} collective-permute-done((bf16[32,2,32,128]{3,2,1,0:T(8,128)(2,1)}, bf16[32,2,32,128]{3,2,1,0:T(8,128)(2,1)}, u32[]{:S(2)}, u32[]{:S(2)}) %collective-permute-start.85) | collective-permute-done | bytes 524320 | tf_op jit(solution)/shard_map/ppermute | solution.py:420
  (366 shorter events, 309.3 us)
Async XLA Ops:
  17.3 69.9 %collective-permute-start.10 = (f32[769,32]{0,1:T(8,128)S(1)}, f32[769,32]{0,1:T(8,128)}, u32[]{:S(2)}, u32[]{:S(2)}) collective-permute-start(f32[769,32]{0,1:T(8,128)S(1)} %constant_dynamic-update-slice_fusion), channel_id=1, source_target_pairs={{0,3},{1,2},{2,1},{3,0},{4,7},{5,6},{6,5},{7,4},{8,11},{9,10},{10,... | collective-permute-start | bytes 295304 | tf_op jit(solution)/shard_map/ppermute | solution.py:420
  56.2 64.0 %collective-permute-start.15 = (bf16[32,2,32,256]{3,2,1,0:T(8,128)(2,1)}, bf16[32,2,32,256]{3,2,1,0:T(8,128)(2,1)}, u32[]{:S(2)}, u32[]{:S(2)}) collective-permute-start(bf16[32,2,32,256]{3,2,1,0:T(8,128)(2,1)} %get-tuple-element.234.refs_0_), channel_id=1, source_target_pairs={{3,2},{2,1},{1,0},{7,6},{6,5},{5,4},{11,10},{10,9},{9,8},{15,14},{... | collective-permute-start | bytes 3145736 | tf_op jit(solution)/shard_map/ppermute | solution.py:414
  57.4 62.7 %collective-permute-start.16 = (bf16[32,2,32,256]{3,2,1,0:T(8,128)(2,1)}, bf16[32,2,32,256]{3,2,1,0:T(8,128)(2,1)}, u32[]{:S(2)}, u32[]{:S(2)}) collective-permute-start(bf16[32,2,32,256]{3,2,1,0:T(8,128)(2,1)} %get-tuple-element.235.refs_1_), channel_id=1, source_target_pairs={{0,1},{1,2},{2,3},{4,5},{5,6},{6,7},{8,9},{9,10},{10,11},{12,13},{... | collective-permute-start | bytes 3145736 | tf_op jit(solution)/shard_map/ppermute | solution.py:414
  200.4 46.7 %collective-permute-start.26 = (bf16[32,2,32,256]{3,2,1,0:T(8,128)(2,1)}, bf16[32,2,32,256]{3,2,1,0:T(8,128)(2,1)}, u32[]{:S(2)}, u32[]{:S(2)}) collective-permute-start(bf16[32,2,32,256]{3,2,1,0:T(8,128)(2,1)} %get-tuple-element.272), channel_id=1, source_target_pairs={{0,8},{8,0},{16,24},{24,16},{1,9},{9,1},{17,25},{25,17},{2,10},{10... | collective-permute-start | bytes 3145736 | tf_op jit(solution)/shard_map/ppermute | solution.py:420
  287.6 51.6 %collective-permute-start.40 = (bf16[32,2,32,256]{3,2,1,0:T(8,128)(2,1)}, bf16[32,2,32,256]{3,2,1,0:T(8,128)(2,1)S(1)}, u32[]{:S(2)}, u32[]{:S(2)}) collective-permute-start(bf16[32,2,32,256]{3,2,1,0:T(8,128)(2,1)} %get-tuple-element.297), channel_id=1, source_target_pairs={{0,8},{8,0},{16,24},{24,16},{1,9},{9,1},{17,25},{25,17},{2,10},{10... | collective-permute-start | bytes 3145736 | tf_op jit(solution)/shard_map/ppermute | solution.py:420
  289.1 52.0 %collective-permute-start.41 = (bf16[32,2,32,256]{3,2,1,0:T(8,128)(2,1)}, bf16[32,2,32,256]{3,2,1,0:T(8,128)(2,1)S(1)}, u32[]{:S(2)}, u32[]{:S(2)}) collective-permute-start(bf16[32,2,32,256]{3,2,1,0:T(8,128)(2,1)} %get-tuple-element.298), channel_id=1, source_target_pairs={{0,16},{8,24},{16,0},{24,8},{1,17},{9,25},{17,1},{25,9},{2,18},{10... | collective-permute-start | bytes 3145736 | tf_op jit(solution)/shard_map/ppermute | solution.py:420
  291.2 49.9 %collective-permute-start.42 = (bf16[32,2,32,256]{3,2,1,0:T(8,128)(2,1)}, bf16[32,2,32,256]{3,2,1,0:T(8,128)(2,1)}, u32[]{:S(2)}, u32[]{:S(2)}) collective-permute-start(bf16[32,2,32,256]{3,2,1,0:T(8,128)(2,1)} %get-tuple-element.299), channel_id=1, source_target_pairs={{0,24},{8,16},{16,8},{24,0},{1,25},{9,17},{17,9},{25,1},{2,26},{10... | collective-permute-start | bytes 3145736 | tf_op jit(solution)/shard_map/ppermute | solution.py:420
  359.1 48.8 %collective-permute-start.50 = (bf16[32,2,32,256]{3,2,1,0:T(8,128)(2,1)}, bf16[32,2,32,256]{3,2,1,0:T(8,128)(2,1)}, u32[]{:S(2)}, u32[]{:S(2)}) collective-permute-start(bf16[32,2,32,256]{3,2,1,0:T(8,128)(2,1)} %get-tuple-element.313), channel_id=1, source_target_pairs={{0,16},{8,24},{16,0},{24,8},{1,17},{9,25},{17,1},{25,9},{2,18},{10... | collective-permute-start | bytes 3145736 | tf_op jit(solution)/shard_map/ppermute | solution.py:420
  362.7 46.8 %collective-permute-start.51 = (bf16[32,2,32,256]{3,2,1,0:T(8,128)(2,1)}, bf16[32,2,32,256]{3,2,1,0:T(8,128)(2,1)}, u32[]{:S(2)}, u32[]{:S(2)}) collective-permute-start(bf16[32,2,32,256]{3,2,1,0:T(8,128)(2,1)} %get-tuple-element.314), channel_id=1, source_target_pairs={{0,24},{8,16},{16,8},{24,0},{1,25},{9,17},{17,9},{25,1},{2,26},{10... | collective-permute-start | bytes 3145736 | tf_op jit(solution)/shard_map/ppermute | solution.py:420
  427.9 50.4 %collective-permute-start.64 = (bf16[32,2,32,256]{3,2,1,0:T(8,128)(2,1)}, bf16[32,2,32,256]{3,2,1,0:T(8,128)(2,1)}, u32[]{:S(2)}, u32[]{:S(2)}) collective-permute-start(bf16[32,2,32,256]{3,2,1,0:T(8,128)(2,1)} %get-tuple-element.346), channel_id=1, source_target_pairs={{0,16},{8,24},{16,0},{24,8},{1,17},{9,25},{17,1},{25,9},{2,18},{10... | collective-permute-start | bytes 3145736 | tf_op jit(solution)/shard_map/ppermute | solution.py:420
  431.5 49.1 %collective-permute-start.65 = (bf16[32,2,32,256]{3,2,1,0:T(8,128)(2,1)}, bf16[32,2,32,256]{3,2,1,0:T(8,128)(2,1)S(1)}, u32[]{:S(2)}, u32[]{:S(2)}) collective-permute-start(bf16[32,2,32,256]{3,2,1,0:T(8,128)(2,1)} %get-tuple-element.347), channel_id=1, source_target_pairs={{0,24},{8,16},{16,8},{24,0},{1,25},{9,17},{17,9},{25,1},{2,26},{10... | collective-permute-start | bytes 3145736 | tf_op jit(solution)/shard_map/ppermute | solution.py:420
  432.6 48.1 %collective-permute-start.63 = (bf16[32,2,32,256]{3,2,1,0:T(8,128)(2,1)S(1)}, bf16[32,2,32,256]{3,2,1,0:T(8,128)(2,1)S(1)}, u32[]{:S(2)}, u32[]{:S(2)}) collective-permute-start(bf16[32,2,32,256]{3,2,1,0:T(8,128)(2,1)S(1)} %collective-permute-done.58.refs_21_.refs_17_), channel_id=1, source_target_pairs={{0,4},{4,0},{1,5},{5,1},{2,6},{6,2},{3,7},{7,3},{8,12},{12,8},{9,1... | collective-permute-start | bytes 3145736 | tf_op jit(solution)/shard_map/ppermute | solution.py:420
  432.7 48.6 %collective-permute-start.55 = (bf16[32,2,32,256]{3,2,1,0:T(8,128)(2,1)}, bf16[32,2,32,256]{3,2,1,0:T(8,128)(2,1)S(1)}, u32[]{:S(2)}, u32[]{:S(2)}) collective-permute-start(bf16[32,2,32,256]{3,2,1,0:T(8,128)(2,1)} %get-tuple-element.328), channel_id=1, source_target_pairs={{0,8},{8,0},{16,24},{24,16},{1,9},{9,1},{17,25},{25,17},{2,10},{10... | collective-permute-start | bytes 3145736 | tf_op jit(solution)/shard_map/ppermute | solution.py:420
  433.3 88.5 %collective-permute-start.56 = (bf16[32,2,32,256]{3,2,1,0:T(8,128)(2,1)}, bf16[32,2,32,256]{3,2,1,0:T(8,128)(2,1)}, u32[]{:S(2)}, u32[]{:S(2)}) collective-permute-start(bf16[32,2,32,256]{3,2,1,0:T(8,128)(2,1)} %get-tuple-element.329), channel_id=1, source_target_pairs={{0,16},{8,24},{16,0},{24,8},{1,17},{9,25},{17,1},{25,9},{2,18},{10... | collective-permute-start | bytes 3145736 | tf_op jit(solution)/shard_map/ppermute | solution.py:420
  542.9 80.2 %collective-permute-start.52 = (bf16[32,2,32,256]{3,2,1,0:T(8,128)(2,1)}, bf16[32,2,32,256]{3,2,1,0:T(8,128)(2,1)S(1)}, u32[]{:S(2)}, u32[]{:S(2)}) collective-permute-start(bf16[32,2,32,256]{3,2,1,0:T(8,128)(2,1)} %get-tuple-element.320), channel_id=1, source_target_pairs={{0,8},{8,0},{16,24},{24,16},{1,9},{9,1},{17,25},{25,17},{2,10},{10... | collective-permute-start | bytes 3145736 | tf_op jit(solution)/shard_map/ppermute | solution.py:420
  543.6 80.7 %collective-permute-start.53 = (bf16[32,2,32,256]{3,2,1,0:T(8,128)(2,1)}, bf16[32,2,32,256]{3,2,1,0:T(8,128)(2,1)S(1)}, u32[]{:S(2)}, u32[]{:S(2)}) collective-permute-start(bf16[32,2,32,256]{3,2,1,0:T(8,128)(2,1)} %get-tuple-element.321), channel_id=1, source_target_pairs={{0,16},{8,24},{16,0},{24,8},{1,17},{9,25},{17,1},{25,9},{2,18},{10... | collective-permute-start | bytes 3145736 | tf_op jit(solution)/shard_map/ppermute | solution.py:420
  545.3 78.9 %collective-permute-start.54 = (bf16[32,2,32,256]{3,2,1,0:T(8,128)(2,1)}, bf16[32,2,32,256]{3,2,1,0:T(8,128)(2,1)S(1)}, u32[]{:S(2)}, u32[]{:S(2)}) collective-permute-start(bf16[32,2,32,256]{3,2,1,0:T(8,128)(2,1)} %get-tuple-element.322), channel_id=1, source_target_pairs={{0,24},{8,16},{16,8},{24,0},{1,25},{9,17},{17,9},{25,1},{2,26},{10... | collective-permute-start | bytes 3145736 | tf_op jit(solution)/shard_map/ppermute | solution.py:420
  548.3 63.2 %collective-permute-start.70 = (bf16[32,2,32,128]{3,2,1,0:T(8,128)(2,1)}, bf16[32,2,32,128]{3,2,1,0:T(8,128)(2,1)}, u32[]{:S(2)}, u32[]{:S(2)}) collective-permute-start(bf16[32,2,32,128]{3,2,1,0:T(8,128)(2,1)} %get-tuple-element.365), channel_id=1, source_target_pairs={{0,16},{8,24},{16,0},{24,8},{1,17},{9,25},{17,1},{25,9},{2,18},{10... | collective-permute-start | bytes 1572872 | tf_op jit(solution)/shard_map/ppermute | solution.py:420
  556.6 57.4 %collective-permute-start.71 = (bf16[32,2,32,128]{3,2,1,0:T(8,128)(2,1)}, bf16[32,2,32,128]{3,2,1,0:T(8,128)(2,1)}, u32[]{:S(2)}, u32[]{:S(2)}) collective-permute-start(bf16[32,2,32,128]{3,2,1,0:T(8,128)(2,1)} %get-tuple-element.366), channel_id=1, source_target_pairs={{0,24},{8,16},{16,8},{24,0},{1,25},{9,17},{17,9},{25,1},{2,26},{10... | collective-permute-start | bytes 1572872 | tf_op jit(solution)/shard_map/ppermute | solution.py:420
  644.1 99.4 %collective-permute-start.72 = (bf16[32,2,32,256]{3,2,1,0:T(8,128)(2,1)}, bf16[32,2,32,256]{3,2,1,0:T(8,128)(2,1)S(1)}, u32[]{:S(2)}, u32[]{:S(2)}) collective-permute-start(bf16[32,2,32,256]{3,2,1,0:T(8,128)(2,1)} %get-tuple-element.379), channel_id=1, source_target_pairs={{0,8},{8,0},{16,24},{24,16},{1,9},{9,1},{17,25},{25,17},{2,10},{10... | collective-permute-start | bytes 3145736 | tf_op jit(solution)/shard_map/ppermute | solution.py:420
  645.5 98.0 %collective-permute-start.73 = (bf16[32,2,32,256]{3,2,1,0:T(8,128)(2,1)}, bf16[32,2,32,256]{3,2,1,0:T(8,128)(2,1)S(1)}, u32[]{:S(2)}, u32[]{:S(2)}) collective-permute-start(bf16[32,2,32,256]{3,2,1,0:T(8,128)(2,1)} %get-tuple-element.380), channel_id=1, source_target_pairs={{0,16},{8,24},{16,0},{24,8},{1,17},{9,25},{17,1},{25,9},{2,18},{10... | collective-permute-start | bytes 3145736 | tf_op jit(solution)/shard_map/ppermute | solution.py:420
  646.5 97.1 %collective-permute-start.74 = (bf16[32,2,32,256]{3,2,1,0:T(8,128)(2,1)}, bf16[32,2,32,256]{3,2,1,0:T(8,128)(2,1)S(1)}, u32[]{:S(2)}, u32[]{:S(2)}) collective-permute-start(bf16[32,2,32,256]{3,2,1,0:T(8,128)(2,1)} %get-tuple-element.381), channel_id=1, source_target_pairs={{0,24},{8,16},{16,8},{24,0},{1,25},{9,17},{17,9},{25,1},{2,26},{10... | collective-permute-start | bytes 3145736 | tf_op jit(solution)/shard_map/ppermute | solution.py:420
  647.6 63.5 %collective-permute-start.79 = (bf16[32,2,32,128]{3,2,1,0:T(8,128)(2,1)}, bf16[32,2,32,128]{3,2,1,0:T(8,128)(2,1)}, u32[]{:S(2)}, u32[]{:S(2)}) collective-permute-start(bf16[32,2,32,128]{3,2,1,0:T(8,128)(2,1)} %get-tuple-element.389), channel_id=1, source_target_pairs={{0,16},{8,24},{16,0},{24,8},{1,17},{9,25},{17,1},{25,9},{2,18},{10... | collective-permute-start | bytes 1572872 | tf_op jit(solution)/shard_map/ppermute | solution.py:420
  658.6 78.3 %collective-permute-start.80 = (bf16[32,2,32,128]{3,2,1,0:T(8,128)(2,1)}, bf16[32,2,32,128]{3,2,1,0:T(8,128)(2,1)}, u32[]{:S(2)}, u32[]{:S(2)}) collective-permute-start(bf16[32,2,32,128]{3,2,1,0:T(8,128)(2,1)} %get-tuple-element.390), channel_id=1, source_target_pairs={{0,24},{8,16},{16,8},{24,0},{1,25},{9,17},{17,9},{25,1},{2,26},{10... | collective-permute-start | bytes 1572872 | tf_op jit(solution)/shard_map/ppermute | solution.py:420
  711.1 55.8 %collective-permute-start.93 = (bf16[32,2,32,128]{3,2,1,0:T(8,128)(2,1)}, bf16[32,2,32,128]{3,2,1,0:T(8,128)(2,1)}, u32[]{:S(2)}, u32[]{:S(2)}) collective-permute-start(bf16[32,2,32,128]{3,2,1,0:T(8,128)(2,1)} %get-tuple-element.429), channel_id=1, source_target_pairs={{0,1},{1,0},{2,3},{3,2},{4,5},{5,4},{6,7},{7,6},{8,9},{9,8},{10,11... | collective-permute-start | bytes 1572872 | tf_op jit(solution)/shard_map/ppermute | solution.py:420
  775.1 64.0 %collective-permute-start.91 = (bf16[32,2,32,128]{3,2,1,0:T(8,128)(2,1)}, bf16[32,2,32,128]{3,2,1,0:T(8,128)(2,1)S(1)}, u32[]{:S(2)}, u32[]{:S(2)}) collective-permute-start(bf16[32,2,32,128]{3,2,1,0:T(8,128)(2,1)} %get-tuple-element.426), channel_id=1, source_target_pairs={{0,2},{1,3},{2,0},{3,1},{4,6},{5,7},{6,4},{7,5},{8,10},{9,11},{10,... | collective-permute-start | bytes 1572872 | tf_op jit(solution)/shard_map/ppermute | solution.py:420
  783.1 56.0 %collective-permute-start.92 = (bf16[32,2,32,128]{3,2,1,0:T(8,128)(2,1)}, bf16[32,2,32,128]{3,2,1,0:T(8,128)(2,1)S(1)}, u32[]{:S(2)}, u32[]{:S(2)}) collective-permute-start(bf16[32,2,32,128]{3,2,1,0:T(8,128)(2,1)} %get-tuple-element.427), channel_id=1, source_target_pairs={{0,3},{1,2},{2,1},{3,0},{4,7},{5,6},{6,5},{7,4},{8,11},{9,10},{10,... | collective-permute-start | bytes 1572872 | tf_op jit(solution)/shard_map/ppermute | solution.py:420
  786.2 82.8 %collective-permute-start.87 = (bf16[32,2,32,128]{3,2,1,0:T(8,128)(2,1)}, bf16[32,2,32,128]{3,2,1,0:T(8,128)(2,1)S(1)}, u32[]{:S(2)}, u32[]{:S(2)}) collective-permute-start(bf16[32,2,32,128]{3,2,1,0:T(8,128)(2,1)} %get-tuple-element.421), channel_id=1, source_target_pairs={{0,1},{1,0},{2,3},{3,2},{4,5},{5,4},{6,7},{7,6},{8,9},{9,8},{10,11... | collective-permute-start | bytes 1572872 | tf_op jit(solution)/shard_map/ppermute | solution.py:420
  786.2 103.8 %collective-permute-start.88 = (bf16[32,2,32,128]{3,2,1,0:T(8,128)(2,1)}, bf16[32,2,32,128]{3,2,1,0:T(8,128)(2,1)S(1)}, u32[]{:S(2)}, u32[]{:S(2)}) collective-permute-start(bf16[32,2,32,128]{3,2,1,0:T(8,128)(2,1)} %get-tuple-element.422), channel_id=1, source_target_pairs={{0,2},{1,3},{2,0},{3,1},{4,6},{5,7},{6,4},{7,5},{8,10},{9,11},{10,... | collective-permute-start | bytes 1572872 | tf_op jit(solution)/shard_map/ppermute | solution.py:420
  806.9 83.2 %collective-permute-start.89 = (bf16[32,2,32,128]{3,2,1,0:T(8,128)(2,1)}, bf16[32,2,32,128]{3,2,1,0:T(8,128)(2,1)S(1)}, u32[]{:S(2)}, u32[]{:S(2)}) collective-permute-start(bf16[32,2,32,128]{3,2,1,0:T(8,128)(2,1)} %get-tuple-element.423), channel_id=1, source_target_pairs={{0,3},{1,2},{2,1},{3,0},{4,7},{5,6},{6,5},{7,4},{8,11},{9,10},{10,... | collective-permute-start | bytes 1572872 | tf_op jit(solution)/shard_map/ppermute | solution.py:420
  839.1 56.6 %collective-permute-start.84 = (bf16[32,2,32,128]{3,2,1,0:T(8,128)(2,1)}, bf16[32,2,32,128]{3,2,1,0:T(8,128)(2,1)}, u32[]{:S(2)}, u32[]{:S(2)}) collective-permute-start(bf16[32,2,32,128]{3,2,1,0:T(8,128)(2,1)} %get-tuple-element.417), channel_id=1, source_target_pairs={{0,1},{1,0},{2,3},{3,2},{4,5},{5,4},{6,7},{7,6},{8,9},{9,8},{10,11... | collective-permute-start | bytes 1572872 | tf_op jit(solution)/shard_map/ppermute | solution.py:420
  839.1 73.6 %collective-permute-start.85 = (bf16[32,2,32,128]{3,2,1,0:T(8,128)(2,1)}, bf16[32,2,32,128]{3,2,1,0:T(8,128)(2,1)}, u32[]{:S(2)}, u32[]{:S(2)}) collective-permute-start(bf16[32,2,32,128]{3,2,1,0:T(8,128)(2,1)} %get-tuple-element.418), channel_id=1, source_target_pairs={{0,2},{1,3},{2,0},{3,1},{4,6},{5,7},{6,4},{7,5},{8,10},{9,11},{10,... | collective-permute-start | bytes 1572872 | tf_op jit(solution)/shard_map/ppermute | solution.py:420
  (120 other events, 3533.0 us)
